TPU v7x, 512 devices: a 4x2x32 block of a 4x8x32 slice. The times are simulated.
512 devices in a mesh: groups: 2 (over y), expert: 32 (over z), tensor: 8 (over x, core).
Axes of the slice: x: 4, y: 2, z: 32, core: 2. Of those that a mesh axis runs over, the one named last changes fastest.
The devices are a block of a 4x8x32 slice.
Arguments:
- tokens: bfloat16 [2048, 4096], P(('groups', 'expert')), parts along dimension 0, may hold values from -6 to 6
- route_ids: int32 [2048, 2], P(('groups', 'expert')), parts along dimension 0, may hold values from 0 to 3, all different within a row; in each aligned block of 32 rows (0 to 31, 32 to 63, ...) at most 24 rows name the same one
- route_gates: float32 [2048, 2], P(('groups', 'expert')), parts along dimension 0, may hold values from 0.1 to 1
- gate_weight: bfloat16 [4096, 32768], P(None, ('expert', 'tensor')), may hold values from -0.09375 to 0.09375
- up_weight: bfloat16 [4096, 32768], P(None, ('expert', 'tensor')), may hold values from -0.09375 to 0.09375
- down_weight: bfloat16 [32768, 4096], P('expert', 'tensor'), may hold values from -0.0625 to 0.0625
Outputs:
- mixed: bfloat16 [2048, 4096], P(('groups', 'expert'), 'tensor'), parts along dimension 0
There are 2 independent parts, one for each index of `groups`. A program takes and returns all parts, laid end to end along the dimension named above; an argument that names none is the same for every part. Nothing has to cross between parts.
Inputs may be any that keep to these rules, and one draw needn't show every extreme that they name: `route_ids`: each row names 2 different experts. In the rows of one device no expert is named more than 24 times, and in some device's rows one expert is named exactly 24 times.
All inputs are finite; a program needn't handle non-finite values.
Results may differ from a plain program's by a relative error of at most 0.005.
Values may be sent and summed in bfloat16 or wider, within the bound.
No kernel may reach another device: no remote copies, remote signals or barrier semaphores. Data moves between devices by JAX's collectives and lax.ppermute only.
A program may use at most 64 MiB of HBM per device.

v0:
```python
import jax
import jax.numpy as jnp
from jax import lax
from jax.sharding import PartitionSpec as P

EXPERTS = 4
TOP = 2
CAP = 24


EPSILON = 1e-05


def from_everyone(array, axis):
    devices = lax.axis_size(axis)
    return lax.all_to_all(
        jnp.broadcast_to(array[None], (devices, *array.shape)), axis, 0, 0, tiled=True
    )


def joined_along(blocks, dim):
    lengths = list(blocks.shape[1:])
    lengths[dim] *= blocks.shape[0]
    return jnp.moveaxis(blocks, 0, dim).reshape(lengths)


def gather_directly(array, axis, dim):
    blocks = from_everyone(array, axis)
    return joined_along(blocks, dim)


def slot_index(id_table):
    flat_ids = id_table.reshape(-1)
    onehot = (flat_ids[:, None] == jnp.arange(EXPERTS, dtype=jnp.int32)[None, :]).astype(jnp.int32)
    earlier = jnp.cumsum(onehot, axis=0) - onehot
    position = jnp.sum(earlier * onehot, axis=1)
    return (flat_ids * CAP + position).reshape(id_table.shape)


def finish(gate_sum, up_sum, down_weight, leading):
    hidden = (jax.nn.silu(gate_sum) * up_sum).astype(jnp.bfloat16)
    produced = jnp.dot(
        gather_directly(hidden, "tensor", 1), down_weight, preferred_element_type=jnp.float32
    )
    return produced.reshape(tuple(leading) + (down_weight.shape[1],))


def full_rows(row_block, gate_weight, up_weight, down_weight):
    flat_rows = row_block.reshape(-1, row_block.shape[-1])
    gate_sum = jnp.dot(flat_rows, gate_weight, preferred_element_type=jnp.float32)
    up_sum = jnp.dot(flat_rows, up_weight, preferred_element_type=jnp.float32)
    return finish(gate_sum, up_sum, down_weight, row_block.shape[:2])


def local(tokens, route_ids, route_gates, gate_weight, up_weight, down_weight):
    floats = tokens.astype(jnp.float32)
    scale = lax.rsqrt(jnp.mean(floats * floats, axis=-1, keepdims=True) + EPSILON)
    normed = (floats * scale).astype(jnp.bfloat16)
    tok_count = tokens.shape[0]
    model_width = tokens.shape[1]
    n_expert = lax.axis_size("expert")
    n_tensor = lax.axis_size("tensor")
    blocks = n_expert // EXPERTS
    slice_width = model_width // n_tensor
    offset_cols = lax.axis_index("tensor") * slice_width
    slot_of = slot_index(route_ids)
    targets = jnp.arange(EXPERTS * CAP, dtype=jnp.int32)
    matches = slot_of[:, :, None] == targets[None, None, :]
    combine = jnp.sum(jnp.where(matches, route_gates[:, :, None], 0.0), axis=1)
    picker = jnp.sum(matches.astype(jnp.int32), axis=1).astype(jnp.bfloat16)
    packed = jnp.dot(picker.T, normed, preferred_element_type=jnp.float32).astype(jnp.bfloat16)
    packed = packed.reshape(EXPERTS, CAP, model_width)
    gathered_rows, gathered_ids = (
        lax.all_gather(normed, "expert", axis=0, tiled=True),
        lax.all_gather(route_ids.astype(jnp.bfloat16), "expert", axis=0, tiled=True),
    )
    id_table = gathered_ids.astype(jnp.int32).reshape(n_expert, tok_count, TOP)
    all_slots = jax.vmap(slot_index)(id_table)
    own_expert = lax.axis_index("expert") // blocks
    wanted = own_expert * CAP + jnp.arange(CAP, dtype=jnp.int32)
    chooser = jnp.sum(
        (all_slots[:, :, :, None] == wanted[None, None, None, :]).astype(jnp.int32), axis=2
    )
    chooser = chooser.astype(jnp.bfloat16)
    source_rows = gathered_rows.reshape(n_expert, tok_count, model_width)
    row_block = jnp.einsum(
        "stc,std->scd", chooser, source_rows, preferred_element_type=jnp.float32
    ).astype(jnp.bfloat16)
    produced = full_rows(row_block, gate_weight, up_weight, down_weight)
    returned = lax.all_to_all(
        produced.astype(jnp.bfloat16), "expert", split_axis=0, concat_axis=0, tiled=True
    ).astype(produced.dtype)
    summed = jnp.sum(returned.reshape(EXPERTS, blocks, CAP, slice_width), axis=1).reshape(
        EXPERTS * CAP, slice_width
    )
    mixture = jnp.dot(
        combine, summed, precision=lax.Precision.HIGHEST, preferred_element_type=jnp.float32
    )
    residual = lax.dynamic_slice_in_dim(floats, offset_cols, slice_width, 1)
    return (residual + mixture).astype(jnp.bfloat16)


def solution(mesh):
    in_specs = (
        P(("groups", "expert"), None),
        P(("groups", "expert"), None),
        P(("groups", "expert"), None),
        P(None, ("expert", "tensor")),
        P(None, ("expert", "tensor")),
        P("expert", "tensor"),
    )
    out_specs = P(("groups", "expert"), "tensor")
    return jax.shard_map(local, mesh=mesh, in_specs=in_specs, out_specs=out_specs, check_vma=False)
```

profile of v0, /device:TPU:33, one launch (start us, length us, event | category | flops | bytes accessed | tf_op | source)
XLA Modules:
  0.0 333.6 jit_solution(16633657564355057485)
XLA Ops:
  6.5 0.0 copy-start
  6.6 0.0 all-gather.3.cloned.1.call-start
  6.6 1.2 multiply_reduce_fusion
  7.8 1.8 multiply_convert_fusion
  9.5 0.1 all-gather.3.cloned.1.call-update
  9.6 0.8 copy.33
  10.4 0.1 eq.56
  10.5 0.1 fusion.9
  10.6 0.1 reduce_window_sum.22
  10.7 0.2 select_reduce_fusion.2
  10.8 0.1 reduce_sum.59
  11.0 0.1 copy.34
  11.0 0.8 convert_bitcast_fusion
  11.8 84.8 %all-gather = bf16[32,32,2]{1,2,0:T(2,128)(2,1)S(1)} all-gather(bf16[1,32,2]{1,2,0:T(2,128)(2,1)S(1)} %get-tuple-element.5), channel_id=1, replica_groups=mesh['groups'=2,'expert'=32,'tensor'=8] {'expert'}, dimensions={0}, use_global_device_ids=true | all-gather | bytes 4224 | tf_op jit(solution)/shard_map/all_gather | solution.py:75
  96.6 0.1 copy.35
  96.7 1.7 select_reduce_fusion
  98.5 0.1 copy.36
  98.6 0.2 convert_reduce_fusion.1
  98.7 68.7 %all-gather.3.cloned.1.call-done = bf16[1024,4096]{1,0:T(8,128)(2,1)} async-done(((bf16[32,4096]{1,0:T(8,128)(2,1)}), bf16[1024,4096]{1,0:T(8,128)(2,1)}) %all-gather.3.cloned.1.call-update) | async-done | bytes 8388624 | tf_op jit(solution)/shard_map/all_gather | solution.py:74
  167.5 0.0 copy-start.3
  167.5 5.7 %convolution_convert_fusion = bf16[32,24,4096]{2,1,0:T(8,128)(2,1)S(1)} fusion(bf16[32,32,4096]{2,1,0:T(8,128)(2,1)} %bitcast.23, s32[32,32,24]{1,2,0:T(8,128)S(1)} %convert_reduce_fusion.1), kind=kOutput, calls=%fused_computation | convolution fusion | flops 204496896 | bytes 14778368 | tf_op jit(solution)/shard_map/stc,std->scd/dot_general | solution.py:86
  173.2 0.0 copy-start.4
  173.2 0.0 copy-done.3
  173.2 1.8 fusion.10
  175.0 0.0 copy-done.4
  175.0 1.8 fusion.4
  176.8 0.2 broadcast_in_dim.16
  177.0 44.6 %all_to_all.10 = bf16[8,768,128]{2,1,0:T(8,128)(2,1)S(1)} all-to-all(bf16[8,768,128]{2,1,0:T(8,128)(2,1)S(1)} %broadcast_in_dim.16), channel_id=1, replica_groups=mesh['groups'=2,'expert'=32,'tensor'=8] {'tensor'}, dimensions={0} | all-to-all | bytes 3145728 | tf_op jit(solution)/shard_map/all_to_all | solution.py:16
  221.6 0.0 copy-start.1
  221.6 0.0 copy-start.2
  221.6 1.0 copy.37
  222.6 2.1 dot_general.20
  224.7 0.0 copy-done
  224.7 3.3 convolution_convert_fusion.1
  228.0 12.0 %all-to-all-start.1 = ((bf16[32,24,512]{2,1,0:T(8,128)(2,1)}), bf16[32,24,512]{2,1,0:T(8,128)(2,1)S(1)}, u32[]{:S(2)}, u32[]{:S(2)}) async-start(bf16[32,24,512]{2,1,0:T(8,128)(2,1)} %convolution_convert_fusion.1), calls=%async_computation.1 | async-start | bytes 1572864 | tf_op jit(solution)/shard_map/all_to_all | solution.py:90
  240.0 0.0 copy-done.1
  240.1 0.0 copy-done.2
  240.1 0.1 select_reduce_fusion.1
  240.2 85.5 %all-to-all-done.1 = bf16[32,24,512]{2,1,0:T(8,128)(2,1)S(1)} async-done(((bf16[32,24,512]{2,1,0:T(8,128)(2,1)}), bf16[32,24,512]{2,1,0:T(8,128)(2,1)S(1)}, u32[]{:S(2)}, u32[]{:S(2)}) %all-to-all-start.1) | async-done | bytes 786464 | tf_op jit(solution)/shard_map/all_to_all | solution.py:90
  325.7 0.1 convert_reduce_fusion
  325.8 0.8 fusion.5
  (5 shorter events, 0.1 us)
Async XLA Ops:
  6.5 218.2 %copy-start = (bf16[1024,512]{1,0:T(8,128)(2,1)S(1)}, bf16[1024,512]{1,0:T(8,128)(2,1)}, u32[]{:S(2)}) copy-start(bf16[1024,512]{1,0:T(8,128)(2,1)} %param.11) | copy-start | bytes 3145732
  6.6 160.9 %all-gather.3.cloned.1.call-start = ((), (), s32[]{:S(2)}) async-start(), calls=%async_computation.2 | async-start | bytes 8650752 | tf_op jit(solution)/shard_map/all_gather | solution.py:74
  167.5 5.8 %copy-start.3 = (bf16[4096,128]{1,0:T(8,128)(2,1)S(1)}, bf16[4096,128]{1,0:T(8,128)(2,1)}, u32[]{:S(2)}) copy-start(bf16[4096,128]{1,0:T(8,128)(2,1)} %param.9) | copy-start | bytes 3145732
  173.2 1.8 copy-start.4
  221.6 18.5 %copy-start.1 = (bf16[32,4096]{1,0:T(8,128)(2,1)S(1)}, bf16[32,4096]{1,0:T(8,128)(2,1)}, u32[]{:S(2)}) copy-start(bf16[32,4096]{1,0:T(8,128)(2,1)} %param.6) | copy-start | bytes 786436
  221.6 18.5 %copy-start.2 = (f32[32,2]{0,1:T(2,128)S(1)}, f32[32,2]{0,1:T(2,128)}, u32[]{:S(2)}) copy-start(f32[32,2]{0,1:T(2,128)} %param.8) | copy-start | bytes 772
  228.0 97.7 %all-to-all-start.1 = ((bf16[32,24,512]{2,1,0:T(8,128)(2,1)}), bf16[32,24,512]{2,1,0:T(8,128)(2,1)S(1)}, u32[]{:S(2)}, u32[]{:S(2)}) async-start(bf16[32,24,512]{2,1,0:T(8,128)(2,1)} %convolution_convert_fusion.1), calls=%async_computation.1 | async-start | bytes 1572864 | tf_op jit(solution)/shard_map/all_to_all | solution.py:90
Sparse Core Ops, SparseCore 0:
  9.7 157.7 all-gather.2
where the time goes:
time: 334 us
  waiting for transfers between devices  154 us (46%)
  blocking collectives  129 us (39%)
  between operations  13.6 us (4%)
  matrix products  13.5 us (4%)
  starting transfers between devices  12 us (4%)
  other arithmetic  6.25 us (2%)
  local copies, waits for them, and re-layouts  4.54 us (1%)
    all_to_all x1, waiting for transfers between devices, local(): lax.all_to_all(produced.astype(jnp.bfloat16), 'expert', split_axis=0, con...  85.5 us
    all_gather x1, blocking collectives, local(): lax.all_gather(route_ids.astype(jnp.bfloat16), 'expert', axis=0, tiled=True)  84.8 us
    all_gather x1, waiting for transfers between devices, local(): lax.all_gather(normed, 'expert', axis=0, tiled=True)  68.7 us
    all_to_all x1, blocking collectives, from_everyone(): lax.all_to_all(jnp.broadcast_to(array[None], (devices, *array.shape)), ax...  44.6 us
    all_to_all x1, starting transfers between devices, local(): lax.all_to_all(produced.astype(jnp.bfloat16), 'expert', split_axis=0, con...  12 us
  transfers between devices with their start and end apart: 2, of which 2 were waited for; matrix products, arithmetic and copies ran while one was open for 1% of the time, Pallas kernels for 0%

commit v1 on v0

v1 whole, which is shorter than its diff:
```python
import jax
import jax.numpy as jnp
from jax import lax
from jax.sharding import Mesh, PartitionSpec as P

EXPERTS = 4
TOP = 2
CAP = 24
NEAR = 4
CORES = 2

EPSILON = 1e-05


def slot_index(id_table):
    flat_ids = id_table.reshape(-1)
    onehot = (flat_ids[:, None] == jnp.arange(EXPERTS, dtype=jnp.int32)[None, :]).astype(jnp.int32)
    earlier = jnp.cumsum(onehot, axis=0) - onehot
    position = jnp.sum(earlier * onehot, axis=1)
    return (flat_ids * CAP + position).reshape(id_table.shape)


def from_everyone(array, axis):
    devices = lax.axis_size(axis)
    return lax.all_to_all(
        jnp.broadcast_to(array[None], (devices, *array.shape)), axis, 0, 0, tiled=True
    )


def local(tokens, route_ids, route_gates, gate_weight, up_weight, down_weight):
    f32, bf16 = jnp.float32, jnp.bfloat16
    tok_count, model_width = tokens.shape
    far, near, xs = lax.axis_size("far"), lax.axis_size("near"), lax.axis_size("x")
    core, x = lax.axis_index("core"), lax.axis_index("x")
    part = CAP // CORES
    chip_width = model_width // xs
    out_width = down_weight.shape[1]
    swap = [(i, (i + 1) % CORES) for i in range(CORES)]
    gate_other = lax.ppermute(gate_weight, "core", swap)
    up_other = lax.ppermute(up_weight, "core", swap)
    down_other = lax.ppermute(down_weight, "core", swap)

    floats = tokens.astype(f32)
    scale = lax.rsqrt(jnp.mean(floats * floats, axis=-1, keepdims=True) + EPSILON)
    chip_cols = lax.dynamic_slice_in_dim(tokens, x * chip_width, chip_width, 1)
    normed = (chip_cols.astype(f32) * scale).astype(bf16)

    slot_of = slot_index(route_ids)
    targets = (
        jnp.arange(EXPERTS, dtype=jnp.int32)[:, None] * CAP
        + core * part
        + jnp.arange(part, dtype=jnp.int32)[None, :]
    ).reshape(-1)
    matches = slot_of[:, :, None] == targets[None, None, :]
    combine = jnp.sum(jnp.where(matches, route_gates[:, :, None], 0.0), axis=1)
    picker = jnp.sum(matches.astype(f32), axis=1).astype(bf16)
    packed = jnp.dot(picker.T, normed, preferred_element_type=f32).astype(bf16)
    lanes = chip_width // 128
    packed = packed.reshape(EXPERTS, 1, part, lanes, 128)
    copies = far // EXPERTS
    sent = jnp.broadcast_to(packed, (EXPERTS, copies, part, lanes, 128))
    sent = sent.reshape(far, part, lanes, 128)
    arrived = lax.all_to_all(sent, "far", 0, 0, tiled=True)
    arrived = arrived.reshape(far * part, chip_width)
    rows = lax.all_gather(arrived, "near", axis=0, tiled=True)
    n_rows = rows.shape[0]
    full = from_everyone(rows, "x").reshape(xs, n_rows, chip_width)

    def project(weight):
        return jnp.einsum(
            "xsd,xdn->sn",
            full,
            weight.reshape(xs, chip_width, weight.shape[1]),
            preferred_element_type=f32,
        )

    hidden_own = (jax.nn.silu(project(gate_weight)) * project(up_weight)).astype(bf16)
    hidden_other = (jax.nn.silu(project(gate_other)) * project(up_other)).astype(bf16)
    first = core == 0
    hidden = jnp.concatenate(
        [
            jnp.where(first, hidden_own, hidden_other),
            jnp.where(first, hidden_other, hidden_own),
        ],
        axis=1,
    )
    units = from_everyone(hidden, "x")

    def down(weight):
        return jnp.einsum(
            "xsu,xun->sn",
            units.reshape(xs, n_rows, hidden.shape[1]),
            weight.reshape(xs, hidden.shape[1], out_width),
            preferred_element_type=f32,
        ).astype(bf16)

    produced = jnp.concatenate([down(down_weight), down(down_other)], axis=1)
    parts = lax.all_to_all(
        produced.reshape(near, far * part, 2 * out_width), "near", 0, 0, tiled=True
    )
    summed = jnp.sum(parts.astype(f32), axis=0).astype(bf16)
    out_lanes = 2 * out_width // 128
    returned = lax.all_to_all(
        summed.reshape(far, part, out_lanes, 128), "far", 0, 0, tiled=True
    )
    returned = jnp.sum(
        returned.reshape(EXPERTS, copies, part, out_lanes, 128).astype(f32), axis=1
    ).reshape(EXPERTS * part, 2 * out_width)
    mixture = jnp.dot(
        combine, returned, precision=lax.Precision.HIGHEST, preferred_element_type=f32
    )
    mixture = mixture[:, :out_width] + lax.ppermute(mixture[:, out_width:], "core", swap)
    residual = lax.dynamic_slice_in_dim(
        tokens, (x * CORES + core) * out_width, out_width, 1
    ).astype(f32)
    return (residual + mixture).astype(bf16)


def solution(mesh):
    groups, experts, tensor = (mesh.shape[n] for n in ("groups", "expert", "tensor"))
    fine = Mesh(
        mesh.devices.reshape(groups, experts // NEAR, NEAR, tensor // CORES, CORES),
        ("groups", "far", "near", "x", "core"),
    )
    tok = ("groups", "far", "near")
    in_specs = (
        P(tok, None),
        P(tok, None),
        P(tok, None),
        P(None, ("far", "near", "x", "core")),
        P(None, ("far", "near", "x", "core")),
        P(("far", "near"), ("x", "core")),
    )
    out_specs = P(tok, ("x", "core"))
    return jax.shard_map(local, mesh=fine, in_specs=in_specs, out_specs=out_specs, check_vma=False)
```

time: 334 us -> 235 us (0.70)
  waiting for transfers between devices: 154 us -> 33.8 us
  blocking collectives: 129 us -> 155 us
  between operations: 13.6 us -> 0.28 us
  starting transfers between devices: 12 us -> 24.6 us
    all_to_all x1 -> x3, blocking collectives: 44.6 us -> 132 us  [the longest x1 71.6 us: local(): arrived = lax.all_to_all(sent, 'far', 0, 0, tiled=True)]
    all_gather x1 -> x0, waiting for transfers between devices: 68.7 us -> none  [local(): lax.all_gather(normed, 'expert', axis=0, tiled=True)]
    all_gather x1, blocking collectives: 84.8 us -> 22.2 us  [local(): rows = lax.all_gather(arrived, 'near', axis=0, tiled=True)]
    all_to_all x1 -> x2, waiting for transfers between devices: 85.5 us -> 32.9 us  [from_everyone(): lax.all_to_all(jnp.broadcast_to(array[None], (devices, *array.shape)), ax...]
    ppermute x0 -> x4, starting transfers between devices: none -> 16.7 us  [the longest x1 7.04 us: local(): lax.ppermute(mixture[:, out_width:], 'core', swap)]
    all_to_all x1 -> x2, starting transfers between devices: 12 us -> 7.88 us  [from_everyone(): lax.all_to_all(jnp.broadcast_to(array[None], (devices, *array.shape)), ax...]
    dot_general x5 -> x8, matrix products: 13.5 us -> 11.5 us  [the longest x4 7.79 us: project(): jnp.einsum('xsd,xdn->sn', full, weight.reshape(xs, chip_width, weight.sha...]
  transfers between devices with their start and end apart: 2 -> 6, of which waited for: 2 -> 3; matrix products, arithmetic and copies ran while one was open for 1% -> 4% of each run, Pallas kernels for 0% -> 0%
where the time goes in v1:
time: 235 us; the launch traced here: 234 us
  blocking collectives  155 us (66%)
  waiting for transfers between devices  33.8 us (14%)
  starting transfers between devices  24.6 us (10%)
  matrix products  11.5 us (5%)
  other arithmetic  4.69 us (2%)
  local copies, waits for them, and re-layouts  4.39 us (2%)
    all_to_all x1, blocking collectives, local(): arrived = lax.all_to_all(sent, 'far', 0, 0, tiled=True)  71.6 us
    all_to_all x1, blocking collectives, local(): lax.all_to_all(summed.reshape(far, part, out_lanes, 128), 'far', 0, 0, ti...  40.5 us
    all_to_all x2, waiting for transfers between devices, from_everyone(): lax.all_to_all(jnp.broadcast_to(array[None], (devices, *array.shape)), ax...  32.9 us
    all_gather x1, blocking collectives, local(): rows = lax.all_gather(arrived, 'near', axis=0, tiled=True)  22.2 us
    all_to_all x1, blocking collectives, local(): lax.all_to_all(produced.reshape(near, far * part, 2 * out_width), 'near',...  20.3 us
    all_to_all x2, starting transfers between devices, from_everyone(): lax.all_to_all(jnp.broadcast_to(array[None], (devices, *array.shape)), ax...  7.88 us
    dot_general x4, matrix products, project(): jnp.einsum('xsd,xdn->sn', full, weight.reshape(xs, chip_width, weight.sha...  7.79 us
    ppermute x1, starting transfers between devices, local(): lax.ppermute(mixture[:, out_width:], 'core', swap)  7.04 us
  transfers between devices with their start and end apart: 6, of which 3 were waited for; matrix products, arithmetic and copies ran while one was open for 4% of the time, Pallas kernels for 0%

profile of v1, /device:TPU:33, one launch (start us, length us, event | category | flops | bytes accessed | tf_op | source)
XLA Modules:
  0.0 233.8 jit_solution(13434737378837629964)
XLA Ops:
  0.0 0.1 iota_add_fusion
  0.1 0.1 add.77
  0.2 0.8 copy.32
  0.9 0.1 eq.31
  1.0 0.1 fusion.14
  1.1 0.1 reduce_window_sum.11
  1.2 0.2 select_reduce_fusion
  1.4 0.1 reduce_sum.60
  1.5 0.1 copy.33
  1.6 0.7 multiply_add_fusion
  2.3 1.1 multiply_reduce_fusion
  3.4 0.8 fusion.13
  4.2 1.1 fusion.4
  5.3 71.6 %all_to_all.25 = bf16[8,12,8,128]{3,2,1,0:T(8,128)(2,1)S(1)} all-to-all(bf16[8,12,8,128]{3,2,1,0:T(8,128)(2,1)S(1)} %bitcast.66), channel_id=1, replica_groups=mesh['groups'=2,'far'=8,'near'=4,'x'=4,'core'=2] {'far'}, dimensions={0} | all-to-all | bytes 393216 | tf_op jit(solution)/shard_map/all_to_all | solution.py:63
  77.0 22.2 %all_gather.3 = bf16[384,1024]{1,0:T(8,128)(2,1)S(1)} all-gather(bf16[96,1024]{1,0:T(8,128)(2,1)S(1)} %bitcast.70), channel_id=1, replica_groups=mesh['groups'=2,'far'=8,'near'=4,'x'=4,'core'=2] {'near'}, dimensions={0}, use_global_device_ids=true | all-gather | bytes 983040 | tf_op jit(solution)/shard_map/all_gather | solution.py:65
  99.2 2.1 broadcast_in_dim.40
  101.2 4.3 %all-to-all-start.1 = ((bf16[4,384,1024]{2,1,0:T(8,128)(2,1)}), bf16[4,384,1024]{2,1,0:T(8,128)(2,1)S(1)}, u32[]{:S(2)}, u32[]{:S(2)}) async-start(bf16[4,384,1024]{2,1,0:T(8,128)(2,1)} %broadcast_in_dim.40), calls=%async_computation.1 | async-start | bytes 6291456 | tf_op jit(solution)/shard_map/all_to_all | solution.py:25
  105.5 5.2 %collective-permute-start = (bf16[4096,128]{1,0:T(8,128)(2,1)}, bf16[4096,128]{1,0:T(8,128)(2,1)}, u32[]{:S(2)}, u32[]{:S(2)}) collective-permute-start(bf16[4096,128]{1,0:T(8,128)(2,1)} %param.9), channel_id=1, source_target_pairs={{0,1},{1,0},{2,3},{3,2},{4,5},{5,4},{6,7},{7,6},{8,9},{9,8},{10,11... | collective-permute-start | bytes 3145736 | tf_op jit(solution)/shard_map/ppermute | solution.py:39
  110.8 2.0 collective-permute-start.1
  112.7 2.4 %collective-permute-start.2 = (bf16[1024,512]{1,0:T(8,128)(2,1)}, bf16[1024,512]{1,0:T(8,128)(2,1)}, u32[]{:S(2)}, u32[]{:S(2)}) collective-permute-start(bf16[1024,512]{1,0:T(8,128)(2,1)} %param.11), channel_id=1, source_target_pairs={{0,1},{1,0},{2,3},{3,2},{4,5},{5,4},{6,7},{7,6},{8,9},{9,8},{10,11... | collective-permute-start | bytes 3145736 | tf_op jit(solution)/shard_map/ppermute | solution.py:41
  115.2 24.7 %all-to-all-done.1 = bf16[4,384,1024]{2,1,0:T(8,128)(2,1)S(1)} async-done(((bf16[4,384,1024]{2,1,0:T(8,128)(2,1)}), bf16[4,384,1024]{2,1,0:T(8,128)(2,1)S(1)}, u32[]{:S(2)}, u32[]{:S(2)}) %all-to-all-start.1) | async-done | bytes 3145760 | tf_op jit(solution)/shard_map/all_to_all | solution.py:25
  139.9 2.2 convolution_bitcast_fusion.5
  142.1 0.0 copy-start
  142.1 0.0 collective-permute-done
  142.1 2.3 convolution_bitcast_fusion.3
  144.4 0.0 copy-done
  144.4 1.0 fusion.3
  145.5 0.0 collective-permute-done.1
  145.5 2.2 broadcast_select_fusion.1
  147.7 0.0 copy-start.1
  147.8 0.1 copy.38
  148.0 0.9 broadcast_in_dim.41
  148.9 3.6 %all-to-all-start.2 = ((bf16[4,384,256]{2,1,0:T(8,128)(2,1)}), bf16[4,384,256]{2,1,0:T(8,128)(2,1)S(1)}, u32[]{:S(2)}, u32[]{:S(2)}) async-start(bf16[4,384,256]{2,1,0:T(8,128)(2,1)} %broadcast_in_dim.41), calls=%async_computation.2 | async-start | bytes 1572864 | tf_op jit(solution)/shard_map/all_to_all | solution.py:25
  152.5 0.0 collective-permute-done.2
  152.5 8.2 %all-to-all-done.2 = bf16[4,384,256]{2,1,0:T(8,128)(2,1)S(1)} async-done(((bf16[4,384,256]{2,1,0:T(8,128)(2,1)}), bf16[4,384,256]{2,1,0:T(8,128)(2,1)S(1)}, u32[]{:S(2)}, u32[]{:S(2)}) %all-to-all-start.2) | async-done | bytes 786464 | tf_op jit(solution)/shard_map/all_to_all | solution.py:25
  160.7 1.8 fusion.1
  162.5 0.0 copy-done.1
  162.5 0.6 fusion
  163.1 0.1 pad_maximum_fusion
  163.2 20.3 %all_to_all.26 = bf16[4,96,1024]{2,1,0:T(8,128)(2,1)S(1)} all-to-all(bf16[4,96,1024]{2,1,0:T(8,128)(2,1)S(1)} %bitcast.62), channel_id=1, replica_groups=mesh['groups'=2,'far'=8,'near'=4,'x'=4,'core'=2] {'near'}, dimensions={0} | all-to-all | bytes 1572864 | tf_op jit(solution)/shard_map/all_to_all | solution.py:98
  183.5 0.1 reduce_sum.64
  183.7 40.5 %all_to_all.27 = bf16[8,12,8,128]{3,2,1,0:T(8,128)(2,1)S(1)} all-to-all(bf16[8,12,8,128]{3,2,1,0:T(8,128)(2,1)S(1)} %bitcast.68), channel_id=1, replica_groups=mesh['groups'=2,'far'=8,'near'=4,'x'=4,'core'=2] {'far'}, dimensions={0} | all-to-all | bytes 393216 | tf_op jit(solution)/shard_map/all_to_all | solution.py:103
  224.2 0.3 fusion.5
  224.5 7.0 %collective-permute-start.3 = (f32[32,512]{1,0:T(8,128)S(1)}, f32[32,512]{1,0:T(8,128)S(1)}, u32[]{:S(2)}, u32[]{:S(2)}) collective-permute-start(f32[32,512]{1,0:T(8,128)S(1)} %slice.9), channel_id=1, source_target_pairs={{0,1},{1,0},{2,3},{3,2},{4,5},{5,4},{6,7},{7,6},{8,9},{9,8},{10,11... | collective-permute-start | bytes 196616 | tf_op jit(solution)/shard_map/ppermute | solution.py:112
  231.6 0.9 collective-permute-done.3
  232.5 1.4 fusion.9
  (10 shorter events, 0.2 us)
Async XLA Ops:
  101.2 38.7 %all-to-all-start.1 = ((bf16[4,384,1024]{2,1,0:T(8,128)(2,1)}), bf16[4,384,1024]{2,1,0:T(8,128)(2,1)S(1)}, u32[]{:S(2)}, u32[]{:S(2)}) async-start(bf16[4,384,1024]{2,1,0:T(8,128)(2,1)} %broadcast_in_dim.40), calls=%async_computation.1 | async-start | bytes 6291456 | tf_op jit(solution)/shard_map/all_to_all | solution.py:25
  105.5 36.6 %collective-permute-start = (bf16[4096,128]{1,0:T(8,128)(2,1)}, bf16[4096,128]{1,0:T(8,128)(2,1)}, u32[]{:S(2)}, u32[]{:S(2)}) collective-permute-start(bf16[4096,128]{1,0:T(8,128)(2,1)} %param.9), channel_id=1, source_target_pairs={{0,1},{1,0},{2,3},{3,2},{4,5},{5,4},{6,7},{7,6},{8,9},{9,8},{10,11... | collective-permute-start | bytes 3145736 | tf_op jit(solution)/shard_map/ppermute | solution.py:39
  110.8 34.7 %collective-permute-start.1 = (bf16[4096,128]{1,0:T(8,128)(2,1)}, bf16[4096,128]{1,0:T(8,128)(2,1)}, u32[]{:S(2)}, u32[]{:S(2)}) collective-permute-start(bf16[4096,128]{1,0:T(8,128)(2,1)} %param.10), channel_id=1, source_target_pairs={{0,1},{1,0},{2,3},{3,2},{4,5},{5,4},{6,7},{7,6},{8,9},{9,8},{10,11... | collective-permute-start | bytes 3145736 | tf_op jit(solution)/shard_map/ppermute | solution.py:40
  112.7 39.8 %collective-permute-start.2 = (bf16[1024,512]{1,0:T(8,128)(2,1)}, bf16[1024,512]{1,0:T(8,128)(2,1)}, u32[]{:S(2)}, u32[]{:S(2)}) collective-permute-start(bf16[1024,512]{1,0:T(8,128)(2,1)} %param.11), channel_id=1, source_target_pairs={{0,1},{1,0},{2,3},{3,2},{4,5},{5,4},{6,7},{7,6},{8,9},{9,8},{10,11... | collective-permute-start | bytes 3145736 | tf_op jit(solution)/shard_map/ppermute | solution.py:41
  142.1 2.3 copy-start
  147.7 14.8 %copy-start.1 = (bf16[1024,512]{1,0:T(8,128)(2,1)S(1)}, bf16[1024,512]{1,0:T(8,128)(2,1)}, u32[]{:S(2)}) copy-start(bf16[1024,512]{1,0:T(8,128)(2,1)} %param.11) | copy-start | bytes 3145732
  148.9 11.8 %all-to-all-start.2 = ((bf16[4,384,256]{2,1,0:T(8,128)(2,1)}), bf16[4,384,256]{2,1,0:T(8,128)(2,1)S(1)}, u32[]{:S(2)}, u32[]{:S(2)}) async-start(bf16[4,384,256]{2,1,0:T(8,128)(2,1)} %broadcast_in_dim.41), calls=%async_computation.2 | async-start | bytes 1572864 | tf_op jit(solution)/shard_map/all_to_all | solution.py:25
  224.5 7.9 %collective-permute-start.3 = (f32[32,512]{1,0:T(8,128)S(1)}, f32[32,512]{1,0:T(8,128)S(1)}, u32[]{:S(2)}, u32[]{:S(2)}) collective-permute-start(f32[32,512]{1,0:T(8,128)S(1)} %slice.9), channel_id=1, source_target_pairs={{0,1},{1,0},{2,3},{3,2},{4,5},{5,4},{6,7},{7,6},{8,9},{9,8},{10,11... | collective-permute-start | bytes 196616 | tf_op jit(solution)/shard_map/ppermute | solution.py:112

commit v2 on v1

--- a/solution.py
+++ b/solution.py
@@ -1,10 +1,11 @@
 import jax
 import jax.numpy as jnp
 from jax import lax
+from jax.experimental import pallas as pl
 from jax.sharding import Mesh, PartitionSpec as P
 
+
 EXPERTS = 4
-TOP = 2
 CAP = 24
 NEAR = 4
 CORES = 2
@@ -27,17 +28,55 @@
     )
 
 
-def local(tokens, route_ids, route_gates, gate_weight, up_weight, down_weight):
+def product_kernel(rows, own, other, out):
+    both = jnp.concatenate([own[0, 0], other[0, 0]], axis=1)
+    product = jnp.dot(rows[...], both, preferred_element_type=jnp.float32)
+    width = own.shape[-1]
+    out[0, 0] = product[:, :width].astype(out.dtype)
+    out[1, 0] = product[:, width:].astype(out.dtype)
+
+
+def products(rows, own, other, shift, dtype):
+    n_rows, depth = rows.shape
+    kinds, width = own.shape[1], own.shape[3]
+    weight_spec = pl.BlockSpec((1, 1, depth, width), lambda kind: (shift, kind, 0, 0))
+    return pl.pallas_call(
+        product_kernel,
+        grid=(kinds,),
+        in_specs=[pl.BlockSpec((n_rows, depth), lambda kind: (0, 0)), weight_spec, weight_spec],
+        out_specs=pl.BlockSpec((CORES, 1, n_rows, width), lambda kind: (0, kind, 0, 0)),
+        out_shape=jax.ShapeDtypeStruct((CORES, kinds, n_rows, width), dtype),
+        cost_estimate=pl.CostEstimate(
+            flops=2 * n_rows * depth * width * kinds * CORES,
+            bytes_accessed=2 * depth * width * kinds * CORES,
+            transcendentals=0,
+        ),
+    )(rows, own, other)
+
+
+def layer(tokens, route_ids, route_gates, gate_weight, up_weight, down_weight):
     f32, bf16 = jnp.float32, jnp.bfloat16
-    tok_count, model_width = tokens.shape
+    _, model_width = tokens.shape
     far, near, xs = lax.axis_size("far"), lax.axis_size("near"), lax.axis_size("x")
     core, x = lax.axis_index("core"), lax.axis_index("x")
     part = CAP // CORES
     chip_width = model_width // xs
     out_width = down_weight.shape[1]
     swap = [(i, (i + 1) % CORES) for i in range(CORES)]
-    gate_other = lax.ppermute(gate_weight, "core", swap)
-    up_other = lax.ppermute(up_weight, "core", swap)
+
+    def chunk(shift):
+        start = (x + shift) % xs * chip_width
+        return jnp.stack(
+            [
+                lax.dynamic_slice_in_dim(weight, start, chip_width, 0)
+                for weight in (gate_weight, up_weight)
+            ]
+        )
+
+    chunks = [chunk(0)]
+    for shift in range(1, xs):
+        chunks.append(lax.ppermute(chunk(shift), "x", [(i, (i + shift) % xs) for i in range(xs)]))
+    own = jnp.stack(chunks)
     down_other = lax.ppermute(down_weight, "core", swap)
 
     floats = tokens.astype(f32)
@@ -61,21 +100,19 @@
     sent = jnp.broadcast_to(packed, (EXPERTS, copies, part, lanes, 128))
     sent = sent.reshape(far, part, lanes, 128)
     arrived = lax.all_to_all(sent, "far", 0, 0, tiled=True)
-    arrived = arrived.reshape(far * part, chip_width)
+    arrived, own = lax.optimization_barrier((arrived.reshape(far * part, chip_width), own))
+    other = lax.ppermute(own, "core", swap)
     rows = lax.all_gather(arrived, "near", axis=0, tiled=True)
     n_rows = rows.shape[0]
-    full = from_everyone(rows, "x").reshape(xs, n_rows, chip_width)
 
-    def project(weight):
-        return jnp.einsum(
-            "xsd,xdn->sn",
-            full,
-            weight.reshape(xs, chip_width, weight.shape[1]),
-            preferred_element_type=f32,
-        )
-
-    hidden_own = (jax.nn.silu(project(gate_weight)) * project(up_weight)).astype(bf16)
-    hidden_other = (jax.nn.silu(project(gate_other)) * project(up_other)).astype(bf16)
+    total = products(rows, own, other, 0, f32)
+    for shift in range(1, xs):
+        total = total + lax.ppermute(
+            products(rows, own, other, shift, bf16),
+            "x",
+            [(i, (i - shift) % xs) for i in range(xs)],
+        ).astype(f32)
+    hidden_own, hidden_other = (jax.nn.silu(total[:, 0]) * total[:, 1]).astype(bf16)
     first = core == 0
     hidden = jnp.concatenate(
         [
@@ -132,4 +169,4 @@
         P(("far", "near"), ("x", "core")),
     )
     out_specs = P(tok, ("x", "core"))
-    return jax.shard_map(local, mesh=fine, in_specs=in_specs, out_specs=out_specs, check_vma=False)
+    return jax.shard_map(layer, mesh=fine, in_specs=in_specs, out_specs=out_specs, check_vma=False)

time: 235 us -> 241 us (1.026)
  blocking collectives: 155 us -> 94.2 us
  starting transfers between devices: 24.6 us -> 81.1 us
  Pallas kernels: 0 us -> 11.2 us
  matrix products: 11.5 us -> 3.7 us
  waiting for transfers between devices: 33.8 us -> 39.1 us
    all_to_all x3 -> x2, blocking collectives: 132 us -> 75.1 us  [the longest x1 52.2 us: layer(): lax.all_to_all(summed.reshape(far, part, out_lanes, 128), 'far', 0, 0, ti...]
    all_to_all x0 -> x1, starting transfers between devices: none -> 44 us  [layer(): arrived = lax.all_to_all(sent, 'far', 0, 0, tiled=True)]
    ppermute x4 -> x9, waiting for transfers between devices: 0.88 us -> 28.8 us  [the longest x3 23.5 us: layer(): lax.ppermute(chunk(shift), 'x', [(i, (i + shift) % xs) for i in range(xs)])]
    all_to_all x2 -> x1, waiting for transfers between devices: 32.9 us -> 10.4 us  [from_everyone(): lax.all_to_all(jnp.broadcast_to(array[None], (devices, *array.shape)), ax...]
    ppermute x4 -> x9, starting transfers between devices: 16.7 us -> 32.5 us  [the longest x3 9.69 us: layer(): lax.ppermute(chunk(shift), 'x', [(i, (i + shift) % xs) for i in range(xs)])]
    pallas_call x0 -> x4, Pallas kernels: none -> 11.2 us  [products(): pl.pallas_call(product_kernel, grid=(kinds,), in_specs=[pl.BlockSpec((n_r...]
    dot_general x6 -> x2, matrix products: 9.13 us -> 1.35 us  [the longest x1 1.06 us: layer(): packed = jnp.dot(picker.T, normed, preferred_element_type=f32).astype(bf16)]
    all_to_all x2 -> x1, starting transfers between devices: 7.88 us -> 4.59 us  [from_everyone(): lax.all_to_all(jnp.broadcast_to(array[None], (devices, *array.shape)), ax...]
  transfers between devices with their start and end apart: 6 -> 11, of which waited for: 3 -> 6; matrix products, arithmetic and copies ran while one was open for 4% -> 2% of each run, Pallas kernels for 0% -> 3%
where the time goes in v2:
time: 241 us; the launch traced here: 240 us
  blocking collectives  94.2 us (39%)
  starting transfers between devices  81.1 us (34%)
  waiting for transfers between devices  39.1 us (16%)
  Pallas kernels  11.2 us (5%)
  other arithmetic  6.57 us (3%)
  local copies, waits for them, and re-layouts  4.31 us (2%)
  matrix products  3.7 us (2%)
    all_to_all x1, blocking collectives, layer(): lax.all_to_all(summed.reshape(far, part, out_lanes, 128), 'far', 0, 0, ti...  52.2 us
    all_to_all x1, starting transfers between devices, layer(): arrived = lax.all_to_all(sent, 'far', 0, 0, tiled=True)  44 us
    ppermute x3, waiting for transfers between devices, layer(): lax.ppermute(chunk(shift), 'x', [(i, (i + shift) % xs) for i in range(xs)])  23.5 us
    all_to_all x1, blocking collectives, layer(): lax.all_to_all(produced.reshape(near, far * part, 2 * out_width), 'near',...  22.9 us
    all_gather x1, blocking collectives, layer(): rows = lax.all_gather(arrived, 'near', axis=0, tiled=True)  19 us
    pallas_call x4, Pallas kernels, products(): pl.pallas_call(product_kernel, grid=(kinds,), in_specs=[pl.BlockSpec((n_r...  11.2 us
    all_to_all x1, waiting for transfers between devices, from_everyone(): lax.all_to_all(jnp.broadcast_to(array[None], (devices, *array.shape)), ax...  10.4 us
    ppermute x3, starting transfers between devices, layer(): lax.ppermute(chunk(shift), 'x', [(i, (i + shift) % xs) for i in range(xs)])  9.69 us
  transfers between devices with their start and end apart: 11, of which 6 were waited for; matrix products, arithmetic and copies ran while one was open for 2% of the time, Pallas kernels for 3%

profile of v2, /device:TPU:33, one launch (start us, length us, event | category | flops | bytes accessed | tf_op | source)
XLA Modules:
  0.0 240.5 jit_solution(5791791708044392918)
XLA Ops:
  0.1 0.1 add.121
  0.2 0.8 copy.22
  1.0 0.1 eq.36
  1.1 0.1 fusion.14
  1.2 0.1 reduce_window_sum.11
  1.3 0.2 select_reduce_fusion
  1.5 0.1 reduce_sum.60
  1.6 0.1 copy.23
  1.7 0.7 multiply_add_fusion
  2.4 1.1 multiply_reduce_fusion
  3.5 0.8 fusion.13
  4.3 1.1 fusion.2
  5.4 0.7 broadcast_in_dim.33
  6.1 44.0 %all-to-all-start = ((bf16[8,12,8,128]{3,2,1,0:T(8,128)(2,1)}), bf16[8,12,8,128]{3,2,1,0:T(8,128)(2,1)S(1)}, u32[]{:S(2)}, u32[]{:S(2)}) async-start(bf16[8,12,8,128]{3,2,1,0:T(8,128)(2,1)} %bitcast), calls=%async_computation | async-start | bytes 393216 | tf_op jit(solution)/shard_map/all_to_all | solution.py:102
  50.1 1.4 dynamic-slice_bitcast_fusion.6
  51.5 4.8 %collective-permute-start.2 = (bf16[2,1024,128]{2,1,0:T(8,128)(2,1)S(1)}, bf16[2,1024,128]{2,1,0:T(8,128)(2,1)S(1)}, u32[]{:S(2)}, u32[]{:S(2)}) collective-permute-start(bf16[2,1024,128]{2,1,0:T(8,128)(2,1)S(1)} %pad_maximum_fusion.4), channel_id=1, source_target_pairs={{0,6},{2,0},{4,2},{6,4},{1,7},{3,1},{5,3},{7,5},{8,14},{10,8},{12,... | collective-permute-start | bytes 1572872 | tf_op jit(solution)/shard_map/ppermute | solution.py:78
  56.4 2.2 collective-permute-start.1
  58.6 2.7 %collective-permute-start = (bf16[2,1024,128]{2,1,0:T(8,128)(2,1)S(1)}, bf16[2,1024,128]{2,1,0:T(8,128)(2,1)S(1)}, u32[]{:S(2)}, u32[]{:S(2)}) collective-permute-start(bf16[2,1024,128]{2,1,0:T(8,128)(2,1)S(1)} %pad_maximum_fusion.2), channel_id=1, source_target_pairs={{0,2},{2,4},{4,6},{6,0},{1,3},{3,5},{5,7},{7,1},{8,10},{10,12},{12... | collective-permute-start | bytes 1572872 | tf_op jit(solution)/shard_map/ppermute | solution.py:78
  61.4 6.7 %collective-permute-done.2 = bf16[2,1024,128]{2,1,0:T(8,128)(2,1)S(1)} collective-permute-done((bf16[2,1024,128]{2,1,0:T(8,128)(2,1)S(1)}, bf16[2,1024,128]{2,1,0:T(8,128)(2,1)S(1)}, u32[]{:S(2)}, u32[]{:S(2)}) %collective-permute-start.2) | collective-permute-done | bytes 524320 | tf_op jit(solution)/shard_map/ppermute | solution.py:78
  68.1 4.0 %collective-permute-done.1 = bf16[2,1024,128]{2,1,0:T(8,128)(2,1)S(1)} collective-permute-done((bf16[2,1024,128]{2,1,0:T(8,128)(2,1)S(1)}, bf16[2,1024,128]{2,1,0:T(8,128)(2,1)S(1)}, u32[]{:S(2)}, u32[]{:S(2)}) %collective-permute-start.1) | collective-permute-done | bytes 524320 | tf_op jit(solution)/shard_map/ppermute | solution.py:78
  72.2 12.7 %collective-permute-done = bf16[2,1024,128]{2,1,0:T(8,128)(2,1)S(1)} collective-permute-done((bf16[2,1024,128]{2,1,0:T(8,128)(2,1)S(1)}, bf16[2,1024,128]{2,1,0:T(8,128)(2,1)S(1)}, u32[]{:S(2)}, u32[]{:S(2)}) %collective-permute-start) | collective-permute-done | bytes 524320 | tf_op jit(solution)/shard_map/ppermute | solution.py:78
  84.9 0.3 pad_maximum_fusion.own
  85.2 2.4 %collective-permute-start.3 = (bf16[4,2,1024,128]{3,2,1,0:T(8,128)(2,1)S(1)}, bf16[4,2,1024,128]{3,2,1,0:T(8,128)(2,1)}, u32[]{:S(2)}, u32[]{:S(2)}) collective-permute-start(bf16[4,2,1024,128]{3,2,1,0:T(8,128)(2,1)S(1)} %pad_maximum_fusion.own), channel_id=1, source_target_pairs={{0,1},{1,0},{2,3},{3,2},{4,5},{5,4},{6,7},{7,6},{8,9},{9,8},{10,11... | collective-permute-start | bytes 6291464 | tf_op jit(solution)/shard_map/ppermute | solution.py:104
  87.6 19.0 %all_gather.3.rows = bf16[384,1024]{1,0:T(8,128)(2,1)} all-gather(bf16[96,1024]{1,0:T(8,128)(2,1)S(1)} %bitcast.80), channel_id=1, replica_groups=mesh['groups'=2,'far'=8,'near'=4,'x'=4,'core'=2] {'near'}, dimensions={0}, use_global_device_ids=true | all-gather | bytes 983040 | tf_op jit(solution)/shard_map/all_gather | solution.py:105
  106.7 2.8 %shard_map.67 = bf16[2,2,384,128]{3,2,1,0:T(8,128)(2,1)} custom-call(bf16[384,1024]{1,0:T(8,128)(2,1)} %all_gather.3.rows, bf16[4,2,1024,128]{3,2,1,0:T(8,128)(2,1)} %copy-done, bf16[4,2,1024,128]{3,2,1,0:T(8,128)(2,1)} %collective-permute-done.3.other), custom_call_target="tpu_custom_call" | custom-call | flops 402653184 | bytes 1048576 | tf_op jit(solution)/shard_map/pallas_call | solution.py:43
  109.5 1.9 collective-permute-start.6
  111.4 2.8 %shard_map.66 = bf16[2,2,384,128]{3,2,1,0:T(8,128)(2,1)} custom-call(bf16[384,1024]{1,0:T(8,128)(2,1)} %all_gather.3.rows, bf16[4,2,1024,128]{3,2,1,0:T(8,128)(2,1)} %copy-done, bf16[4,2,1024,128]{3,2,1,0:T(8,128)(2,1)} %collective-permute-done.3.other), custom_call_target="tpu_custom_call" | custom-call | flops 402653184 | bytes 1048576 | tf_op jit(solution)/shard_map/pallas_call | solution.py:43
  114.2 3.6 %collective-permute-start.5 = (bf16[2,2,384,128]{3,2,1,0:T(8,128)(2,1)}, bf16[2,2,384,128]{3,2,1,0:T(8,128)(2,1)S(1)}, u32[]{:S(2)}, u32[]{:S(2)}) collective-permute-start(bf16[2,2,384,128]{3,2,1,0:T(8,128)(2,1)} %shard_map.66), channel_id=1, source_target_pairs={{0,4},{2,6},{4,0},{6,2},{1,5},{3,7},{5,1},{7,3},{8,12},{10,14},{12... | collective-permute-start | bytes 1179656 | tf_op jit(solution)/shard_map/ppermute | solution.py:110
  117.8 2.8 %shard_map.65 = bf16[2,2,384,128]{3,2,1,0:T(8,128)(2,1)} custom-call(bf16[384,1024]{1,0:T(8,128)(2,1)} %all_gather.3.rows, bf16[4,2,1024,128]{3,2,1,0:T(8,128)(2,1)} %copy-done, bf16[4,2,1024,128]{3,2,1,0:T(8,128)(2,1)} %collective-permute-done.3.other), custom_call_target="tpu_custom_call" | custom-call | flops 402653184 | bytes 1048576 | tf_op jit(solution)/shard_map/pallas_call | solution.py:43
  120.6 3.1 %collective-permute-start.4 = (bf16[2,2,384,128]{3,2,1,0:T(8,128)(2,1)}, bf16[2,2,384,128]{3,2,1,0:T(8,128)(2,1)S(1)}, u32[]{:S(2)}, u32[]{:S(2)}) collective-permute-start(bf16[2,2,384,128]{3,2,1,0:T(8,128)(2,1)} %shard_map.65), channel_id=1, source_target_pairs={{0,6},{2,0},{4,2},{6,4},{1,7},{3,1},{5,3},{7,5},{8,14},{10,8},{12,... | collective-permute-start | bytes 1179656 | tf_op jit(solution)/shard_map/ppermute | solution.py:110
  123.7 4.9 %collective-permute-start.7 = (bf16[1024,512]{1,0:T(8,128)(2,1)S(1)}, bf16[1024,512]{1,0:T(8,128)(2,1)}, u32[]{:S(2)}, u32[]{:S(2)}) collective-permute-start(bf16[1024,512]{1,0:T(8,128)(2,1)S(1)} %copy-done.2), channel_id=1, source_target_pairs={{0,1},{1,0},{2,3},{3,2},{4,5},{5,4},{6,7},{7,6},{8,9},{9,8},{10,11... | collective-permute-start | bytes 3145736 | tf_op jit(solution)/shard_map/ppermute | solution.py:80
  128.6 2.8 %shard_map.64 = f32[2,2,384,128]{3,2,1,0:T(8,128)} custom-call(bf16[384,1024]{1,0:T(8,128)(2,1)} %all_gather.3.rows, bf16[4,2,1024,128]{3,2,1,0:T(8,128)(2,1)} %copy-done, bf16[4,2,1024,128]{3,2,1,0:T(8,128)(2,1)} %collective-permute-done.3.other), custom_call_target="tpu_custom_call" | custom-call | flops 402653184 | bytes 1048576 | tf_op jit(solution)/shard_map/pallas_call | solution.py:43
  131.5 4.4 %collective-permute-done.4 = bf16[2,2,384,128]{3,2,1,0:T(8,128)(2,1)S(1)} collective-permute-done((bf16[2,2,384,128]{3,2,1,0:T(8,128)(2,1)}, bf16[2,2,384,128]{3,2,1,0:T(8,128)(2,1)S(1)}, u32[]{:S(2)}, u32[]{:S(2)}) %collective-permute-start.4) | collective-permute-done | bytes 393248 | tf_op jit(solution)/shard_map/ppermute | solution.py:110
  135.8 1.3 convert_add_fusion
  137.1 0.1 fusion.4
  137.3 0.9 broadcast_in_dim.34
  138.2 4.6 %all-to-all-start.1 = ((bf16[4,384,256]{2,1,0:T(8,128)(2,1)}), bf16[4,384,256]{2,1,0:T(8,128)(2,1)S(1)}, u32[]{:S(2)}, u32[]{:S(2)}) async-start(bf16[4,384,256]{2,1,0:T(8,128)(2,1)} %broadcast_in_dim.34), calls=%async_computation.1 | async-start | bytes 1572864 | tf_op jit(solution)/shard_map/all_to_all | solution.py:26
  142.8 10.4 %all-to-all-done.1 = bf16[4,384,256]{2,1,0:T(8,128)(2,1)S(1)} async-done(((bf16[4,384,256]{2,1,0:T(8,128)(2,1)}), bf16[4,384,256]{2,1,0:T(8,128)(2,1)S(1)}, u32[]{:S(2)}, u32[]{:S(2)}) %all-to-all-start.1) | async-done | bytes 786464 | tf_op jit(solution)/shard_map/all_to_all | solution.py:26
  153.2 1.8 fusion.1
  155.0 0.6 fusion
  155.6 0.1 pad_maximum_fusion.1
  155.7 22.9 %all_to_all.20 = bf16[4,96,1024]{2,1,0:T(8,128)(2,1)S(1)} all-to-all(bf16[4,96,1024]{2,1,0:T(8,128)(2,1)S(1)} %bitcast.75), channel_id=1, replica_groups=mesh['groups'=2,'far'=8,'near'=4,'x'=4,'core'=2] {'near'}, dimensions={0} | all-to-all | bytes 1572864 | tf_op jit(solution)/shard_map/all_to_all | solution.py:135
  178.6 0.1 reduce_sum.64
  178.8 52.2 %all_to_all.21 = bf16[8,12,8,128]{3,2,1,0:T(8,128)(2,1)S(1)} all-to-all(bf16[8,12,8,128]{3,2,1,0:T(8,128)(2,1)S(1)} %bitcast.78), channel_id=1, replica_groups=mesh['groups'=2,'far'=8,'near'=4,'x'=4,'core'=2] {'far'}, dimensions={0} | all-to-all | bytes 393216 | tf_op jit(solution)/shard_map/all_to_all | solution.py:140
  231.0 0.3 fusion.5
  231.3 6.8 %collective-permute-start.8 = (f32[32,512]{1,0:T(8,128)S(1)}, f32[32,512]{1,0:T(8,128)S(1)}, u32[]{:S(2)}, u32[]{:S(2)}) collective-permute-start(f32[32,512]{1,0:T(8,128)S(1)} %slice.19), channel_id=1, source_target_pairs={{0,1},{1,0},{2,3},{3,2},{4,5},{5,4},{6,7},{7,6},{8,9},{9,8},{10,11... | collective-permute-start | bytes 196616 | tf_op jit(solution)/shard_map/ppermute | solution.py:149
  238.2 0.9 collective-permute-done.8
  239.1 1.4 fusion.9
  (25 shorter events, 0.5 us)
Async XLA Ops:
  0.0 50.1 %copy-start.1 = (bf16[4096,128]{1,0:T(8,128)(2,1)S(1)}, bf16[4096,128]{1,0:T(8,128)(2,1)}, u32[]{:S(2)}) copy-start(bf16[4096,128]{1,0:T(8,128)(2,1)} %param.10) | copy-start | bytes 3145732
  6.1 79.1 %all-to-all-start = ((bf16[8,12,8,128]{3,2,1,0:T(8,128)(2,1)}), bf16[8,12,8,128]{3,2,1,0:T(8,128)(2,1)S(1)}, u32[]{:S(2)}, u32[]{:S(2)}) async-start(bf16[8,12,8,128]{3,2,1,0:T(8,128)(2,1)} %bitcast), calls=%async_computation | async-start | bytes 393216 | tf_op jit(solution)/shard_map/all_to_all | solution.py:102
  51.5 16.6 %collective-permute-start.2 = (bf16[2,1024,128]{2,1,0:T(8,128)(2,1)S(1)}, bf16[2,1024,128]{2,1,0:T(8,128)(2,1)S(1)}, u32[]{:S(2)}, u32[]{:S(2)}) collective-permute-start(bf16[2,1024,128]{2,1,0:T(8,128)(2,1)S(1)} %pad_maximum_fusion.4), channel_id=1, source_target_pairs={{0,6},{2,0},{4,2},{6,4},{1,7},{3,1},{5,3},{7,5},{8,14},{10,8},{12,... | collective-permute-start | bytes 1572872 | tf_op jit(solution)/shard_map/ppermute | solution.py:78
  56.4 15.8 %collective-permute-start.1 = (bf16[2,1024,128]{2,1,0:T(8,128)(2,1)S(1)}, bf16[2,1024,128]{2,1,0:T(8,128)(2,1)S(1)}, u32[]{:S(2)}, u32[]{:S(2)}) collective-permute-start(bf16[2,1024,128]{2,1,0:T(8,128)(2,1)S(1)} %pad_maximum_fusion.3), channel_id=1, source_target_pairs={{0,4},{2,6},{4,0},{6,2},{1,5},{3,7},{5,1},{7,3},{8,12},{10,14},{12... | collective-permute-start | bytes 1572872 | tf_op jit(solution)/shard_map/ppermute | solution.py:78
  58.6 26.3 %collective-permute-start = (bf16[2,1024,128]{2,1,0:T(8,128)(2,1)S(1)}, bf16[2,1024,128]{2,1,0:T(8,128)(2,1)S(1)}, u32[]{:S(2)}, u32[]{:S(2)}) collective-permute-start(bf16[2,1024,128]{2,1,0:T(8,128)(2,1)S(1)} %pad_maximum_fusion.2), channel_id=1, source_target_pairs={{0,2},{2,4},{4,6},{6,0},{1,3},{3,5},{5,7},{7,1},{8,10},{10,12},{12... | collective-permute-start | bytes 1572872 | tf_op jit(solution)/shard_map/ppermute | solution.py:78
  85.1 21.5 %copy-start = (bf16[4,2,1024,128]{3,2,1,0:T(8,128)(2,1)}, bf16[4,2,1024,128]{3,2,1,0:T(8,128)(2,1)S(1)}, u32[]{:S(2)}) copy-start(bf16[4,2,1024,128]{3,2,1,0:T(8,128)(2,1)S(1)} %pad_maximum_fusion.own) | copy-start | bytes 6291460
  85.2 21.5 %collective-permute-start.3 = (bf16[4,2,1024,128]{3,2,1,0:T(8,128)(2,1)S(1)}, bf16[4,2,1024,128]{3,2,1,0:T(8,128)(2,1)}, u32[]{:S(2)}, u32[]{:S(2)}) collective-permute-start(bf16[4,2,1024,128]{3,2,1,0:T(8,128)(2,1)S(1)} %pad_maximum_fusion.own), channel_id=1, source_target_pairs={{0,1},{1,0},{2,3},{3,2},{4,5},{5,4},{6,7},{7,6},{8,9},{9,8},{10,11... | collective-permute-start | bytes 6291464 | tf_op jit(solution)/shard_map/ppermute | solution.py:104
  109.5 22.0 %collective-permute-start.6 = (bf16[2,2,384,128]{3,2,1,0:T(8,128)(2,1)}, bf16[2,2,384,128]{3,2,1,0:T(8,128)(2,1)S(1)}, u32[]{:S(2)}, u32[]{:S(2)}) collective-permute-start(bf16[2,2,384,128]{3,2,1,0:T(8,128)(2,1)} %shard_map.67), channel_id=1, source_target_pairs={{0,2},{2,4},{4,6},{6,0},{1,3},{3,5},{5,7},{7,1},{8,10},{10,12},{12... | collective-permute-start | bytes 1179656 | tf_op jit(solution)/shard_map/ppermute | solution.py:110
  114.2 9.5 %copy-start.2 = (bf16[1024,512]{1,0:T(8,128)(2,1)S(1)}, bf16[1024,512]{1,0:T(8,128)(2,1)}, u32[]{:S(2)}) copy-start(bf16[1024,512]{1,0:T(8,128)(2,1)} %param.11) | copy-start | bytes 3145732
  114.2 17.2 %collective-permute-start.5 = (bf16[2,2,384,128]{3,2,1,0:T(8,128)(2,1)}, bf16[2,2,384,128]{3,2,1,0:T(8,128)(2,1)S(1)}, u32[]{:S(2)}, u32[]{:S(2)}) collective-permute-start(bf16[2,2,384,128]{3,2,1,0:T(8,128)(2,1)} %shard_map.66), channel_id=1, source_target_pairs={{0,4},{2,6},{4,0},{6,2},{1,5},{3,7},{5,1},{7,3},{8,12},{10,14},{12... | collective-permute-start | bytes 1179656 | tf_op jit(solution)/shard_map/ppermute | solution.py:110
  120.6 15.3 %collective-permute-start.4 = (bf16[2,2,384,128]{3,2,1,0:T(8,128)(2,1)}, bf16[2,2,384,128]{3,2,1,0:T(8,128)(2,1)S(1)}, u32[]{:S(2)}, u32[]{:S(2)}) collective-permute-start(bf16[2,2,384,128]{3,2,1,0:T(8,128)(2,1)} %shard_map.65), channel_id=1, source_target_pairs={{0,6},{2,0},{4,2},{6,4},{1,7},{3,1},{5,3},{7,5},{8,14},{10,8},{12,... | collective-permute-start | bytes 1179656 | tf_op jit(solution)/shard_map/ppermute | solution.py:110
  123.7 19.2 %collective-permute-start.7 = (bf16[1024,512]{1,0:T(8,128)(2,1)S(1)}, bf16[1024,512]{1,0:T(8,128)(2,1)}, u32[]{:S(2)}, u32[]{:S(2)}) collective-permute-start(bf16[1024,512]{1,0:T(8,128)(2,1)S(1)} %copy-done.2), channel_id=1, source_target_pairs={{0,1},{1,0},{2,3},{3,2},{4,5},{5,4},{6,7},{7,6},{8,9},{9,8},{10,11... | collective-permute-start | bytes 3145736 | tf_op jit(solution)/shard_map/ppermute | solution.py:80
  138.2 15.0 %all-to-all-start.1 = ((bf16[4,384,256]{2,1,0:T(8,128)(2,1)}), bf16[4,384,256]{2,1,0:T(8,128)(2,1)S(1)}, u32[]{:S(2)}, u32[]{:S(2)}) async-start(bf16[4,384,256]{2,1,0:T(8,128)(2,1)} %broadcast_in_dim.34), calls=%async_computation.1 | async-start | bytes 1572864 | tf_op jit(solution)/shard_map/all_to_all | solution.py:26
  231.3 7.7 %collective-permute-start.8 = (f32[32,512]{1,0:T(8,128)S(1)}, f32[32,512]{1,0:T(8,128)S(1)}, u32[]{:S(2)}, u32[]{:S(2)}) collective-permute-start(f32[32,512]{1,0:T(8,128)S(1)} %slice.19), channel_id=1, source_target_pairs={{0,1},{1,0},{2,3},{3,2},{4,5},{5,4},{6,7},{7,6},{8,9},{9,8},{10,11... | collective-permute-start | bytes 196616 | tf_op jit(solution)/shard_map/ppermute | solution.py:149

commit v3 on v2

v3 whole, which is shorter than its diff:
```python
import jax
import jax.numpy as jnp
from jax import lax
from jax.experimental import pallas as pl
from jax.experimental.pallas import tpu as pltpu
from jax.sharding import Mesh, PartitionSpec as P


EXPERTS = 4
CAP = 24
NEAR = 4
CORES = 2
PART = CAP // CORES
SLOTS = EXPERTS * PART

EPSILON = 1e-05


def pack_kernel(place, tokens, ids, gates, packed, combine):
    f32, bf16 = jnp.float32, jnp.bfloat16
    width = packed.shape[1]
    rows = tokens.shape[0]
    floats = tokens[...].astype(f32)
    scale = lax.rsqrt(jnp.mean(floats * floats, axis=1, keepdims=True) + EPSILON)
    start = pl.multiple_of(place[0] * width, width)
    normed = (tokens[:, pl.ds(start, width)].astype(f32) * scale).astype(bf16)
    slot = lax.broadcasted_iota(jnp.int32, (SLOTS, rows), 0)
    expert = sum((slot >= PART * e).astype(jnp.int32) for e in range(1, EXPERTS))
    wanted = (slot - expert * PART + place[1] * PART).astype(f32)
    first = ids[0:1, :] == expert
    second = ids[1:2, :] == expert
    named = jnp.where(jnp.logical_or(first, second), 1.0, 0.0)
    before = jnp.where(
        lax.broadcasted_iota(jnp.int32, (rows, rows), 0)
        < lax.broadcasted_iota(jnp.int32, (rows, rows), 1),
        1.0,
        0.0,
    ).astype(bf16)
    position = jnp.dot(named.astype(bf16), before, preferred_element_type=f32)
    picker = jnp.where(position == wanted, named, 0.0)
    gate = jnp.where(first, gates[0:1, :], jnp.where(second, gates[1:2, :], 0.0))
    combine[...] = picker * gate
    packed[...] = jnp.dot(picker.astype(bf16), normed, preferred_element_type=f32).astype(bf16)


def pack(place, tokens, ids, gates, width):
    rows = tokens.shape[0]
    whole = pl.BlockSpec(memory_space=pltpu.VMEM)
    return pl.pallas_call(
        pack_kernel,
        in_specs=[pl.BlockSpec(memory_space=pltpu.SMEM), whole, whole, whole],
        out_specs=[whole, whole],
        out_shape=[
            jax.ShapeDtypeStruct((SLOTS, width), jnp.bfloat16),
            jax.ShapeDtypeStruct((SLOTS, rows), jnp.float32),
        ],
    )(place, tokens, ids.T, gates.T)


def product_kernel(place, rows, own, other, out):
    width = own.shape[-1]
    both = jnp.concatenate([own[0, 0], own[0, 1], other[0, 0], other[0, 1]], axis=1)
    product = jnp.dot(rows[...], both, preferred_element_type=jnp.float32).astype(out.dtype)
    for core in range(CORES):
        for kind in range(2):
            at = (core * 2 + kind) * width
            out[0, core, kind] = product[:, at : at + width]


def products(place, rows, own, other):
    n_rows, depth = rows.shape
    xs, kinds, width = own.shape[0], own.shape[1], own.shape[3]
    weight_spec = pl.BlockSpec((1, kinds, depth, width), lambda shift, place: (shift, 0, 0, 0))
    return pl.pallas_call(
        product_kernel,
        grid_spec=pltpu.PrefetchScalarGridSpec(
            num_scalar_prefetch=1,
            grid=(xs,),
            in_specs=[
                pl.BlockSpec((n_rows, depth), lambda shift, place: (0, 0)),
                weight_spec,
                weight_spec,
            ],
            out_specs=pl.BlockSpec(
                (1, CORES, kinds, n_rows, width),
                lambda shift, place: (lax.rem(place[0] + xs - shift, xs), 0, 0, 0, 0),
            ),
        ),
        out_shape=jax.ShapeDtypeStruct((xs, CORES, kinds, n_rows, width), jnp.bfloat16),
    )(place, rows, own, other)


def hidden_kernel(place, sums, out):
    f32 = jnp.float32
    total = jnp.sum(sums[...].astype(f32), axis=0)
    width = sums.shape[-1]
    gate, up = total[:, 0], total[:, 1]
    hidden = (gate / (1.0 + jnp.exp(-gate)) * up).astype(out.dtype)
    straight = place[1] == 0
    low = jnp.where(straight, hidden[0], hidden[1])
    high = jnp.where(straight, hidden[1], hidden[0])
    for copy in range(out.shape[0]):
        out[copy, :, 0:width] = low
        out[copy, :, width : 2 * width] = high


def hidden_units(place, sums):
    xs, cores, kinds, n_rows, width = sums.shape
    block = n_rows // 3
    return pl.pallas_call(
        hidden_kernel,
        grid_spec=pltpu.PrefetchScalarGridSpec(
            num_scalar_prefetch=1,
            grid=(n_rows // block,),
            in_specs=[
                pl.BlockSpec((xs, cores, kinds, block, width), lambda i, place: (0, 0, 0, i, 0))
            ],
            out_specs=pl.BlockSpec((xs, block, cores * width), lambda i, place: (0, i, 0)),
        ),
        out_shape=jax.ShapeDtypeStruct((xs, n_rows, cores * width), jnp.bfloat16),
    )(place, sums)


def layer(tokens, route_ids, route_gates, gate_weight, up_weight, down_weight):
    f32, bf16 = jnp.float32, jnp.bfloat16
    model_width = tokens.shape[1]
    far, near, xs = lax.axis_size("far"), lax.axis_size("near"), lax.axis_size("x")
    core, x = lax.axis_index("core"), lax.axis_index("x")
    chip_width = model_width // xs
    out_width = down_weight.shape[1]
    lanes = chip_width // 128
    copies = far // EXPERTS
    swap = [(i, (i + 1) % CORES) for i in range(CORES)]
    place = jnp.stack([x, core]).astype(jnp.int32)

    packed, combine = pack(place, tokens, route_ids, route_gates, chip_width)
    sent = jnp.broadcast_to(
        packed.reshape(EXPERTS, 1, PART, lanes, 128), (EXPERTS, copies, PART, lanes, 128)
    ).reshape(far, PART, lanes, 128)
    arrived = lax.all_to_all(sent, "far", 0, 0, tiled=True)

    def chunk(shift):
        start = (x + shift) % xs * chip_width
        return jnp.stack(
            [
                lax.dynamic_slice_in_dim(weight, start, chip_width, 0)
                for weight in (gate_weight, up_weight)
            ]
        )

    chunks = [chunk(0)]
    for shift in range(1, xs):
        chunks.append(lax.ppermute(chunk(shift), "x", [(i, (i + shift) % xs) for i in range(xs)]))
    own = jnp.stack(chunks)
    other = lax.ppermute(own, "core", swap)
    down_other = lax.ppermute(down_weight, "core", swap)

    arrived = arrived.reshape(1, far * PART, chip_width)
    rows = lax.all_to_all(
        jnp.broadcast_to(arrived, (near, far * PART, chip_width)), "near", 0, 0, tiled=True
    )
    n_rows = near * far * PART
    partial = products(place, rows.reshape(n_rows, chip_width), own, other)
    sums = lax.all_to_all(partial, "x", 0, 0, tiled=True)
    units = lax.all_to_all(hidden_units(place, sums), "x", 0, 0, tiled=True)

    def down(weight):
        return jnp.einsum(
            "xsu,xun->sn",
            units,
            weight.reshape(xs, units.shape[2], out_width),
            preferred_element_type=f32,
        ).astype(bf16)

    produced = jnp.concatenate([down(down_weight), down(down_other)], axis=1)
    parts = lax.all_to_all(
        produced.reshape(near, far * PART, 2 * out_width), "near", 0, 0, tiled=True
    )
    summed = jnp.sum(parts.astype(f32), axis=0).astype(bf16)
    out_lanes = 2 * out_width // 128
    returned = lax.all_to_all(
        summed.reshape(far, PART, out_lanes, 128), "far", 0, 0, tiled=True
    )
    returned = jnp.sum(
        returned.reshape(EXPERTS, copies, PART, out_lanes, 128).astype(f32), axis=1
    ).reshape(SLOTS, 2 * out_width)
    mixture = jnp.einsum(
        "st,sd->td",
        combine,
        returned,
        precision=lax.Precision.HIGHEST,
        preferred_element_type=f32,
    )
    mixture = mixture[:, :out_width] + lax.ppermute(mixture[:, out_width:], "core", swap)
    residual = lax.dynamic_slice_in_dim(
        tokens, (x * CORES + core) * out_width, out_width, 1
    ).astype(f32)
    return (residual + mixture).astype(bf16)


def solution(mesh):
    groups, experts, tensor = (mesh.shape[n] for n in ("groups", "expert", "tensor"))
    fine = Mesh(
        mesh.devices.reshape(groups, experts // NEAR, NEAR, tensor // CORES, CORES),
        ("groups", "far", "near", "x", "core"),
    )
    tok = ("groups", "far", "near")
    in_specs = (
        P(tok, None),
        P(tok, None),
        P(tok, None),
        P(None, ("far", "near", "x", "core")),
        P(None, ("far", "near", "x", "core")),
        P(("far", "near"), ("x", "core")),
    )
    out_specs = P(tok, ("x", "core"))
    return jax.shard_map(layer, mesh=fine, in_specs=in_specs, out_specs=out_specs, check_vma=False)
```

time: 241 us -> 250 us (1.037)
  starting transfers between devices: 81.1 us -> 38.6 us
  blocking collectives: 94.2 us -> 131 us
  waiting for transfers between devices: 39.1 us -> 57.3 us
  other arithmetic: 6.57 us -> 2.75 us
    all_to_all x2 -> x3, blocking collectives: 75.1 us -> 131 us  [the longest x1 71.6 us: layer(): arrived = lax.all_to_all(sent, 'far', 0, 0, tiled=True)]
    all_to_all x2 -> x3, starting transfers between devices: 48.6 us -> 17.3 us  [the longest x1 9.94 us: layer(): lax.all_to_all(jnp.broadcast_to(arrived, (near, far * PART, chip_width)),...]
    all_gather x1 -> x0, blocking collectives: 19 us -> none  [layer(): rows = lax.all_gather(arrived, 'near', axis=0, tiled=True)]
    all_to_all x2 -> x3, waiting for transfers between devices: 10.4 us -> 29.1 us  [the longest x1 18 us: layer(): sums = lax.all_to_all(partial, 'x', 0, 0, tiled=True)]
    ppermute x3 -> x0, starting transfers between devices: 8.6 us -> none  [layer(): lax.ppermute(products(rows, own, other, shift, bf16), 'x', [(i, (i - shif...]
    ppermute x3 -> x0, waiting for transfers between devices: 4.39 us -> none  [layer(): lax.ppermute(products(rows, own, other, shift, bf16), 'x', [(i, (i - shif...]
    ppermute x1, waiting for transfers between devices: 0.01 us -> 3.9 us  [layer(): other = lax.ppermute(own, 'core', swap)]
    ppermute x1, starting transfers between devices: 4.93 us -> 2.31 us  [layer(): down_other = lax.ppermute(down_weight, 'core', swap)]
  transfers between devices with their start and end apart: 11 -> 9, of which waited for: 6 -> 7; matrix products, arithmetic and copies ran while one was open for 2% -> 0% of each run, Pallas kernels for 3% -> 2%
where the time goes in v3:
time: 250 us; the launch traced here: 249 us
  blocking collectives  131 us (52%)
  waiting for transfers between devices  57.3 us (23%)
  starting transfers between devices  38.6 us (15%)
  Pallas kernels  12.1 us (5%)
  local copies, waits for them, and re-layouts  4.24 us (2%)
  other arithmetic  2.75 us (1%)
  matrix products  2.67 us (1%)
    all_to_all x1, blocking collectives, layer(): arrived = lax.all_to_all(sent, 'far', 0, 0, tiled=True)  71.6 us
    all_to_all x1, blocking collectives, layer(): lax.all_to_all(summed.reshape(far, PART, out_lanes, 128), 'far', 0, 0, ti...  36.2 us
    all_to_all x1, blocking collectives, layer(): lax.all_to_all(produced.reshape(near, far * PART, 2 * out_width), 'near',...  23.5 us
    ppermute x3, waiting for transfers between devices, layer(): lax.ppermute(chunk(shift), 'x', [(i, (i + shift) % xs) for i in range(xs)])  23.5 us
    all_to_all x1, waiting for transfers between devices, layer(): sums = lax.all_to_all(partial, 'x', 0, 0, tiled=True)  18 us
    all_to_all x1, waiting for transfers between devices, layer(): units = lax.all_to_all(hidden_units(place, sums), 'x', 0, 0, tiled=True)  11 us
    all_to_all x1, starting transfers between devices, layer(): lax.all_to_all(jnp.broadcast_to(arrived, (near, far * PART, chip_width)),...  9.94 us
    ppermute x3, starting transfers between devices, layer(): lax.ppermute(chunk(shift), 'x', [(i, (i + shift) % xs) for i in range(xs)])  9.69 us
  transfers between devices with their start and end apart: 9, of which 7 were waited for; matrix products, arithmetic and copies ran while one was open for 0% of the time, Pallas kernels for 2%

profile of v3, /device:TPU:33, one launch (start us, length us, event | category | flops | bytes accessed | tf_op | source)
XLA Modules:
  0.0 249.3 jit_solution(7041687266015178570)
XLA Ops:
  0.0 0.6 pad_add_fusion.place
  0.7 2.1 shard_map.64
  2.7 0.9 copy.7
  3.7 71.6 %all_to_all.30 = bf16[8,12,8,128]{3,2,1,0:T(8,128)(2,1)S(1)} all-to-all(bf16[8,12,8,128]{3,2,1,0:T(8,128)(2,1)S(1)} %bitcast.65), channel_id=1, replica_groups=mesh['groups'=2,'far'=8,'near'=4,'x'=4,'core'=2] {'far'}, dimensions={0} | all-to-all | bytes 393216 | tf_op jit(solution)/shard_map/all_to_all | solution.py:140
  75.3 1.0 broadcast_in_dim.17
  76.3 9.9 %all-to-all-start.1 = ((bf16[4,96,1024]{2,1,0:T(8,128)(2,1)}), bf16[4,96,1024]{2,1,0:T(8,128)(2,1)S(1)}, u32[]{:S(2)}, u32[]{:S(2)}) async-start(bf16[4,96,1024]{2,1,0:T(8,128)(2,1)} %broadcast_in_dim.17), calls=%async_computation.1 | async-start | bytes 1572864 | tf_op jit(solution)/shard_map/all_to_all | solution.py:159
  86.3 0.0 copy-done.3
  86.3 0.0 copy-done.4
  86.3 0.2 dynamic-slice_bitcast_fusion.6
  86.5 0.1 pad_maximum_fusion.4
  86.5 4.8 %collective-permute-start.2 = (bf16[2,1024,128]{2,1,0:T(8,128)(2,1)S(1)}, bf16[2,1024,128]{2,1,0:T(8,128)(2,1)S(1)}, u32[]{:S(2)}, u32[]{:S(2)}) collective-permute-start(bf16[2,1024,128]{2,1,0:T(8,128)(2,1)S(1)} %pad_maximum_fusion.4), channel_id=1, source_target_pairs={{0,6},{2,0},{4,2},{6,4},{1,7},{3,1},{5,3},{7,5},{8,14},{10,8},{12,... | collective-permute-start | bytes 1572872 | tf_op jit(solution)/shard_map/ppermute | solution.py:153
  91.3 0.1 pad_maximum_fusion.3
  91.4 2.2 collective-permute-start.1
  93.6 0.1 pad_maximum_fusion.2
  93.7 2.7 %collective-permute-start = (bf16[2,1024,128]{2,1,0:T(8,128)(2,1)S(1)}, bf16[2,1024,128]{2,1,0:T(8,128)(2,1)S(1)}, u32[]{:S(2)}, u32[]{:S(2)}) collective-permute-start(bf16[2,1024,128]{2,1,0:T(8,128)(2,1)S(1)} %pad_maximum_fusion.2), channel_id=1, source_target_pairs={{0,2},{2,4},{4,6},{6,0},{1,3},{3,5},{5,7},{7,1},{8,10},{10,12},{12... | collective-permute-start | bytes 1572872 | tf_op jit(solution)/shard_map/ppermute | solution.py:153
  96.3 0.1 maximum_bitcast_fusion
  96.4 4.3 %collective-permute-done.2 = bf16[2,1024,128]{2,1,0:T(8,128)(2,1)S(1)} collective-permute-done((bf16[2,1024,128]{2,1,0:T(8,128)(2,1)S(1)}, bf16[2,1024,128]{2,1,0:T(8,128)(2,1)S(1)}, u32[]{:S(2)}, u32[]{:S(2)}) %collective-permute-start.2) | collective-permute-done | bytes 524320 | tf_op jit(solution)/shard_map/ppermute | solution.py:153
  100.7 4.7 %collective-permute-done.1 = bf16[2,1024,128]{2,1,0:T(8,128)(2,1)S(1)} collective-permute-done((bf16[2,1024,128]{2,1,0:T(8,128)(2,1)S(1)}, bf16[2,1024,128]{2,1,0:T(8,128)(2,1)S(1)}, u32[]{:S(2)}, u32[]{:S(2)}) %collective-permute-start.1) | collective-permute-done | bytes 524320 | tf_op jit(solution)/shard_map/ppermute | solution.py:153
  105.4 14.5 %collective-permute-done = bf16[2,1024,128]{2,1,0:T(8,128)(2,1)S(1)} collective-permute-done((bf16[2,1024,128]{2,1,0:T(8,128)(2,1)S(1)}, bf16[2,1024,128]{2,1,0:T(8,128)(2,1)S(1)}, u32[]{:S(2)}, u32[]{:S(2)}) %collective-permute-start) | collective-permute-done | bytes 524320 | tf_op jit(solution)/shard_map/ppermute | solution.py:153
  119.9 0.3 pad_maximum_fusion.own
  120.2 0.0 copy-start
  120.2 2.4 collective-permute-start.3
  122.6 3.9 %collective-permute-done.3.other = bf16[4,2,1024,128]{3,2,1,0:T(8,128)(2,1)} collective-permute-done((bf16[4,2,1024,128]{3,2,1,0:T(8,128)(2,1)S(1)}, bf16[4,2,1024,128]{3,2,1,0:T(8,128)(2,1)}, u32[]{:S(2)}, u32[]{:S(2)}) %collective-permute-start.3) | collective-permute-done | bytes 2097184 | tf_op jit(solution)/shard_map/ppermute | solution.py:155
  126.5 0.0 all-to-all-done.1
  126.5 0.0 copy-done
  126.5 0.9 copy-done.2
  127.4 6.1 %shard_map.65 = bf16[4,2,2,384,128]{4,3,2,1,0:T(8,128)(2,1)} custom-call(s32[2]{0:T(128)} %pad_add_fusion.place, bf16[384,1024]{1,0:T(8,128)(2,1)} %bitcast.63, bf16[4,2,1024,128]{3,2,1,0:T(8,128)(2,1)} %copy-done, bf16[4,2,1024,128]{3,2,1,0:T(8,128)(2,1)} %collective-permute-done.3.other), custom_call_target="tpu_custom_call" | custom-call | tf_op jit(solution)/shard_map/pallas_call | solution.py:74
  133.5 3.8 %all-to-all-start.2 = ((bf16[4,2,2,384,128]{4,3,2,1,0:T(8,128)(2,1)}), bf16[4,2,2,384,128]{4,3,2,1,0:T(8,128)(2,1)S(1)}, u32[]{:S(2)}, u32[]{:S(2)}) async-start(bf16[4,2,2,384,128]{4,3,2,1,0:T(8,128)(2,1)} %shard_map.65), calls=%async_computation.2 | async-start | bytes 3145728 | tf_op jit(solution)/shard_map/all_to_all | solution.py:164
  137.3 0.0 copy-done.6
  137.3 2.3 collective-permute-start.4
  139.7 18.0 %all-to-all-done.2.sums = bf16[4,2,2,384,128]{4,3,2,1,0:T(8,128)(2,1)S(1)} async-done(((bf16[4,2,2,384,128]{4,3,2,1,0:T(8,128)(2,1)}), bf16[4,2,2,384,128]{4,3,2,1,0:T(8,128)(2,1)S(1)}, u32[]{:S(2)}, u32[]{:S(2)}) %all-to-all-start.2) | async-done | bytes 1572896 | tf_op jit(solution)/shard_map/all_to_all | solution.py:164
  157.7 1.2 copy-done.1
  158.8 3.9 %shard_map.66 = bf16[4,384,256]{2,1,0:T(8,128)(2,1)} custom-call(s32[2]{0:T(128)} %pad_add_fusion.place, bf16[4,2,2,384,128]{4,3,2,1,0:T(8,128)(2,1)} %copy-done.1), custom_call_target="tpu_custom_call" | custom-call | tf_op jit(solution)/shard_map/pallas_call | solution.py:110
  162.7 3.6 %all-to-all-start.3 = ((bf16[4,384,256]{2,1,0:T(8,128)(2,1)}), bf16[4,384,256]{2,1,0:T(8,128)(2,1)S(1)}, u32[]{:S(2)}, u32[]{:S(2)}) async-start(bf16[4,384,256]{2,1,0:T(8,128)(2,1)} %shard_map.66), calls=%async_computation.3 | async-start | bytes 1572864 | tf_op jit(solution)/shard_map/all_to_all | solution.py:165
  166.3 0.0 collective-permute-done.4
  166.3 11.0 %all-to-all-done.3 = bf16[4,384,256]{2,1,0:T(8,128)(2,1)S(1)} async-done(((bf16[4,384,256]{2,1,0:T(8,128)(2,1)}), bf16[4,384,256]{2,1,0:T(8,128)(2,1)S(1)}, u32[]{:S(2)}, u32[]{:S(2)}) %all-to-all-start.3) | async-done | bytes 786464 | tf_op jit(solution)/shard_map/all_to_all | solution.py:165
  177.4 1.8 fusion.1
  179.2 0.6 fusion
  179.7 0.1 pad_maximum_fusion.1
  179.8 0.0 copy-start.5
  179.9 23.5 %all_to_all.31 = bf16[4,96,1024]{2,1,0:T(8,128)(2,1)S(1)} all-to-all(bf16[4,96,1024]{2,1,0:T(8,128)(2,1)S(1)} %bitcast.62), channel_id=1, replica_groups=mesh['groups'=2,'far'=8,'near'=4,'x'=4,'core'=2] {'near'}, dimensions={0} | all-to-all | bytes 1572864 | tf_op jit(solution)/shard_map/all_to_all | solution.py:176
  203.4 0.1 reduce_sum.21
  203.6 36.2 %all_to_all.32 = bf16[8,12,8,128]{3,2,1,0:T(8,128)(2,1)S(1)} all-to-all(bf16[8,12,8,128]{3,2,1,0:T(8,128)(2,1)S(1)} %bitcast.67), channel_id=1, replica_groups=mesh['groups'=2,'far'=8,'near'=4,'x'=4,'core'=2] {'far'}, dimensions={0} | all-to-all | bytes 393216 | tf_op jit(solution)/shard_map/all_to_all | solution.py:181
  239.8 0.0 copy-done.5
  239.9 0.3 fusion.2
  240.2 6.8 %collective-permute-start.5 = (f32[32,512]{1,0:T(8,128)S(1)}, f32[32,512]{1,0:T(8,128)S(1)}, u32[]{:S(2)}, u32[]{:S(2)}) collective-permute-start(f32[32,512]{1,0:T(8,128)S(1)} %slice.9), channel_id=1, source_target_pairs={{0,1},{1,0},{2,3},{3,2},{4,5},{5,4},{6,7},{7,6},{8,9},{9,8},{10,11... | collective-permute-start | bytes 196616 | tf_op jit(solution)/shard_map/ppermute | solution.py:194
  247.1 0.9 collective-permute-done.5
  247.9 1.4 fusion.6
  (10 shorter events, 0.1 us)
Async XLA Ops:
  0.6 85.6 %copy-start.3 = (bf16[4096,128]{1,0:T(8,128)(2,1)S(1)}, bf16[4096,128]{1,0:T(8,128)(2,1)}, u32[]{:S(2)}) copy-start(bf16[4096,128]{1,0:T(8,128)(2,1)} %param.10) | copy-start | bytes 3145732
  0.6 85.6 %copy-start.4 = (bf16[4096,128]{1,0:T(8,128)(2,1)S(1)}, bf16[4096,128]{1,0:T(8,128)(2,1)}, u32[]{:S(2)}) copy-start(bf16[4096,128]{1,0:T(8,128)(2,1)} %param.9) | copy-start | bytes 3145732
  76.3 50.2 %all-to-all-start.1 = ((bf16[4,96,1024]{2,1,0:T(8,128)(2,1)}), bf16[4,96,1024]{2,1,0:T(8,128)(2,1)S(1)}, u32[]{:S(2)}, u32[]{:S(2)}) async-start(bf16[4,96,1024]{2,1,0:T(8,128)(2,1)} %broadcast_in_dim.17), calls=%async_computation.1 | async-start | bytes 1572864 | tf_op jit(solution)/shard_map/all_to_all | solution.py:159
  86.5 14.2 %collective-permute-start.2 = (bf16[2,1024,128]{2,1,0:T(8,128)(2,1)S(1)}, bf16[2,1024,128]{2,1,0:T(8,128)(2,1)S(1)}, u32[]{:S(2)}, u32[]{:S(2)}) collective-permute-start(bf16[2,1024,128]{2,1,0:T(8,128)(2,1)S(1)} %pad_maximum_fusion.4), channel_id=1, source_target_pairs={{0,6},{2,0},{4,2},{6,4},{1,7},{3,1},{5,3},{7,5},{8,14},{10,8},{12,... | collective-permute-start | bytes 1572872 | tf_op jit(solution)/shard_map/ppermute | solution.py:153
  91.4 14.0 %collective-permute-start.1 = (bf16[2,1024,128]{2,1,0:T(8,128)(2,1)S(1)}, bf16[2,1024,128]{2,1,0:T(8,128)(2,1)S(1)}, u32[]{:S(2)}, u32[]{:S(2)}) collective-permute-start(bf16[2,1024,128]{2,1,0:T(8,128)(2,1)S(1)} %pad_maximum_fusion.3), channel_id=1, source_target_pairs={{0,4},{2,6},{4,0},{6,2},{1,5},{3,7},{5,1},{7,3},{8,12},{10,14},{12... | collective-permute-start | bytes 1572872 | tf_op jit(solution)/shard_map/ppermute | solution.py:153
  93.7 26.3 %collective-permute-start = (bf16[2,1024,128]{2,1,0:T(8,128)(2,1)S(1)}, bf16[2,1024,128]{2,1,0:T(8,128)(2,1)S(1)}, u32[]{:S(2)}, u32[]{:S(2)}) collective-permute-start(bf16[2,1024,128]{2,1,0:T(8,128)(2,1)S(1)} %pad_maximum_fusion.2), channel_id=1, source_target_pairs={{0,2},{2,4},{4,6},{6,0},{1,3},{3,5},{5,7},{7,1},{8,10},{10,12},{12... | collective-permute-start | bytes 1572872 | tf_op jit(solution)/shard_map/ppermute | solution.py:153
  120.2 6.4 %copy-start = (bf16[4,2,1024,128]{3,2,1,0:T(8,128)(2,1)}, bf16[4,2,1024,128]{3,2,1,0:T(8,128)(2,1)S(1)}, u32[]{:S(2)}) copy-start(bf16[4,2,1024,128]{3,2,1,0:T(8,128)(2,1)S(1)} %pad_maximum_fusion.own) | copy-start | bytes 6291460
  120.2 6.3 %collective-permute-start.3 = (bf16[4,2,1024,128]{3,2,1,0:T(8,128)(2,1)S(1)}, bf16[4,2,1024,128]{3,2,1,0:T(8,128)(2,1)}, u32[]{:S(2)}, u32[]{:S(2)}) collective-permute-start(bf16[4,2,1024,128]{3,2,1,0:T(8,128)(2,1)S(1)} %pad_maximum_fusion.own), channel_id=1, source_target_pairs={{0,1},{1,0},{2,3},{3,2},{4,5},{5,4},{6,7},{7,6},{8,9},{9,8},{10,11... | collective-permute-start | bytes 6291464 | tf_op jit(solution)/shard_map/ppermute | solution.py:155
  126.5 0.9 copy-start.2
  133.5 3.8 %copy-start.6 = (bf16[1024,512]{1,0:T(8,128)(2,1)S(1)}, bf16[1024,512]{1,0:T(8,128)(2,1)}, u32[]{:S(2)}) copy-start(bf16[1024,512]{1,0:T(8,128)(2,1)} %param.11) | copy-start | bytes 3145732
  133.5 24.1 %all-to-all-start.2 = ((bf16[4,2,2,384,128]{4,3,2,1,0:T(8,128)(2,1)}), bf16[4,2,2,384,128]{4,3,2,1,0:T(8,128)(2,1)S(1)}, u32[]{:S(2)}, u32[]{:S(2)}) async-start(bf16[4,2,2,384,128]{4,3,2,1,0:T(8,128)(2,1)} %shard_map.65), calls=%async_computation.2 | async-start | bytes 3145728 | tf_op jit(solution)/shard_map/all_to_all | solution.py:164
  137.3 29.0 %collective-permute-start.4 = (bf16[1024,512]{1,0:T(8,128)(2,1)S(1)}, bf16[1024,512]{1,0:T(8,128)(2,1)}, u32[]{:S(2)}, u32[]{:S(2)}) collective-permute-start(bf16[1024,512]{1,0:T(8,128)(2,1)S(1)} %copy-done.6), channel_id=1, source_target_pairs={{0,1},{1,0},{2,3},{3,2},{4,5},{5,4},{6,7},{7,6},{8,9},{9,8},{10,11... | collective-permute-start | bytes 3145736 | tf_op jit(solution)/shard_map/ppermute | solution.py:156
  157.7 1.2 copy-start.1
  162.7 14.7 %all-to-all-start.3 = ((bf16[4,384,256]{2,1,0:T(8,128)(2,1)}), bf16[4,384,256]{2,1,0:T(8,128)(2,1)S(1)}, u32[]{:S(2)}, u32[]{:S(2)}) async-start(bf16[4,384,256]{2,1,0:T(8,128)(2,1)} %shard_map.66), calls=%async_computation.3 | async-start | bytes 1572864 | tf_op jit(solution)/shard_map/all_to_all | solution.py:165
  179.8 60.0 %copy-start.5 = (f32[48,32]{1,0:T(8,128)S(1)}, f32[48,32]{1,0:T(8,128)}, u32[]{:S(2)}) copy-start(f32[48,32]{1,0:T(8,128)} %get-tuple-element.7) | copy-start | bytes 18436
  240.2 7.7 %collective-permute-start.5 = (f32[32,512]{1,0:T(8,128)S(1)}, f32[32,512]{1,0:T(8,128)S(1)}, u32[]{:S(2)}, u32[]{:S(2)}) collective-permute-start(f32[32,512]{1,0:T(8,128)S(1)} %slice.9), channel_id=1, source_target_pairs={{0,1},{1,0},{2,3},{3,2},{4,5},{5,4},{6,7},{7,6},{8,9},{9,8},{10,11... | collective-permute-start | bytes 196616 | tf_op jit(solution)/shard_map/ppermute | solution.py:194

commit v4 on v3

v4 whole, which is shorter than its diff:
```python
import jax
import jax.numpy as jnp
from jax import lax
from jax.experimental import pallas as pl
from jax.experimental.pallas import tpu as pltpu
from jax.sharding import Mesh, PartitionSpec as P


EXPERTS = 4
CAP = 24
NEAR = 4
CORES = 2
PART = CAP // CORES
SLOTS = EXPERTS * PART

EPSILON = 1e-05


def whole(space=None):
    return pl.BlockSpec(memory_space=space or pltpu.VMEM)


PARAMS = pltpu.CompilerParams(vmem_limit_bytes=16 << 20)


def near_memory(*arrays):
    return [pltpu.with_memory_space_constraint(array, pltpu.VMEM) for array in arrays]


def pack_kernel(tokens, ids, gates, packed, combine, residual):
    f32, bf16 = jnp.float32, jnp.bfloat16
    half = packed.shape[2]
    rows = tokens.shape[0]
    x, core = lax.axis_index("x"), lax.axis_index("core")
    out_width = residual.shape[1]
    floats = tokens[...].astype(f32)
    scale = lax.rsqrt(jnp.mean(floats * floats, axis=1, keepdims=True) + EPSILON)
    slot = lax.broadcasted_iota(jnp.int32, (SLOTS, rows), 0)
    expert = sum((slot >= PART * e).astype(jnp.int32) for e in range(1, EXPERTS))
    wanted = (slot - expert * PART + core * PART).astype(f32)
    first = ids[0:1, :] == expert
    second = ids[1:2, :] == expert
    before = jnp.where(
        lax.broadcasted_iota(jnp.int32, (rows, rows), 0)
        < lax.broadcasted_iota(jnp.int32, (rows, rows), 1),
        1.0,
        0.0,
    ).astype(bf16)

    def picked(named, wanted):
        position = jnp.dot(named.astype(bf16), before, preferred_element_type=f32)
        return jnp.where(position == wanted, named, 0.0)

    gate = jnp.where(first, gates[0:1, :], jnp.where(second, gates[1:2, :], 0.0))
    named = jnp.where(jnp.logical_or(first, second), 1.0, 0.0)
    combine[...] = picked(named, wanted) * gate
    line = lax.broadcasted_iota(jnp.int32, (2 * SLOTS, rows), 0)
    expert = sum((line >= 2 * PART * e).astype(jnp.int32) for e in range(1, EXPERTS))
    at = line - expert * (2 * PART)
    upper = (at >= PART).astype(jnp.int32)
    wanted = (at - upper * PART + core * PART).astype(f32)
    named = jnp.where(jnp.logical_or(ids[0:1, :] == expert, ids[1:2, :] == expert), 1.0, 0.0)
    picker = picked(named, wanted)
    total = jnp.zeros((2 * SLOTS, half), f32)
    for part in range(2):
        start = pl.multiple_of((x * 2 + part) * half, half)
        normed = (tokens[:, pl.ds(start, half)].astype(f32) * scale).astype(bf16)
        mine = jnp.where(upper == part, picker, 0.0).astype(bf16)
        total = total + jnp.dot(mine, normed, preferred_element_type=f32)
    total = total.astype(bf16)
    copies = packed.shape[0] // EXPERTS
    for e in range(EXPERTS):
        for copy in range(copies):
            packed[e * copies + copy] = total[e * 2 * PART : (e + 1) * 2 * PART]
    start = pl.multiple_of((x * CORES + core) * out_width, out_width)
    residual[...] = tokens[:, pl.ds(start, out_width)]


def pack(tokens, ids, gates, far, chip_width, out_width):
    rows = tokens.shape[0]
    return pl.pallas_call(
        pack_kernel,
        compiler_params=PARAMS,
        in_specs=[whole()] * 3,
        out_specs=[whole()] * 3,
        out_shape=[
            pltpu.VMEM((far, 2 * PART, chip_width // 2), jnp.bfloat16),
            pltpu.VMEM((SLOTS, rows), jnp.float32),
            pltpu.VMEM((rows, out_width), jnp.bfloat16),
        ],
    )(tokens, ids.T, gates.T)


def product_kernel(rows, own, other, out):
    xs, kinds, _, width = own.shape
    x = lax.axis_index("x")
    left = rows[...]
    for shift in range(xs):
        to = lax.rem(x + (xs - shift), xs)
        for core, weights in enumerate((own, other)):
            both = jnp.concatenate([weights[shift, kind] for kind in range(kinds)], axis=1)
            product = jnp.dot(left, both, preferred_element_type=jnp.float32).astype(out.dtype)
            for kind in range(kinds):
                out[to, core, kind] = product[:, kind * width : (kind + 1) * width]


def products(rows, own, other):
    n_rows = rows.shape[0]
    xs, kinds, _, width = own.shape
    return pl.pallas_call(
        product_kernel,
        compiler_params=PARAMS,
        in_specs=[whole()] * 3,
        out_specs=whole(),
        out_shape=pltpu.VMEM((xs, CORES, kinds, n_rows, width), jnp.bfloat16),
    )(*near_memory(rows, own, other))


def hidden_kernel(sums, out):
    f32 = jnp.float32
    xs, _, _, n_rows, width = sums.shape
    straight = lax.axis_index("core") == 0
    block = 32
    for at in range(0, n_rows, block):
        total = sums[0, :, :, at : at + block, :].astype(f32)
        for source in range(1, xs):
            total = total + sums[source, :, :, at : at + block, :].astype(f32)
        gate, up = total[:, 0], total[:, 1]
        hidden = (gate / (1.0 + jnp.exp(-gate)) * up).astype(out.dtype)
        low = jnp.where(straight, hidden[0], hidden[1])
        high = jnp.where(straight, hidden[1], hidden[0])
        for copy in range(out.shape[0]):
            out[copy, at : at + block, 0:width] = low
            out[copy, at : at + block, width : 2 * width] = high


def hidden_units(sums):
    xs, cores, _, n_rows, width = sums.shape
    return pl.pallas_call(
        hidden_kernel,
        compiler_params=PARAMS,
        in_specs=[whole()],
        out_specs=whole(),
        out_shape=pltpu.VMEM((xs, n_rows, cores * width), jnp.bfloat16),
    )(*near_memory(sums))


def down_kernel(units, own, other, out):
    xs, _, _ = units.shape
    near, block, _ = out.shape
    width = own.shape[1]
    left = jnp.concatenate([units[source] for source in range(xs)], axis=1)
    for core, weight in enumerate((own, other)):
        product = jnp.dot(left, weight[...], preferred_element_type=jnp.float32).astype(out.dtype)
        for line in range(near):
            out[line, :, core * width : (core + 1) * width] = product[
                line * block : (line + 1) * block
            ]


def down(units, own, other, near):
    n_rows = units.shape[1]
    return pl.pallas_call(
        down_kernel,
        compiler_params=PARAMS,
        in_specs=[whole()] * 3,
        out_specs=whole(),
        out_shape=pltpu.VMEM((near, n_rows // near, CORES * own.shape[1]), jnp.bfloat16),
    )(*near_memory(units, own, other))


def layer(tokens, route_ids, route_gates, gate_weight, up_weight, down_weight):
    f32, bf16 = jnp.float32, jnp.bfloat16
    model_width = tokens.shape[1]
    far, near, xs = lax.axis_size("far"), lax.axis_size("near"), lax.axis_size("x")
    x = lax.axis_index("x")
    chip_width = model_width // xs
    out_width = down_weight.shape[1]
    copies = far // EXPERTS
    swap = [(i, (i + 1) % CORES) for i in range(CORES)]
    sent, combine, residual = pack(tokens, route_ids, route_gates, far, chip_width, out_width)
    arrived = lax.all_to_all(sent, "far", 0, 0, tiled=True)

    def chunk(shift):
        start = (x + shift) % xs * chip_width
        return jnp.stack(
            [
                lax.dynamic_slice_in_dim(weight, start, chip_width, 0)
                for weight in (gate_weight, up_weight)
            ]
        )

    chunks = [chunk(0)]
    for shift in range(1, xs):
        chunks.append(lax.ppermute(chunk(shift), "x", [(i, (i + shift) % xs) for i in range(xs)]))
    own = jnp.stack(chunks)
    other = lax.ppermute(own, "core", swap)
    down_other = lax.ppermute(down_weight, "core", swap)

    arrived = arrived.reshape(far, 2, PART, chip_width // 2)
    arrived = jnp.swapaxes(arrived, 1, 2).reshape(1, far * PART, chip_width)
    rows = lax.all_to_all(
        jnp.broadcast_to(arrived, (near, far * PART, chip_width)), "near", 0, 0, tiled=True
    )
    n_rows = near * far * PART
    partial = products(rows.reshape(n_rows, chip_width), own, other)
    sums = lax.all_to_all(partial, "x", 0, 0, tiled=True)
    units = lax.all_to_all(hidden_units(sums), "x", 0, 0, tiled=True)
    produced = down(units, down_weight, down_other, near)
    parts = lax.all_to_all(produced, "near", 0, 0, tiled=True)
    summed = jnp.sum(parts.astype(f32), axis=0).astype(bf16)
    out_lanes = 2 * out_width // 128
    returned = lax.all_to_all(
        summed.reshape(far, PART, out_lanes, 128), "far", 0, 0, tiled=True
    )
    returned = jnp.sum(
        returned.reshape(EXPERTS, copies, PART, out_lanes, 128).astype(f32), axis=1
    ).reshape(SLOTS, 2 * out_width)
    mixture = jnp.einsum(
        "st,sd->td",
        combine,
        returned,
        precision=lax.Precision.HIGHEST,
        preferred_element_type=f32,
    )
    mixture = mixture[:, :out_width] + lax.ppermute(mixture[:, out_width:], "core", swap)
    return (residual.astype(f32) + mixture).astype(bf16)


def solution(mesh):
    groups, experts, tensor = (mesh.shape[n] for n in ("groups", "expert", "tensor"))
    fine = Mesh(
        mesh.devices.reshape(groups, experts // NEAR, NEAR, tensor // CORES, CORES),
        ("groups", "far", "near", "x", "core"),
    )
    tok = ("groups", "far", "near")
    in_specs = (
        P(tok, None),
        P(tok, None),
        P(tok, None),
        P(None, ("far", "near", "x", "core")),
        P(None, ("far", "near", "x", "core")),
        P(("far", "near"), ("x", "core")),
    )
    out_specs = P(tok, ("x", "core"))
    return jax.shard_map(layer, mesh=fine, in_specs=in_specs, out_specs=out_specs, check_vma=False)
```

time: 250 us -> 241 us (0.964)
  Pallas kernels: 12.1 us -> 5.51 us
  waiting for transfers between devices: 57.3 us -> 51.9 us
  local copies, waits for them, and re-layouts: 4.24 us -> 7.89 us
  starting transfers between devices: 38.6 us -> 41.5 us
    pallas_call x3 -> x4, Pallas kernels: 12.1 us -> 5.51 us  [the longest x1 2.19 us: down(): pl.pallas_call(down_kernel, compiler_params=PARAMS, in_specs=[whole()] *...]
    ppermute x3, waiting for transfers between devices: 23.5 us -> 18.9 us  [layer(): lax.ppermute(chunk(shift), 'x', [(i, (i + shift) % xs) for i in range(xs)])]
    unnamed x17 -> x20, local copies, waits for them, and re-layouts: 3.05 us -> 6.47 us
  transfers between devices with their start and end apart: 9 -> 9, of which waited for: 7 -> 7; matrix products, arithmetic and copies ran while one was open for 0% -> 0% of each run, Pallas kernels for 2% -> 1%
where the time goes in v4:
time: 241 us; the launch traced here: 240 us
  blocking collectives  131 us (54%)
  waiting for transfers between devices  51.9 us (22%)
  starting transfers between devices  41.5 us (17%)
  local copies, waits for them, and re-layouts  7.89 us (3%)
  Pallas kernels  5.51 us (2%)
    all_to_all x1, blocking collectives, layer(): arrived = lax.all_to_all(sent, 'far', 0, 0, tiled=True)  71.8 us
    all_to_all x1, blocking collectives, layer(): lax.all_to_all(summed.reshape(far, PART, out_lanes, 128), 'far', 0, 0, ti...  36.3 us
    all_to_all x1, blocking collectives, layer(): parts = lax.all_to_all(produced, 'near', 0, 0, tiled=True)  23.4 us
    ppermute x3, waiting for transfers between devices, layer(): lax.ppermute(chunk(shift), 'x', [(i, (i + shift) % xs) for i in range(xs)])  18.9 us
    all_to_all x1, waiting for transfers between devices, layer(): sums = lax.all_to_all(partial, 'x', 0, 0, tiled=True)  17.6 us
    ppermute x3, starting transfers between devices, layer(): lax.ppermute(chunk(shift), 'x', [(i, (i + shift) % xs) for i in range(xs)])  10.9 us
    all_to_all x1, waiting for transfers between devices, layer(): units = lax.all_to_all(hidden_units(sums), 'x', 0, 0, tiled=True)  10.8 us
    all_to_all x1, starting transfers between devices, layer(): lax.all_to_all(jnp.broadcast_to(arrived, (near, far * PART, chip_width)),...  9.92 us
  transfers between devices with their start and end apart: 9, of which 7 were waited for; matrix products, arithmetic and copies ran while one was open for 0% of the time, Pallas kernels for 1%

profile of v4, /device:TPU:33, one launch (start us, length us, event | category | flops | bytes accessed | tf_op | source)
XLA Modules:
  0.0 240.1 jit_solution(3374124043971969093)
XLA Ops:
  0.0 0.9 copy-done.4
  1.0 0.7 copy-done.5
  1.6 0.7 copy-done.6
  2.3 0.3 shard_map.64
  2.6 0.0 copy-start.7
  2.7 0.0 copy-start.8
  2.7 71.8 %all_to_all.30 = bf16[8,24,512]{2,1,0:T(8,128)(2,1)S(1)} all-to-all(bf16[8,24,512]{2,1,0:T(8,128)(2,1)S(1)} %get-tuple-element.10), channel_id=1, replica_groups=mesh['groups'=2,'far'=8,'near'=4,'x'=4,'core'=2] {'far'}, dimensions={0} | all-to-all | bytes 393216 | tf_op jit(solution)/shard_map/all_to_all | solution.py:182
  74.5 0.1 copy.9
  74.5 0.2 copy.10
  74.8 1.0 broadcast_in_dim.8
  75.7 9.9 %all-to-all-start.1 = ((bf16[4,96,1024]{2,1,0:T(8,128)(2,1)}), bf16[4,96,1024]{2,1,0:T(8,128)(2,1)S(1)}, u32[]{:S(2)}, u32[]{:S(2)}) async-start(bf16[4,96,1024]{2,1,0:T(8,128)(2,1)} %broadcast_in_dim.8), calls=%async_computation.1 | async-start | bytes 1572864 | tf_op jit(solution)/shard_map/all_to_all | solution.py:202
  85.7 0.0 copy-done.7
  85.7 0.0 copy-done.8
  85.7 0.2 dynamic-slice_bitcast_fusion.6
  85.8 0.1 pad_maximum_fusion.1
  85.9 3.3 %collective-permute-start = (bf16[2,1024,128]{2,1,0:T(8,128)(2,1)S(1)}, bf16[2,1024,128]{2,1,0:T(8,128)(2,1)S(1)}, u32[]{:S(2)}, u32[]{:S(2)}) collective-permute-start(bf16[2,1024,128]{2,1,0:T(8,128)(2,1)S(1)} %pad_maximum_fusion.1), channel_id=1, source_target_pairs={{0,2},{2,4},{4,6},{6,0},{1,3},{3,5},{5,7},{7,1},{8,10},{10,12},{12... | collective-permute-start | bytes 1572872 | tf_op jit(solution)/shard_map/ppermute | solution.py:195
  89.2 0.1 pad_maximum_fusion.2
  89.3 4.7 %collective-permute-start.1 = (bf16[2,1024,128]{2,1,0:T(8,128)(2,1)S(1)}, bf16[2,1024,128]{2,1,0:T(8,128)(2,1)S(1)}, u32[]{:S(2)}, u32[]{:S(2)}) collective-permute-start(bf16[2,1024,128]{2,1,0:T(8,128)(2,1)S(1)} %pad_maximum_fusion.2), channel_id=1, source_target_pairs={{0,4},{2,6},{4,0},{6,2},{1,5},{3,7},{5,1},{7,3},{8,12},{10,14},{12... | collective-permute-start | bytes 1572872 | tf_op jit(solution)/shard_map/ppermute | solution.py:195
  93.9 0.1 pad_maximum_fusion.3
  94.0 3.0 %collective-permute-start.2 = (bf16[2,1024,128]{2,1,0:T(8,128)(2,1)S(1)}, bf16[2,1024,128]{2,1,0:T(8,128)(2,1)S(1)}, u32[]{:S(2)}, u32[]{:S(2)}) collective-permute-start(bf16[2,1024,128]{2,1,0:T(8,128)(2,1)S(1)} %pad_maximum_fusion.3), channel_id=1, source_target_pairs={{0,6},{2,0},{4,2},{6,4},{1,7},{3,1},{5,3},{7,5},{8,14},{10,8},{12,... | collective-permute-start | bytes 1572872 | tf_op jit(solution)/shard_map/ppermute | solution.py:195
  96.9 0.1 maximum_bitcast_fusion
  97.0 4.8 %collective-permute-done = bf16[2,1024,128]{2,1,0:T(8,128)(2,1)S(1)} collective-permute-done((bf16[2,1024,128]{2,1,0:T(8,128)(2,1)S(1)}, bf16[2,1024,128]{2,1,0:T(8,128)(2,1)S(1)}, u32[]{:S(2)}, u32[]{:S(2)}) %collective-permute-start) | collective-permute-done | bytes 524320 | tf_op jit(solution)/shard_map/ppermute | solution.py:195
  101.8 12.2 %collective-permute-done.1 = bf16[2,1024,128]{2,1,0:T(8,128)(2,1)S(1)} collective-permute-done((bf16[2,1024,128]{2,1,0:T(8,128)(2,1)S(1)}, bf16[2,1024,128]{2,1,0:T(8,128)(2,1)S(1)}, u32[]{:S(2)}, u32[]{:S(2)}) %collective-permute-start.1) | collective-permute-done | bytes 524320 | tf_op jit(solution)/shard_map/ppermute | solution.py:195
  113.9 2.0 collective-permute-done.2
  115.9 0.3 pad_maximum_fusion.own
  116.2 3.5 %collective-permute-start.3 = (bf16[4,2,1024,128]{3,2,1,0:T(8,128)(2,1)S(1)}, bf16[4,2,1024,128]{3,2,1,0:T(8,128)(2,1)S(1)}, u32[]{:S(2)}, u32[]{:S(2)}) collective-permute-start(bf16[4,2,1024,128]{3,2,1,0:T(8,128)(2,1)S(1)} %pad_maximum_fusion.own), channel_id=1, source_target_pairs={{0,1},{1,0},{2,3},{3,2},{4,5},{5,4},{6,7},{7,6},{8,9},{9,8},{10,11... | collective-permute-start | bytes 6291464 | tf_op jit(solution)/shard_map/ppermute | solution.py:197
  119.7 3.8 %collective-permute-done.3.other = bf16[4,2,1024,128]{3,2,1,0:T(8,128)(2,1)S(1)} collective-permute-done((bf16[4,2,1024,128]{3,2,1,0:T(8,128)(2,1)S(1)}, bf16[4,2,1024,128]{3,2,1,0:T(8,128)(2,1)S(1)}, u32[]{:S(2)}, u32[]{:S(2)}) %collective-permute-start.3) | collective-permute-done | bytes 2097184 | tf_op jit(solution)/shard_map/ppermute | solution.py:197
  123.4 1.3 copy-done.1
  124.8 0.0 all-to-all-done.1
  124.8 1.6 copy-done.2
  126.4 1.8 shard_map.65
  128.2 1.2 copy-done
  129.4 4.2 %all-to-all-start.2 = ((bf16[4,2,2,384,128]{4,3,2,1,0:T(8,128)(2,1)}), bf16[4,2,2,384,128]{4,3,2,1,0:T(8,128)(2,1)S(1)}, u32[]{:S(2)}, u32[]{:S(2)}) async-start(bf16[4,2,2,384,128]{4,3,2,1,0:T(8,128)(2,1)} %copy-done), calls=%async_computation.2 | async-start | bytes 3145728 | tf_op jit(solution)/shard_map/all_to_all | solution.py:207
  133.6 0.0 copy-done.3
  133.6 2.6 %collective-permute-start.4 = (bf16[1024,512]{1,0:T(8,128)(2,1)S(1)}, bf16[1024,512]{1,0:T(8,128)(2,1)}, u32[]{:S(2)}, u32[]{:S(2)}) collective-permute-start(bf16[1024,512]{1,0:T(8,128)(2,1)S(1)} %copy-done.3), channel_id=1, source_target_pairs={{0,1},{1,0},{2,3},{3,2},{4,5},{5,4},{6,7},{7,6},{8,9},{9,8},{10,11... | collective-permute-start | bytes 3145736 | tf_op jit(solution)/shard_map/ppermute | solution.py:198
  136.1 17.6 %all-to-all-done.2.sums = bf16[4,2,2,384,128]{4,3,2,1,0:T(8,128)(2,1)S(1)} async-done(((bf16[4,2,2,384,128]{4,3,2,1,0:T(8,128)(2,1)}), bf16[4,2,2,384,128]{4,3,2,1,0:T(8,128)(2,1)S(1)}, u32[]{:S(2)}, u32[]{:S(2)}) %all-to-all-start.2) | async-done | bytes 1572896 | tf_op jit(solution)/shard_map/all_to_all | solution.py:207
  153.7 1.2 shard_map.66
  154.9 3.6 %all-to-all-start.3 = ((bf16[4,384,256]{2,1,0:T(8,128)(2,1)}), bf16[4,384,256]{2,1,0:T(8,128)(2,1)S(1)}, u32[]{:S(2)}, u32[]{:S(2)}) async-start(bf16[4,384,256]{2,1,0:T(8,128)(2,1)} %shard_map.66), calls=%async_computation.3 | async-start | bytes 1572864 | tf_op jit(solution)/shard_map/all_to_all | solution.py:208
  158.5 0.0 collective-permute-done.4.other
  158.5 10.8 %all-to-all-done.3.units = bf16[4,384,256]{2,1,0:T(8,128)(2,1)S(1)} async-done(((bf16[4,384,256]{2,1,0:T(8,128)(2,1)}), bf16[4,384,256]{2,1,0:T(8,128)(2,1)S(1)}, u32[]{:S(2)}, u32[]{:S(2)}) %all-to-all-start.3) | async-done | bytes 786464 | tf_op jit(solution)/shard_map/all_to_all | solution.py:208
  169.3 2.2 shard_map.67
  171.5 23.4 %all_to_all.31 = bf16[4,96,1024]{2,1,0:T(8,128)(2,1)S(1)} all-to-all(bf16[4,96,1024]{2,1,0:T(8,128)(2,1)S(1)} %shard_map.67), channel_id=1, replica_groups=mesh['groups'=2,'far'=8,'near'=4,'x'=4,'core'=2] {'near'}, dimensions={0} | all-to-all | bytes 1572864 | tf_op jit(solution)/shard_map/all_to_all | solution.py:210
  194.9 0.1 reduce_sum.21
  195.1 36.3 %all_to_all.32 = bf16[8,12,8,128]{3,2,1,0:T(8,128)(2,1)S(1)} all-to-all(bf16[8,12,8,128]{3,2,1,0:T(8,128)(2,1)S(1)} %bitcast.48), channel_id=1, replica_groups=mesh['groups'=2,'far'=8,'near'=4,'x'=4,'core'=2] {'far'}, dimensions={0} | all-to-all | bytes 393216 | tf_op jit(solution)/shard_map/all_to_all | solution.py:213
  231.4 0.3 fusion
  231.7 6.8 %collective-permute-start.5 = (f32[32,512]{1,0:T(8,128)S(1)}, f32[32,512]{1,0:T(8,128)S(1)}, u32[]{:S(2)}, u32[]{:S(2)}) collective-permute-start(f32[32,512]{1,0:T(8,128)S(1)} %slice.9), channel_id=1, source_target_pairs={{0,1},{1,0},{2,3},{3,2},{4,5},{5,4},{6,7},{7,6},{8,9},{9,8},{10,11... | collective-permute-start | bytes 196616 | tf_op jit(solution)/shard_map/ppermute | solution.py:226
  238.5 0.9 collective-permute-done.5
  239.4 0.6 fusion.4
  (11 shorter events, 0.1 us)
Async XLA Ops:
  0.0 0.9 copy-start.4
  1.0 0.7 copy-start.5
  1.6 0.7 copy-start.6
  2.6 83.0 %copy-start.7 = (bf16[4096,128]{1,0:T(8,128)(2,1)S(1)}, bf16[4096,128]{1,0:T(8,128)(2,1)}, u32[]{:S(2)}) copy-start(bf16[4096,128]{1,0:T(8,128)(2,1)} %param.10) | copy-start | bytes 3145732
  2.7 83.0 %copy-start.8 = (bf16[4096,128]{1,0:T(8,128)(2,1)S(1)}, bf16[4096,128]{1,0:T(8,128)(2,1)}, u32[]{:S(2)}) copy-start(bf16[4096,128]{1,0:T(8,128)(2,1)} %param.9) | copy-start | bytes 3145732
  75.7 49.0 %all-to-all-start.1 = ((bf16[4,96,1024]{2,1,0:T(8,128)(2,1)}), bf16[4,96,1024]{2,1,0:T(8,128)(2,1)S(1)}, u32[]{:S(2)}, u32[]{:S(2)}) async-start(bf16[4,96,1024]{2,1,0:T(8,128)(2,1)} %broadcast_in_dim.8), calls=%async_computation.1 | async-start | bytes 1572864 | tf_op jit(solution)/shard_map/all_to_all | solution.py:202
  85.9 15.9 %collective-permute-start = (bf16[2,1024,128]{2,1,0:T(8,128)(2,1)S(1)}, bf16[2,1024,128]{2,1,0:T(8,128)(2,1)S(1)}, u32[]{:S(2)}, u32[]{:S(2)}) collective-permute-start(bf16[2,1024,128]{2,1,0:T(8,128)(2,1)S(1)} %pad_maximum_fusion.1), channel_id=1, source_target_pairs={{0,2},{2,4},{4,6},{6,0},{1,3},{3,5},{5,7},{7,1},{8,10},{10,12},{12... | collective-permute-start | bytes 1572872 | tf_op jit(solution)/shard_map/ppermute | solution.py:195
  89.3 24.7 %collective-permute-start.1 = (bf16[2,1024,128]{2,1,0:T(8,128)(2,1)S(1)}, bf16[2,1024,128]{2,1,0:T(8,128)(2,1)S(1)}, u32[]{:S(2)}, u32[]{:S(2)}) collective-permute-start(bf16[2,1024,128]{2,1,0:T(8,128)(2,1)S(1)} %pad_maximum_fusion.2), channel_id=1, source_target_pairs={{0,4},{2,6},{4,0},{6,2},{1,5},{3,7},{5,1},{7,3},{8,12},{10,14},{12... | collective-permute-start | bytes 1572872 | tf_op jit(solution)/shard_map/ppermute | solution.py:195
  94.0 21.9 %collective-permute-start.2 = (bf16[2,1024,128]{2,1,0:T(8,128)(2,1)S(1)}, bf16[2,1024,128]{2,1,0:T(8,128)(2,1)S(1)}, u32[]{:S(2)}, u32[]{:S(2)}) collective-permute-start(bf16[2,1024,128]{2,1,0:T(8,128)(2,1)S(1)} %pad_maximum_fusion.3), channel_id=1, source_target_pairs={{0,6},{2,0},{4,2},{6,4},{1,7},{3,1},{5,3},{7,5},{8,14},{10,8},{12,... | collective-permute-start | bytes 1572872 | tf_op jit(solution)/shard_map/ppermute | solution.py:195
  116.2 7.3 %collective-permute-start.3 = (bf16[4,2,1024,128]{3,2,1,0:T(8,128)(2,1)S(1)}, bf16[4,2,1024,128]{3,2,1,0:T(8,128)(2,1)S(1)}, u32[]{:S(2)}, u32[]{:S(2)}) collective-permute-start(bf16[4,2,1024,128]{3,2,1,0:T(8,128)(2,1)S(1)} %pad_maximum_fusion.own), channel_id=1, source_target_pairs={{0,1},{1,0},{2,3},{3,2},{4,5},{5,4},{6,7},{7,6},{8,9},{9,8},{10,11... | collective-permute-start | bytes 6291464 | tf_op jit(solution)/shard_map/ppermute | solution.py:197
  123.4 1.3 copy-start.1
  124.8 1.6 copy-start.2
  128.2 1.2 copy-start
  129.4 4.2 %copy-start.3 = (bf16[1024,512]{1,0:T(8,128)(2,1)S(1)}, bf16[1024,512]{1,0:T(8,128)(2,1)}, u32[]{:S(2)}) copy-start(bf16[1024,512]{1,0:T(8,128)(2,1)} %own.1) | copy-start | bytes 3145732
  129.4 24.4 %all-to-all-start.2 = ((bf16[4,2,2,384,128]{4,3,2,1,0:T(8,128)(2,1)}), bf16[4,2,2,384,128]{4,3,2,1,0:T(8,128)(2,1)S(1)}, u32[]{:S(2)}, u32[]{:S(2)}) async-start(bf16[4,2,2,384,128]{4,3,2,1,0:T(8,128)(2,1)} %copy-done), calls=%async_computation.2 | async-start | bytes 3145728 | tf_op jit(solution)/shard_map/all_to_all | solution.py:207
  133.6 25.0 %collective-permute-start.4 = (bf16[1024,512]{1,0:T(8,128)(2,1)S(1)}, bf16[1024,512]{1,0:T(8,128)(2,1)}, u32[]{:S(2)}, u32[]{:S(2)}) collective-permute-start(bf16[1024,512]{1,0:T(8,128)(2,1)S(1)} %copy-done.3), channel_id=1, source_target_pairs={{0,1},{1,0},{2,3},{3,2},{4,5},{5,4},{6,7},{7,6},{8,9},{9,8},{10,11... | collective-permute-start | bytes 3145736 | tf_op jit(solution)/shard_map/ppermute | solution.py:198
  154.9 14.4 %all-to-all-start.3 = ((bf16[4,384,256]{2,1,0:T(8,128)(2,1)}), bf16[4,384,256]{2,1,0:T(8,128)(2,1)S(1)}, u32[]{:S(2)}, u32[]{:S(2)}) async-start(bf16[4,384,256]{2,1,0:T(8,128)(2,1)} %shard_map.66), calls=%async_computation.3 | async-start | bytes 1572864 | tf_op jit(solution)/shard_map/all_to_all | solution.py:208
  231.7 7.7 %collective-permute-start.5 = (f32[32,512]{1,0:T(8,128)S(1)}, f32[32,512]{1,0:T(8,128)S(1)}, u32[]{:S(2)}, u32[]{:S(2)}) collective-permute-start(f32[32,512]{1,0:T(8,128)S(1)} %slice.9), channel_id=1, source_target_pairs={{0,1},{1,0},{2,3},{3,2},{4,5},{5,4},{6,7},{7,6},{8,9},{9,8},{10,11... | collective-permute-start | bytes 196616 | tf_op jit(solution)/shard_map/ppermute | solution.py:226

commit v5 on v4

--- a/solution.py
+++ b/solution.py
@@ -27,7 +27,17 @@
     return [pltpu.with_memory_space_constraint(array, pltpu.VMEM) for array in arrays]
 
 
-def pack_kernel(tokens, ids, gates, packed, combine, residual):
+def pack_kernel(*refs):
+    sources, (packed, combine, residual), held, sems = refs[:3], refs[3:6], refs[6:9], refs[9]
+    moves = [
+        pltpu.make_async_copy(source, place, sems.at[number])
+        for number, (source, place) in enumerate(zip(sources, held))
+    ]
+    for move in moves:
+        move.start()
+    for move in moves:
+        move.wait()
+    tokens, ids, gates = held
     f32, bf16 = jnp.float32, jnp.bfloat16
     half = packed.shape[2]
     rows = tokens.shape[0]
@@ -78,71 +88,130 @@
 
 def pack(tokens, ids, gates, far, chip_width, out_width):
     rows = tokens.shape[0]
+    arrays = (tokens, ids.T, gates.T)
     return pl.pallas_call(
         pack_kernel,
         compiler_params=PARAMS,
-        in_specs=[whole()] * 3,
+        in_specs=[whole(pltpu.HBM)] * 3,
         out_specs=[whole()] * 3,
         out_shape=[
             pltpu.VMEM((far, 2 * PART, chip_width // 2), jnp.bfloat16),
             pltpu.VMEM((SLOTS, rows), jnp.float32),
             pltpu.VMEM((rows, out_width), jnp.bfloat16),
         ],
-    )(tokens, ids.T, gates.T)
-
-
-def product_kernel(rows, own, other, out):
-    xs, kinds, _, width = own.shape
+        scratch_shapes=[pltpu.VMEM(array.shape, array.dtype) for array in arrays]
+        + [pltpu.SemaphoreType.DMA((3,))],
+    )(*[pltpu.with_memory_space_constraint(array, pltpu.HBM) for array in arrays])
+
+
+def own_kernel(rows, *refs):
+    chunks, out, stacked, sems = refs[:-3], refs[-3], refs[-2], refs[-1]
+    xs, width = len(chunks), out.shape[-1]
+    moves = [
+        pltpu.make_async_copy(weights, stacked.at[shift], sems.at[shift])
+        for shift, weights in enumerate(chunks)
+    ]
+    for move in moves:
+        move.start()
+    x = lax.axis_index("x")
+    left = rows[...]
+    for shift, weights in enumerate(chunks):
+        to = lax.rem(x + (xs - shift), xs)
+        gate, up = weights[0], weights[1]
+        product = jnp.dot(
+            left, jnp.concatenate([gate, up], axis=1), preferred_element_type=jnp.float32
+        ).astype(out.dtype)
+        out[to, 0] = product[:, :width]
+        out[to, 1] = product[:, width:]
+    for move in moves:
+        move.wait()
+
+
+def own_products(rows, chunks):
+    xs, n_rows = len(chunks), rows.shape[0]
+    return pl.pallas_call(
+        own_kernel,
+        compiler_params=PARAMS,
+        in_specs=[whole()] * (1 + xs),
+        out_specs=[whole(), whole(pltpu.HBM)],
+        out_shape=[
+            pltpu.VMEM((xs, 2, n_rows, chunks[0].shape[2]), jnp.bfloat16),
+            pltpu.HBM((xs, *chunks[0].shape), jnp.bfloat16),
+        ],
+        scratch_shapes=[pltpu.SemaphoreType.DMA((xs,))],
+    )(rows, *chunks)
+
+
+def other_kernel(rows, stacked, out):
+    xs, _, _, width = stacked.shape
     x = lax.axis_index("x")
     left = rows[...]
     for shift in range(xs):
         to = lax.rem(x + (xs - shift), xs)
-        for core, weights in enumerate((own, other)):
-            both = jnp.concatenate([weights[shift, kind] for kind in range(kinds)], axis=1)
-            product = jnp.dot(left, both, preferred_element_type=jnp.float32).astype(out.dtype)
-            for kind in range(kinds):
-                out[to, core, kind] = product[:, kind * width : (kind + 1) * width]
-
-
-def products(rows, own, other):
-    n_rows = rows.shape[0]
-    xs, kinds, _, width = own.shape
-    return pl.pallas_call(
-        product_kernel,
-        compiler_params=PARAMS,
-        in_specs=[whole()] * 3,
+        both = jnp.concatenate([stacked[shift, 0], stacked[shift, 1]], axis=1)
+        product = jnp.dot(left, both, preferred_element_type=jnp.float32).astype(out.dtype)
+        out[to, 0] = product[:, :width]
+        out[to, 1] = product[:, width:]
+
+
+def other_products(rows, stacked):
+    xs, _, _, width = stacked.shape
+    return pl.pallas_call(
+        other_kernel,
+        compiler_params=PARAMS,
+        in_specs=[whole()] * 2,
         out_specs=whole(),
-        out_shape=pltpu.VMEM((xs, CORES, kinds, n_rows, width), jnp.bfloat16),
-    )(*near_memory(rows, own, other))
-
-
-def hidden_kernel(sums, out):
+        out_shape=pltpu.VMEM((xs, 2, rows.shape[0], width), jnp.bfloat16),
+    )(rows, stacked)
+
+
+def hidden_of(sums, at, block, dtype):
     f32 = jnp.float32
-    xs, _, _, n_rows, width = sums.shape
+    total = sums[0, :, at : at + block, :].astype(f32)
+    for source in range(1, sums.shape[0]):
+        total = total + sums[source, :, at : at + block, :].astype(f32)
+    gate, up = total[0], total[1]
+    return (gate / (1.0 + jnp.exp(-gate)) * up).astype(dtype)
+
+
+def first_kernel(sums, out):
+    block = 64
+    for at in range(0, out.shape[0], block):
+        out[at : at + block, :] = hidden_of(sums, at, block, out.dtype)
+
+
+def first_units(sums):
+    return pl.pallas_call(
+        first_kernel,
+        compiler_params=PARAMS,
+        in_specs=[whole()],
+        out_specs=whole(),
+        out_shape=pltpu.VMEM(sums.shape[2:], jnp.bfloat16),
+    )(*near_memory(sums))
+
+
+def hidden_kernel(ready, sums, out):
     straight = lax.axis_index("core") == 0
-    block = 32
-    for at in range(0, n_rows, block):
-        total = sums[0, :, :, at : at + block, :].astype(f32)
-        for source in range(1, xs):
-            total = total + sums[source, :, :, at : at + block, :].astype(f32)
-        gate, up = total[:, 0], total[:, 1]
-        hidden = (gate / (1.0 + jnp.exp(-gate)) * up).astype(out.dtype)
-        low = jnp.where(straight, hidden[0], hidden[1])
-        high = jnp.where(straight, hidden[1], hidden[0])
+    block, width = 64, ready.shape[1]
+    for at in range(0, ready.shape[0], block):
+        mine = ready[at : at + block, :]
+        theirs = hidden_of(sums, at, block, out.dtype)
+        low = jnp.where(straight, mine, theirs)
+        high = jnp.where(straight, theirs, mine)
         for copy in range(out.shape[0]):
             out[copy, at : at + block, 0:width] = low
             out[copy, at : at + block, width : 2 * width] = high
 
 
-def hidden_units(sums):
-    xs, cores, _, n_rows, width = sums.shape
+def hidden_units(ready, sums):
+    xs, _, n_rows, width = sums.shape
     return pl.pallas_call(
         hidden_kernel,
         compiler_params=PARAMS,
-        in_specs=[whole()],
+        in_specs=[whole()] * 2,
         out_specs=whole(),
-        out_shape=pltpu.VMEM((xs, n_rows, cores * width), jnp.bfloat16),
-    )(*near_memory(sums))
+        out_shape=pltpu.VMEM((xs, n_rows, CORES * width), jnp.bfloat16),
+    )(*near_memory(ready, sums))
 
 
 def down_kernel(units, own, other, out):
@@ -193,19 +262,18 @@
     chunks = [chunk(0)]
     for shift in range(1, xs):
         chunks.append(lax.ppermute(chunk(shift), "x", [(i, (i + shift) % xs) for i in range(xs)]))
-    own = jnp.stack(chunks)
-    other = lax.ppermute(own, "core", swap)
     down_other = lax.ppermute(down_weight, "core", swap)
 
     arrived = arrived.reshape(far, 2, PART, chip_width // 2)
-    arrived = jnp.swapaxes(arrived, 1, 2).reshape(1, far * PART, chip_width)
-    rows = lax.all_to_all(
-        jnp.broadcast_to(arrived, (near, far * PART, chip_width)), "near", 0, 0, tiled=True
-    )
-    n_rows = near * far * PART
-    partial = products(rows.reshape(n_rows, chip_width), own, other)
-    sums = lax.all_to_all(partial, "x", 0, 0, tiled=True)
-    units = lax.all_to_all(hidden_units(sums), "x", 0, 0, tiled=True)
+    arrived = jnp.swapaxes(arrived, 1, 2).reshape(far * PART, chip_width)
+    rows = lax.all_gather(arrived, "near", axis=0, tiled=True)
+    mine, stacked = own_products(rows, chunks)
+    mine = lax.all_to_all(mine, "x", 0, 0, tiled=True)
+    stacked = lax.ppermute(stacked, "core", swap)
+    theirs = other_products(rows, stacked)
+    theirs = lax.all_to_all(theirs, "x", 0, 0, tiled=True)
+    ready = first_units(mine)
+    units = lax.all_to_all(hidden_units(ready, theirs), "x", 0, 0, tiled=True)
     produced = down(units, down_weight, down_other, near)
     parts = lax.all_to_all(produced, "near", 0, 0, tiled=True)
     summed = jnp.sum(parts.astype(f32), axis=0).astype(bf16)

time: 241 us -> 220 us (0.913)
  blocking collectives: 131 us -> 80.1 us
  starting transfers between devices: 41.5 us -> 81.4 us
  waiting for transfers between devices: 51.9 us -> 40.7 us
  Pallas kernels: 5.51 us -> 11.6 us
  local copies, waits for them, and re-layouts: 7.89 us -> 1.97 us
    all_to_all x1 -> x0, blocking collectives: 71.8 us -> none  [layer(): arrived = lax.all_to_all(sent, 'far', 0, 0, tiled=True)]
    all_to_all x3 -> x4, starting transfers between devices: 17.7 us -> 55.5 us  [the longest x1 44 us: layer(): arrived = lax.all_to_all(sent, 'far', 0, 0, tiled=True)]
    all_gather x0 -> x1, blocking collectives: none -> 22.2 us  [layer(): rows = lax.all_gather(arrived, 'near', axis=0, tiled=True)]
    ppermute x3, waiting for transfers between devices: 18.9 us -> 0.01 us  [layer(): lax.ppermute(chunk(shift), 'x', [(i, (i + shift) % xs) for i in range(xs)])]
    all_to_all x3 -> x4, waiting for transfers between devices: 28.3 us -> 39.8 us  [the longest x1 13.5 us: layer(): arrived = lax.all_to_all(sent, 'far', 0, 0, tiled=True)]
    unnamed x20 -> x4, local copies, waits for them, and re-layouts: 6.47 us -> 0.06 us
    pallas_call x3 -> x5, Pallas kernels: 3.32 us -> 9.39 us  [the longest x1 3.58 us: other_products(): pl.pallas_call(other_kernel, compiler_params=PARAMS, in_specs=[whole()] *...]
    ppermute x1, waiting for transfers between devices: 3.76 us -> 0.01 us  [layer(): stacked = lax.ppermute(stacked, 'core', swap)]
  transfers between devices with their start and end apart: 9 -> 10, of which waited for: 7 -> 5; matrix products, arithmetic and copies ran while one was open for 0% -> 2% of each run, Pallas kernels for 1% -> 2%
where the time goes in v5:
time: 220 us; the launch traced here: 219 us
  starting transfers between devices  81.4 us (37%)
  blocking collectives  80.1 us (36%)
  waiting for transfers between devices  40.7 us (19%)
  Pallas kernels  11.6 us (5%)
  other arithmetic  2.59 us (1%)
    all_to_all x1, starting transfers between devices, layer(): arrived = lax.all_to_all(sent, 'far', 0, 0, tiled=True)  44 us
    all_to_all x1, blocking collectives, layer(): lax.all_to_all(summed.reshape(far, PART, out_lanes, 128), 'far', 0, 0, ti...  36.3 us
    all_gather x1, blocking collectives, layer(): rows = lax.all_gather(arrived, 'near', axis=0, tiled=True)  22.2 us
    all_to_all x1, blocking collectives, layer(): parts = lax.all_to_all(produced, 'near', 0, 0, tiled=True)  21.6 us
    all_to_all x1, waiting for transfers between devices, layer(): arrived = lax.all_to_all(sent, 'far', 0, 0, tiled=True)  13.5 us
    ppermute x3, starting transfers between devices, layer(): lax.ppermute(chunk(shift), 'x', [(i, (i + shift) % xs) for i in range(xs)])  10.9 us
    all_to_all x1, waiting for transfers between devices, layer(): units = lax.all_to_all(hidden_units(ready, theirs), 'x', 0, 0, tiled=True)  9.98 us
    all_to_all x1, waiting for transfers between devices, layer(): mine = lax.all_to_all(mine, 'x', 0, 0, tiled=True)  8.5 us
  transfers between devices with their start and end apart: 10, of which 5 were waited for; matrix products, arithmetic and copies ran while one was open for 2% of the time, Pallas kernels for 2%

profile of v5, /device:TPU:33, one launch (start us, length us, event | category | flops | bytes accessed | tf_op | source)
XLA Modules:
  0.0 218.8 jit_solution(12467009645258766022)
XLA Ops:
  0.0 2.0 shard_map.64
  2.0 44.0 %all-to-all-start = ((bf16[8,24,512]{2,1,0:T(8,128)(2,1)}), bf16[8,24,512]{2,1,0:T(8,128)(2,1)S(1)}, u32[]{:S(2)}, u32[]{:S(2)}) async-start(bf16[8,24,512]{2,1,0:T(8,128)(2,1)} %get-tuple-element.12), calls=%async_computation | async-start | bytes 393216 | tf_op jit(solution)/shard_map/all_to_all | solution.py:251
  46.0 1.6 dynamic-slice_bitcast_fusion
  47.6 0.1 pad_maximum_fusion.1
  47.7 3.3 %collective-permute-start = (bf16[2,1024,128]{2,1,0:T(8,128)(2,1)S(1)}, bf16[2,1024,128]{2,1,0:T(8,128)(2,1)S(1)}, u32[]{:S(2)}, u32[]{:S(2)}) collective-permute-start(bf16[2,1024,128]{2,1,0:T(8,128)(2,1)S(1)} %pad_maximum_fusion.1), channel_id=1, source_target_pairs={{0,2},{2,4},{4,6},{6,0},{1,3},{3,5},{5,7},{7,1},{8,10},{10,12},{12... | collective-permute-start | bytes 1572872 | tf_op jit(solution)/shard_map/ppermute | solution.py:264
  51.0 0.9 pad_maximum_fusion.2
  51.9 4.6 %collective-permute-start.1 = (bf16[2,1024,128]{2,1,0:T(8,128)(2,1)}, bf16[2,1024,128]{2,1,0:T(8,128)(2,1)S(1)}, u32[]{:S(2)}, u32[]{:S(2)}) collective-permute-start(bf16[2,1024,128]{2,1,0:T(8,128)(2,1)} %pad_maximum_fusion.2), channel_id=1, source_target_pairs={{0,4},{2,6},{4,0},{6,2},{1,5},{3,7},{5,1},{7,3},{8,12},{10,14},{12... | collective-permute-start | bytes 1572872 | tf_op jit(solution)/shard_map/ppermute | solution.py:264
  56.5 0.8 pad_maximum_fusion.3
  57.4 2.9 %collective-permute-start.2 = (bf16[2,1024,128]{2,1,0:T(8,128)(2,1)}, bf16[2,1024,128]{2,1,0:T(8,128)(2,1)S(1)}, u32[]{:S(2)}, u32[]{:S(2)}) collective-permute-start(bf16[2,1024,128]{2,1,0:T(8,128)(2,1)} %pad_maximum_fusion.3), channel_id=1, source_target_pairs={{0,6},{2,0},{4,2},{6,4},{1,7},{3,1},{5,3},{7,5},{8,14},{10,8},{12,... | collective-permute-start | bytes 1572872 | tf_op jit(solution)/shard_map/ppermute | solution.py:264
  60.3 0.1 pad_maximum_fusion.refs_0_
  60.4 13.5 %all-to-all-done = bf16[8,24,512]{2,1,0:T(8,128)(2,1)S(1)} async-done(((bf16[8,24,512]{2,1,0:T(8,128)(2,1)}), bf16[8,24,512]{2,1,0:T(8,128)(2,1)S(1)}, u32[]{:S(2)}, u32[]{:S(2)}) %all-to-all-start) | async-done | bytes 196640 | tf_op jit(solution)/shard_map/all_to_all | solution.py:251
  73.8 0.1 copy.10
  73.9 0.2 copy.11
  74.2 22.2 %all_gather.3.rows = bf16[384,1024]{1,0:T(8,128)(2,1)S(1)} all-gather(bf16[96,1024]{1,0:T(8,128)(2,1)S(1)} %bitcast.41), channel_id=1, replica_groups=mesh['groups'=2,'far'=8,'near'=4,'x'=4,'core'=2] {'near'}, dimensions={0}, use_global_device_ids=true | all-gather | bytes 983040 | tf_op jit(solution)/shard_map/all_gather | solution.py:269
  96.4 0.0 collective-permute-done.refs_1_
  96.4 0.0 collective-permute-done.1.refs_2_
  96.4 0.0 collective-permute-done.2.refs_3_
  96.4 2.6 %shard_map.65 = (bf16[4,2,384,128]{3,2,1,0:T(8,128)(2,1)}, bf16[4,2,1024,128]{3,2,1,0:T(8,128)(2,1)}) custom-call(bf16[384,1024]{1,0:T(8,128)(2,1)S(1)} %all_gather.3.rows, bf16[2,1024,128]{2,1,0:T(8,128)(2,1)S(1)} %pad_maximum_fusion.refs_0_, bf16[2,1024,128]{2,1,0:T(8,128)(2,1)S(1)} %collective-permute-done.refs_1_, ...), custom_call_target="tpu_custom_call" | custom-call | tf_op jit(solution)/shard_map/pallas_call | solution.py:132
  98.9 5.0 %collective-permute-start.3 = (bf16[4,2,1024,128]{3,2,1,0:T(8,128)(2,1)}, bf16[4,2,1024,128]{3,2,1,0:T(8,128)(2,1)}, u32[]{:S(2)}, u32[]{:S(2)}) collective-permute-start(bf16[4,2,1024,128]{3,2,1,0:T(8,128)(2,1)} %get-tuple-element.14), channel_id=1, source_target_pairs={{0,1},{1,0},{2,3},{3,2},{4,5},{5,4},{6,7},{7,6},{8,9},{9,8},{10,11... | collective-permute-start | bytes 6291464 | tf_op jit(solution)/shard_map/ppermute | solution.py:272
  103.9 4.3 %all-to-all-start.1 = ((bf16[4,2,384,128]{3,2,1,0:T(8,128)(2,1)}), bf16[4,2,384,128]{3,2,1,0:T(8,128)(2,1)S(1)}, u32[]{:S(2)}, u32[]{:S(2)}) async-start(bf16[4,2,384,128]{3,2,1,0:T(8,128)(2,1)} %get-tuple-element.13), calls=%async_computation.1 | async-start | bytes 1572864 | tf_op jit(solution)/shard_map/all_to_all | solution.py:271
  108.2 0.0 copy-start
  108.2 0.0 collective-permute-done.3.stacked
  108.2 3.6 %shard_map.67 = bf16[4,2,384,128]{3,2,1,0:T(8,128)(2,1)} custom-call(bf16[384,1024]{1,0:T(8,128)(2,1)S(1)} %all_gather.3.rows, bf16[4,2,1024,128]{3,2,1,0:T(8,128)(2,1)} %collective-permute-done.3.stacked), custom_call_target="tpu_custom_call" | custom-call | tf_op jit(solution)/shard_map/pallas_call | solution.py:159
  111.8 8.5 %all-to-all-done.1.sums = bf16[4,2,384,128]{3,2,1,0:T(8,128)(2,1)S(1)} async-done(((bf16[4,2,384,128]{3,2,1,0:T(8,128)(2,1)}), bf16[4,2,384,128]{3,2,1,0:T(8,128)(2,1)S(1)}, u32[]{:S(2)}, u32[]{:S(2)}) %all-to-all-start.1) | async-done | bytes 786464 | tf_op jit(solution)/shard_map/all_to_all | solution.py:271
  120.3 3.6 %all-to-all-start.2 = ((bf16[4,2,384,128]{3,2,1,0:T(8,128)(2,1)}), bf16[4,2,384,128]{3,2,1,0:T(8,128)(2,1)S(1)}, u32[]{:S(2)}, u32[]{:S(2)}) async-start(bf16[4,2,384,128]{3,2,1,0:T(8,128)(2,1)} %shard_map.67), calls=%async_computation.2 | async-start | bytes 1572864 | tf_op jit(solution)/shard_map/all_to_all | solution.py:274
  123.9 0.0 copy-done
  123.9 3.1 %collective-permute-start.4 = (bf16[1024,512]{1,0:T(8,128)(2,1)S(1)}, bf16[1024,512]{1,0:T(8,128)(2,1)}, u32[]{:S(2)}, u32[]{:S(2)}) collective-permute-start(bf16[1024,512]{1,0:T(8,128)(2,1)S(1)} %copy-done), channel_id=1, source_target_pairs={{0,1},{1,0},{2,3},{3,2},{4,5},{5,4},{6,7},{7,6},{8,9},{9,8},{10,11... | collective-permute-start | bytes 3145736 | tf_op jit(solution)/shard_map/ppermute | solution.py:265
  127.0 0.1 shard_map.66.ready
  127.2 7.9 %all-to-all-done.2.sums = bf16[4,2,384,128]{3,2,1,0:T(8,128)(2,1)S(1)} async-done(((bf16[4,2,384,128]{3,2,1,0:T(8,128)(2,1)}), bf16[4,2,384,128]{3,2,1,0:T(8,128)(2,1)S(1)}, u32[]{:S(2)}, u32[]{:S(2)}) %all-to-all-start.2) | async-done | bytes 786464 | tf_op jit(solution)/shard_map/all_to_all | solution.py:274
  135.0 1.1 shard_map.68
  136.1 3.6 %all-to-all-start.3 = ((bf16[4,384,256]{2,1,0:T(8,128)(2,1)}), bf16[4,384,256]{2,1,0:T(8,128)(2,1)S(1)}, u32[]{:S(2)}, u32[]{:S(2)}) async-start(bf16[4,384,256]{2,1,0:T(8,128)(2,1)} %shard_map.68), calls=%async_computation.3 | async-start | bytes 1572864 | tf_op jit(solution)/shard_map/all_to_all | solution.py:276
  139.7 0.0 collective-permute-done.4.other
  139.7 10.0 %all-to-all-done.3.units = bf16[4,384,256]{2,1,0:T(8,128)(2,1)S(1)} async-done(((bf16[4,384,256]{2,1,0:T(8,128)(2,1)}), bf16[4,384,256]{2,1,0:T(8,128)(2,1)S(1)}, u32[]{:S(2)}, u32[]{:S(2)}) %all-to-all-start.3) | async-done | bytes 786464 | tf_op jit(solution)/shard_map/all_to_all | solution.py:276
  149.7 2.2 %shard_map.69 = bf16[4,96,1024]{2,1,0:T(8,128)(2,1)S(1)} custom-call(bf16[4,384,256]{2,1,0:T(8,128)(2,1)S(1)} %all-to-all-done.3.units, bf16[1024,512]{1,0:T(8,128)(2,1)S(1)} %copy-done, bf16[1024,512]{1,0:T(8,128)(2,1)} %collective-permute-done.4.other), custom_call_target="tpu_custom_call" | custom-call | tf_op jit(solution)/shard_map/pallas_call | solution.py:232
  151.9 21.6 %all_to_all.30 = bf16[4,96,1024]{2,1,0:T(8,128)(2,1)S(1)} all-to-all(bf16[4,96,1024]{2,1,0:T(8,128)(2,1)S(1)} %shard_map.69), channel_id=1, replica_groups=mesh['groups'=2,'far'=8,'near'=4,'x'=4,'core'=2] {'near'}, dimensions={0} | all-to-all | bytes 1572864 | tf_op jit(solution)/shard_map/all_to_all | solution.py:278
  173.5 0.1 reduce_sum.21
  173.7 36.3 %all_to_all.31 = bf16[8,12,8,128]{3,2,1,0:T(8,128)(2,1)S(1)} all-to-all(bf16[8,12,8,128]{3,2,1,0:T(8,128)(2,1)S(1)} %bitcast.39), channel_id=1, replica_groups=mesh['groups'=2,'far'=8,'near'=4,'x'=4,'core'=2] {'far'}, dimensions={0} | all-to-all | bytes 393216 | tf_op jit(solution)/shard_map/all_to_all | solution.py:281
  210.0 0.3 fusion
  210.3 7.0 %collective-permute-start.5 = (f32[32,512]{1,0:T(8,128)S(1)}, f32[32,512]{1,0:T(8,128)S(1)}, u32[]{:S(2)}, u32[]{:S(2)}) collective-permute-start(f32[32,512]{1,0:T(8,128)S(1)} %slice.9), channel_id=1, source_target_pairs={{0,1},{1,0},{2,3},{3,2},{4,5},{5,4},{6,7},{7,6},{8,9},{9,8},{10,11... | collective-permute-start | bytes 196616 | tf_op jit(solution)/shard_map/ppermute | solution.py:294
  217.3 0.9 collective-permute-done.5
  218.2 0.6 fusion.4
  (4 shorter events, 0.1 us)
Async XLA Ops:
  2.0 71.8 %all-to-all-start = ((bf16[8,24,512]{2,1,0:T(8,128)(2,1)}), bf16[8,24,512]{2,1,0:T(8,128)(2,1)S(1)}, u32[]{:S(2)}, u32[]{:S(2)}) async-start(bf16[8,24,512]{2,1,0:T(8,128)(2,1)} %get-tuple-element.12), calls=%async_computation | async-start | bytes 393216 | tf_op jit(solution)/shard_map/all_to_all | solution.py:251
  47.7 48.7 %collective-permute-start = (bf16[2,1024,128]{2,1,0:T(8,128)(2,1)S(1)}, bf16[2,1024,128]{2,1,0:T(8,128)(2,1)S(1)}, u32[]{:S(2)}, u32[]{:S(2)}) collective-permute-start(bf16[2,1024,128]{2,1,0:T(8,128)(2,1)S(1)} %pad_maximum_fusion.1), channel_id=1, source_target_pairs={{0,2},{2,4},{4,6},{6,0},{1,3},{3,5},{5,7},{7,1},{8,10},{10,12},{12... | collective-permute-start | bytes 1572872 | tf_op jit(solution)/shard_map/ppermute | solution.py:264
  51.9 44.5 %collective-permute-start.1 = (bf16[2,1024,128]{2,1,0:T(8,128)(2,1)}, bf16[2,1024,128]{2,1,0:T(8,128)(2,1)S(1)}, u32[]{:S(2)}, u32[]{:S(2)}) collective-permute-start(bf16[2,1024,128]{2,1,0:T(8,128)(2,1)} %pad_maximum_fusion.2), channel_id=1, source_target_pairs={{0,4},{2,6},{4,0},{6,2},{1,5},{3,7},{5,1},{7,3},{8,12},{10,14},{12... | collective-permute-start | bytes 1572872 | tf_op jit(solution)/shard_map/ppermute | solution.py:264
  57.4 39.0 %collective-permute-start.2 = (bf16[2,1024,128]{2,1,0:T(8,128)(2,1)}, bf16[2,1024,128]{2,1,0:T(8,128)(2,1)S(1)}, u32[]{:S(2)}, u32[]{:S(2)}) collective-permute-start(bf16[2,1024,128]{2,1,0:T(8,128)(2,1)} %pad_maximum_fusion.3), channel_id=1, source_target_pairs={{0,6},{2,0},{4,2},{6,4},{1,7},{3,1},{5,3},{7,5},{8,14},{10,8},{12,... | collective-permute-start | bytes 1572872 | tf_op jit(solution)/shard_map/ppermute | solution.py:264
  98.9 9.3 %collective-permute-start.3 = (bf16[4,2,1024,128]{3,2,1,0:T(8,128)(2,1)}, bf16[4,2,1024,128]{3,2,1,0:T(8,128)(2,1)}, u32[]{:S(2)}, u32[]{:S(2)}) collective-permute-start(bf16[4,2,1024,128]{3,2,1,0:T(8,128)(2,1)} %get-tuple-element.14), channel_id=1, source_target_pairs={{0,1},{1,0},{2,3},{3,2},{4,5},{5,4},{6,7},{7,6},{8,9},{9,8},{10,11... | collective-permute-start | bytes 6291464 | tf_op jit(solution)/shard_map/ppermute | solution.py:272
  103.9 16.4 %all-to-all-start.1 = ((bf16[4,2,384,128]{3,2,1,0:T(8,128)(2,1)}), bf16[4,2,384,128]{3,2,1,0:T(8,128)(2,1)S(1)}, u32[]{:S(2)}, u32[]{:S(2)}) async-start(bf16[4,2,384,128]{3,2,1,0:T(8,128)(2,1)} %get-tuple-element.13), calls=%async_computation.1 | async-start | bytes 1572864 | tf_op jit(solution)/shard_map/all_to_all | solution.py:271
  108.2 15.7 %copy-start = (bf16[1024,512]{1,0:T(8,128)(2,1)S(1)}, bf16[1024,512]{1,0:T(8,128)(2,1)}, u32[]{:S(2)}) copy-start(bf16[1024,512]{1,0:T(8,128)(2,1)} %own.1) | copy-start | bytes 3145732
  120.3 14.7 %all-to-all-start.2 = ((bf16[4,2,384,128]{3,2,1,0:T(8,128)(2,1)}), bf16[4,2,384,128]{3,2,1,0:T(8,128)(2,1)S(1)}, u32[]{:S(2)}, u32[]{:S(2)}) async-start(bf16[4,2,384,128]{3,2,1,0:T(8,128)(2,1)} %shard_map.67), calls=%async_computation.2 | async-start | bytes 1572864 | tf_op jit(solution)/shard_map/all_to_all | solution.py:274
  123.9 15.8 %collective-permute-start.4 = (bf16[1024,512]{1,0:T(8,128)(2,1)S(1)}, bf16[1024,512]{1,0:T(8,128)(2,1)}, u32[]{:S(2)}, u32[]{:S(2)}) collective-permute-start(bf16[1024,512]{1,0:T(8,128)(2,1)S(1)} %copy-done), channel_id=1, source_target_pairs={{0,1},{1,0},{2,3},{3,2},{4,5},{5,4},{6,7},{7,6},{8,9},{9,8},{10,11... | collective-permute-start | bytes 3145736 | tf_op jit(solution)/shard_map/ppermute | solution.py:265
  136.1 13.6 %all-to-all-start.3 = ((bf16[4,384,256]{2,1,0:T(8,128)(2,1)}), bf16[4,384,256]{2,1,0:T(8,128)(2,1)S(1)}, u32[]{:S(2)}, u32[]{:S(2)}) async-start(bf16[4,384,256]{2,1,0:T(8,128)(2,1)} %shard_map.68), calls=%async_computation.3 | async-start | bytes 1572864 | tf_op jit(solution)/shard_map/all_to_all | solution.py:276
  210.3 7.9 %collective-permute-start.5 = (f32[32,512]{1,0:T(8,128)S(1)}, f32[32,512]{1,0:T(8,128)S(1)}, u32[]{:S(2)}, u32[]{:S(2)}) collective-permute-start(f32[32,512]{1,0:T(8,128)S(1)} %slice.9), channel_id=1, source_target_pairs={{0,1},{1,0},{2,3},{3,2},{4,5},{5,4},{6,7},{7,6},{8,9},{9,8},{10,11... | collective-permute-start | bytes 196616 | tf_op jit(solution)/shard_map/ppermute | solution.py:294

commit v6 on v4

v6 whole, which is shorter than its diff:
```python
import jax
import jax.numpy as jnp
from jax import lax
from jax.experimental import pallas as pl
from jax.experimental.pallas import tpu as pltpu
from jax.sharding import Mesh, PartitionSpec as P


EXPERTS = 4
CAP = 24
NEAR = 4
CORES = 2
PART = CAP // CORES

EPSILON = 1e-05


def whole(space=None):
    return pl.BlockSpec(memory_space=space or pltpu.VMEM)


PARAMS = pltpu.CompilerParams(vmem_limit_bytes=16 << 20)


def near_memory(*arrays):
    return [pltpu.with_memory_space_constraint(array, pltpu.VMEM) for array in arrays]


def pack_kernel(*refs):
    sources, (packed, combine, residual), held, sems = refs[:3], refs[3:6], refs[6:9], refs[9]
    moves = [
        pltpu.make_async_copy(source, place, sems.at[number])
        for number, (source, place) in enumerate(zip(sources, held))
    ]
    for move in moves:
        move.start()
    for move in moves:
        move.wait()
    tokens, ids, gates = held
    f32, bf16 = jnp.float32, jnp.bfloat16
    width = packed.shape[2]
    rows = tokens.shape[0]
    slots = EXPERTS * CAP
    floats = tokens[...].astype(f32)
    scale = lax.rsqrt(jnp.mean(floats * floats, axis=1, keepdims=True) + EPSILON)
    slot = lax.broadcasted_iota(jnp.int32, (slots, rows), 0)
    expert = sum((slot >= CAP * e).astype(jnp.int32) for e in range(1, EXPERTS))
    wanted = (slot - expert * CAP).astype(f32)
    first = ids[0:1, :] == expert
    second = ids[1:2, :] == expert
    named = jnp.where(jnp.logical_or(first, second), 1.0, 0.0)
    before = jnp.where(
        lax.broadcasted_iota(jnp.int32, (rows, rows), 0)
        < lax.broadcasted_iota(jnp.int32, (rows, rows), 1),
        1.0,
        0.0,
    ).astype(bf16)
    position = jnp.dot(named.astype(bf16), before, preferred_element_type=f32)
    picker = jnp.where(position == wanted, named, 0.0)
    gate = jnp.where(first, gates[0:1, :], jnp.where(second, gates[1:2, :], 0.0))
    combine[...] = picker * gate
    start = pl.multiple_of((lax.axis_index("x") * CORES + lax.axis_index("core")) * width, width)
    mine = tokens[:, pl.ds(start, width)]
    residual[...] = mine
    normed = (mine.astype(f32) * scale).astype(bf16)
    total = jnp.dot(picker.astype(bf16), normed, preferred_element_type=f32).astype(bf16)
    copies = packed.shape[0] // EXPERTS
    for e in range(EXPERTS):
        for copy in range(copies):
            packed[e * copies + copy] = total[e * CAP : (e + 1) * CAP]


def pack(tokens, ids, gates, far, width):
    rows = tokens.shape[0]
    arrays = (tokens, ids.T, gates.T)
    return pl.pallas_call(
        pack_kernel,
        compiler_params=PARAMS,
        in_specs=[whole(pltpu.HBM)] * 3,
        out_specs=[whole()] * 3,
        out_shape=[
            pltpu.VMEM((far, CAP, width), jnp.bfloat16),
            pltpu.VMEM((EXPERTS * CAP, rows), jnp.float32),
            pltpu.VMEM((rows, width), jnp.bfloat16),
        ],
        scratch_shapes=[pltpu.VMEM(array.shape, array.dtype) for array in arrays]
        + [pltpu.SemaphoreType.DMA((3,))],
    )(*[pltpu.with_memory_space_constraint(array, pltpu.HBM) for array in arrays])


def product_kernel(own, other, *refs):
    count = (len(refs) - 2) // 2
    sources, out, held, sems = refs[:count], refs[count], refs[count + 1 : -1], refs[-1]
    moves = [
        pltpu.make_async_copy(source, place, sems.at[shift])
        for shift, (source, place) in enumerate(zip(sources, held))
    ]
    for move in moves:
        move.start()
    x, core = lax.axis_index("x"), lax.axis_index("core")
    width, depth = out.shape[-1], own.shape[1]
    for shift in range(count):
        moves[shift].wait()
        to = lax.rem(x + (count - shift), count)
        product = 0.0
        for left, side in ((own, core), (other, 1 - core)):
            at = pl.multiple_of(side * depth, depth)
            both = jnp.concatenate(
                [held[shift][kind, pl.ds(at, depth), :] for kind in range(2)], axis=1
            )
            product = product + jnp.dot(left[...], both, preferred_element_type=jnp.float32)
        product = product.astype(out.dtype)
        for kind in range(2):
            out[to, kind] = product[:, kind * width : (kind + 1) * width]


def products(own, other, chunks):
    xs, n_rows, width = len(chunks), own.shape[0], chunks[0].shape[2]
    chunks = [pltpu.with_memory_space_constraint(chunk, pltpu.HBM) for chunk in chunks]
    return pl.pallas_call(
        product_kernel,
        compiler_params=PARAMS,
        in_specs=[whole()] * 2 + [whole(pltpu.HBM)] * xs,
        out_specs=whole(),
        out_shape=pltpu.VMEM((xs, 2, n_rows, width), jnp.bfloat16),
        scratch_shapes=[pltpu.VMEM(chunk.shape, chunk.dtype) for chunk in chunks]
        + [pltpu.SemaphoreType.DMA((xs,))],
    )(*near_memory(own, other), *chunks)


def hidden_kernel(sums, out):
    f32 = jnp.float32
    block = sums.shape[2] // (NEAR * CORES)
    for line in range(NEAR):
        for side in range(CORES):
            at = (line * CORES + side) * block
            total = sums[0, :, at : at + block, :].astype(f32)
            for source in range(1, sums.shape[0]):
                total = total + sums[source, :, at : at + block, :].astype(f32)
            gate, up = total[0], total[1]
            hidden = (gate / (1.0 + jnp.exp(-gate)) * up).astype(out.dtype)
            for copy in range(out.shape[0] // CORES):
                out[copy * CORES + side, line * block : (line + 1) * block, :] = hidden


def hidden_units(sums):
    xs, _, n_rows, width = sums.shape
    return pl.pallas_call(
        hidden_kernel,
        compiler_params=PARAMS,
        in_specs=[whole()],
        out_specs=whole(),
        out_shape=pltpu.VMEM((xs * CORES, n_rows // CORES, width), jnp.bfloat16),
    )(*near_memory(sums))


def down_kernel(units, own, other, out):
    near, _, block, _ = out.shape
    core = lax.axis_index("core")
    left = jnp.concatenate([units[source] for source in range(units.shape[0])], axis=1)
    for side, weight in ((core, own), (1 - core, other)):
        product = jnp.dot(left, weight[...], preferred_element_type=jnp.float32).astype(out.dtype)
        for line in range(near):
            out[line, side] = product[line * block : (line + 1) * block]


def down(units, own, other, near):
    n_rows = units.shape[1]
    return pl.pallas_call(
        down_kernel,
        compiler_params=PARAMS,
        in_specs=[whole()] * 3,
        out_specs=whole(),
        out_shape=pltpu.VMEM((near, CORES, n_rows // near, own.shape[1]), jnp.bfloat16),
    )(*near_memory(units, own, other))


def layer(tokens, route_ids, route_gates, gate_weight, up_weight, down_weight):
    f32, bf16 = jnp.float32, jnp.bfloat16
    model_width = tokens.shape[1]
    far, near, xs = lax.axis_size("far"), lax.axis_size("near"), lax.axis_size("x")
    x = lax.axis_index("x")
    chip_width = model_width // xs
    out_width = down_weight.shape[1]
    copies = far // EXPERTS
    swap = [(i, (i + 1) % CORES) for i in range(CORES)]
    sent, combine, residual = pack(tokens, route_ids, route_gates, far, out_width)
    arrived = lax.all_to_all(sent, "far", 0, 0, tiled=True)

    def chunk(shift):
        start = (x + shift) % xs * chip_width
        return jnp.stack(
            [
                lax.dynamic_slice_in_dim(weight, start, chip_width, 0)
                for weight in (gate_weight, up_weight)
            ]
        )

    chunks = [chunk(0)]
    for shift in range(1, xs):
        chunks.append(lax.ppermute(chunk(shift), "x", [(i, (i + shift) % xs) for i in range(xs)]))
    down_other = lax.ppermute(down_weight, "core", swap)

    arrived = arrived.reshape(far, CORES, PART, out_width)
    arrived = jnp.swapaxes(arrived, 0, 1).reshape(far * CAP, out_width)
    rows = lax.all_gather(arrived, "near", axis=0, tiled=True)
    rows_other = lax.ppermute(rows, "core", swap)
    sums = lax.all_to_all(products(rows, rows_other, chunks), "x", 0, 0, tiled=True)
    units = lax.all_to_all(hidden_units(sums), ("x", "core"), 0, 0, tiled=True)
    produced = down(units, down_weight, down_other, near)
    parts = lax.all_to_all(
        produced.reshape(near * CORES, far * PART, out_width), ("near", "core"), 0, 0, tiled=True
    )
    summed = jnp.sum(
        parts.reshape(near, CORES, far, PART, out_width).astype(f32), axis=0
    ).astype(bf16)
    summed = jnp.swapaxes(summed, 0, 1).reshape(far, CAP, out_width)
    returned = lax.all_to_all(summed, "far", 0, 0, tiled=True)
    returned = jnp.sum(
        returned.reshape(EXPERTS, copies, CAP, out_width).astype(f32), axis=1
    ).reshape(EXPERTS * CAP, out_width)
    mixture = jnp.einsum(
        "st,sd->td",
        combine,
        returned,
        precision=lax.Precision.HIGHEST,
        preferred_element_type=f32,
    )
    return (residual.astype(f32) + mixture).astype(bf16)


def solution(mesh):
    groups, experts, tensor = (mesh.shape[n] for n in ("groups", "expert", "tensor"))
    fine = Mesh(
        mesh.devices.reshape(groups, experts // NEAR, NEAR, tensor // CORES, CORES),
        ("groups", "far", "near", "x", "core"),
    )
    tok = ("groups", "far", "near")
    in_specs = (
        P(tok, None),
        P(tok, None),
        P(tok, None),
        P(None, ("far", "near", "x", "core")),
        P(None, ("far", "near", "x", "core")),
        P(("far", "near"), ("x", "core")),
    )
    out_specs = P(tok, ("x", "core"))
    return jax.shard_map(layer, mesh=fine, in_specs=in_specs, out_specs=out_specs, check_vma=False)
```

time: 241 us -> 251 us (1.041)
  the two profiles are of different devices: /device:TPU:33 before, /device:TPU:40 now
where the time goes in v6:
time: 251 us; the launch traced here: 250 us
  blocking collectives  85.3 us (34%)
  waiting for transfers between devices  84.8 us (34%)
  starting transfers between devices  63.4 us (25%)
  Pallas kernels  11.4 us (5%)
  local copies, waits for them, and re-layouts  2.94 us (1%)
    all_to_all x1, starting transfers between devices, layer(): arrived = lax.all_to_all(sent, 'far', 0, 0, tiled=True)  43.5 us
    all_to_all x1, blocking collectives, layer(): returned = lax.all_to_all(summed, 'far', 0, 0, tiled=True)  38.7 us
    all_to_all x1, waiting for transfers between devices, layer(): arrived = lax.all_to_all(sent, 'far', 0, 0, tiled=True)  30.4 us
    all_to_all x1, blocking collectives, layer(): lax.all_to_all(produced.reshape(near * CORES, far * PART, out_width), ('n...  24.4 us
    ppermute x3, waiting for transfers between devices, layer(): lax.ppermute(chunk(shift), 'x', [(i, (i + shift) % xs) for i in range(xs)])  22.4 us
    all_gather x1, blocking collectives, layer(): rows = lax.all_gather(arrived, 'near', axis=0, tiled=True)  22.2 us
    all_to_all x1, waiting for transfers between devices, layer(): lax.all_to_all(products(rows, rows_other, chunks), 'x', 0, 0, tiled=True)  19.1 us
    all_to_all x1, waiting for transfers between devices, layer(): units = lax.all_to_all(hidden_units(sums), ('x', 'core'), 0, 0, tiled=True)  12.9 us
  transfers between devices with their start and end apart: 8, of which 6 were waited for; matrix products, arithmetic and copies ran while one was open for 1% of the time, Pallas kernels for 0%

profile of v6, /device:TPU:40, one launch (start us, length us, event | category | flops | bytes accessed | tf_op | source)
XLA Modules:
  0.0 250.1 jit_solution(5661741463408855517)
XLA Ops:
  0.0 2.0 shard_map.64
  2.0 43.5 %all-to-all-start = ((bf16[8,24,512]{2,1,0:T(8,128)(2,1)}), bf16[8,24,512]{2,1,0:T(8,128)(2,1)S(1)}, u32[]{:S(2)}, u32[]{:S(2)}) async-start(bf16[8,24,512]{2,1,0:T(8,128)(2,1)} %get-tuple-element.10), calls=%async_computation | async-start | bytes 393216 | tf_op jit(solution)/shard_map/all_to_all | solution.py:188
  45.4 1.6 dynamic-slice_bitcast_fusion
  47.1 30.4 %all-to-all-done = bf16[8,24,512]{2,1,0:T(8,128)(2,1)S(1)} async-done(((bf16[8,24,512]{2,1,0:T(8,128)(2,1)}), bf16[8,24,512]{2,1,0:T(8,128)(2,1)S(1)}, u32[]{:S(2)}, u32[]{:S(2)}) %all-to-all-start) | async-done | bytes 196640 | tf_op jit(solution)/shard_map/all_to_all | solution.py:188
  77.5 0.1 copy.17
  77.5 0.1 copy.18
  77.7 22.2 %all_gather.3.own = bf16[768,512]{1,0:T(8,128)(2,1)S(1)} all-gather(bf16[192,512]{1,0:T(8,128)(2,1)S(1)} %reshape.22), channel_id=1, replica_groups=mesh['groups'=2,'far'=8,'near'=4,'x'=4,'core'=2] {'near'}, dimensions={0}, use_global_device_ids=true | all-gather | bytes 983040 | tf_op jit(solution)/shard_map/all_gather | solution.py:206
  99.8 1.9 collective-permute-start
  101.8 0.1 pad_maximum_fusion.3
  101.8 3.1 %collective-permute-start.3 = (bf16[2,1024,128]{2,1,0:T(8,128)(2,1)S(1)}, bf16[2,1024,128]{2,1,0:T(8,128)(2,1)S(1)}, u32[]{:S(2)}, u32[]{:S(2)}) collective-permute-start(bf16[2,1024,128]{2,1,0:T(8,128)(2,1)S(1)} %pad_maximum_fusion.3), channel_id=1, source_target_pairs={{0,6},{2,0},{4,2},{6,4},{1,7},{3,1},{5,3},{7,5},{8,14},{10,8},{12,... | collective-permute-start | bytes 1572872 | tf_op jit(solution)/shard_map/ppermute | solution.py:201
  104.9 0.1 pad_maximum_fusion.2
  105.0 2.5 collective-permute-start.2
  107.4 0.1 pad_maximum_fusion.1
  107.5 3.0 %collective-permute-start.1 = (bf16[2,1024,128]{2,1,0:T(8,128)(2,1)S(1)}, bf16[2,1024,128]{2,1,0:T(8,128)(2,1)S(1)}, u32[]{:S(2)}, u32[]{:S(2)}) collective-permute-start(bf16[2,1024,128]{2,1,0:T(8,128)(2,1)S(1)} %pad_maximum_fusion.1), channel_id=1, source_target_pairs={{0,2},{2,4},{4,6},{6,0},{1,3},{3,5},{5,7},{7,1},{8,10},{10,12},{12... | collective-permute-start | bytes 1572872 | tf_op jit(solution)/shard_map/ppermute | solution.py:201
  110.5 0.8 pad_maximum_fusion.refs_0_
  111.3 7.2 %collective-permute-done.3.refs_3_ = bf16[2,1024,128]{2,1,0:T(8,128)(2,1)S(1)} collective-permute-done((bf16[2,1024,128]{2,1,0:T(8,128)(2,1)S(1)}, bf16[2,1024,128]{2,1,0:T(8,128)(2,1)S(1)}, u32[]{:S(2)}, u32[]{:S(2)}) %collective-permute-start.3) | collective-permute-done | bytes 524320 | tf_op jit(solution)/shard_map/ppermute | solution.py:201
  118.5 0.0 copy-start.1
  118.5 4.7 %collective-permute-done.2.refs_2_ = bf16[2,1024,128]{2,1,0:T(8,128)(2,1)S(1)} collective-permute-done((bf16[2,1024,128]{2,1,0:T(8,128)(2,1)S(1)}, bf16[2,1024,128]{2,1,0:T(8,128)(2,1)S(1)}, u32[]{:S(2)}, u32[]{:S(2)}) %collective-permute-start.2) | collective-permute-done | bytes 524320 | tf_op jit(solution)/shard_map/ppermute | solution.py:201
  123.2 0.0 copy-start.2
  123.2 10.4 %collective-permute-done.1.refs_1_ = bf16[2,1024,128]{2,1,0:T(8,128)(2,1)S(1)} collective-permute-done((bf16[2,1024,128]{2,1,0:T(8,128)(2,1)S(1)}, bf16[2,1024,128]{2,1,0:T(8,128)(2,1)S(1)}, u32[]{:S(2)}, u32[]{:S(2)}) %collective-permute-start.1) | collective-permute-done | bytes 524320 | tf_op jit(solution)/shard_map/ppermute | solution.py:201
  133.7 0.0 copy-start.3
  133.7 0.0 collective-permute-done.other
  133.7 0.0 copy-done.1
  133.7 0.0 copy-done.2
  133.7 0.8 copy-done.3
  134.5 6.1 %shard_map.65 = bf16[4,2,768,128]{3,2,1,0:T(8,128)(2,1)} custom-call(bf16[768,512]{1,0:T(8,128)(2,1)S(1)} %all_gather.3.own, bf16[768,512]{1,0:T(8,128)(2,1)S(1)} %collective-permute-done.other, bf16[2,1024,128]{2,1,0:T(8,128)(2,1)} %pad_maximum_fusion.refs_0_, bf16[2,1024,128]{2,1,0:T(8,128)(2,1)} %copy-done.3, bf16[2,1024,128]{2,1,0:T(8,128)(2,1)} %copy-done.2, ...), custom_call_target="tpu_custom_call" | custom-call | tf_op jit(solution)/shard_map/pallas_call | solution.py:120
  140.6 0.0 copy-start
  140.6 3.8 %all-to-all-start.1 = ((bf16[4,2,768,128]{3,2,1,0:T(8,128)(2,1)}), bf16[4,2,768,128]{3,2,1,0:T(8,128)(2,1)S(1)}, u32[]{:S(2)}, u32[]{:S(2)}) async-start(bf16[4,2,768,128]{3,2,1,0:T(8,128)(2,1)} %shard_map.65), calls=%async_computation.1 | async-start | bytes 3145728 | tf_op jit(solution)/shard_map/all_to_all | solution.py:208
  144.4 0.0 copy-done
  144.4 2.0 collective-permute-start.4
  146.4 19.1 %all-to-all-done.1.sums = bf16[4,2,768,128]{3,2,1,0:T(8,128)(2,1)S(1)} async-done(((bf16[4,2,768,128]{3,2,1,0:T(8,128)(2,1)}), bf16[4,2,768,128]{3,2,1,0:T(8,128)(2,1)S(1)}, u32[]{:S(2)}, u32[]{:S(2)}) %all-to-all-start.1) | async-done | bytes 1572896 | tf_op jit(solution)/shard_map/all_to_all | solution.py:208
  165.5 1.2 shard_map.66
  166.6 3.8 %all-to-all-start.2 = ((bf16[8,384,128]{2,1,0:T(8,128)(2,1)}), bf16[8,384,128]{2,1,0:T(8,128)(2,1)S(1)}, u32[]{:S(2)}, u32[]{:S(2)}) async-start(bf16[8,384,128]{2,1,0:T(8,128)(2,1)} %shard_map.66), calls=%async_computation.2 | async-start | bytes 1572864 | tf_op jit(solution)/shard_map/all_to_all | solution.py:209
  170.4 0.0 collective-permute-done.4.other
  170.4 12.9 %all-to-all-done.2.units = bf16[8,384,128]{2,1,0:T(8,128)(2,1)S(1)} async-done(((bf16[8,384,128]{2,1,0:T(8,128)(2,1)}), bf16[8,384,128]{2,1,0:T(8,128)(2,1)S(1)}, u32[]{:S(2)}, u32[]{:S(2)}) %all-to-all-start.2) | async-done | bytes 786464 | tf_op jit(solution)/shard_map/all_to_all | solution.py:209
  183.3 2.2 shard_map.67
  185.5 24.4 %all_to_all.25 = bf16[8,96,512]{2,1,0:T(8,128)(2,1)S(1)} all-to-all(bf16[8,96,512]{2,1,0:T(8,128)(2,1)S(1)} %bitcast.33), channel_id=1, replica_groups=mesh['groups'=2,'far'=8,'near'=4,'x'=4,'core'=2] {'near','core'}, dimensions={0} | all-to-all | bytes 1572864 | tf_op jit(solution)/shard_map/all_to_all | solution.py:211
  209.9 0.2 reduce.1
  210.1 0.2 copy.24
  210.3 0.1 copy.20
  210.3 0.1 copy.21
  210.4 38.7 %all_to_all.26 = bf16[8,24,512]{2,1,0:T(8,128)(2,1)S(1)} all-to-all(bf16[8,24,512]{2,1,0:T(8,128)(2,1)S(1)} %copy.21), channel_id=1, replica_groups=mesh['groups'=2,'far'=8,'near'=4,'x'=4,'core'=2] {'far'}, dimensions={0} | all-to-all | bytes 393216 | tf_op jit(solution)/shard_map/all_to_all | solution.py:218
  249.2 0.9 fusion
  (2 shorter events, 0.1 us)
Async XLA Ops:
  2.0 75.5 %all-to-all-start = ((bf16[8,24,512]{2,1,0:T(8,128)(2,1)}), bf16[8,24,512]{2,1,0:T(8,128)(2,1)S(1)}, u32[]{:S(2)}, u32[]{:S(2)}) async-start(bf16[8,24,512]{2,1,0:T(8,128)(2,1)} %get-tuple-element.10), calls=%async_computation | async-start | bytes 393216 | tf_op jit(solution)/shard_map/all_to_all | solution.py:188
  99.8 33.9 %collective-permute-start = (bf16[768,512]{1,0:T(8,128)(2,1)S(1)}, bf16[768,512]{1,0:T(8,128)(2,1)S(1)}, u32[]{:S(2)}, u32[]{:S(2)}) collective-permute-start(bf16[768,512]{1,0:T(8,128)(2,1)S(1)} %all_gather.3.own), channel_id=1, source_target_pairs={{0,1},{1,0},{2,3},{3,2},{4,5},{5,4},{6,7},{7,6},{8,9},{9,8},{10,11... | collective-permute-start | bytes 2359304 | tf_op jit(solution)/shard_map/ppermute | solution.py:207
  101.8 16.7 %collective-permute-start.3 = (bf16[2,1024,128]{2,1,0:T(8,128)(2,1)S(1)}, bf16[2,1024,128]{2,1,0:T(8,128)(2,1)S(1)}, u32[]{:S(2)}, u32[]{:S(2)}) collective-permute-start(bf16[2,1024,128]{2,1,0:T(8,128)(2,1)S(1)} %pad_maximum_fusion.3), channel_id=1, source_target_pairs={{0,6},{2,0},{4,2},{6,4},{1,7},{3,1},{5,3},{7,5},{8,14},{10,8},{12,... | collective-permute-start | bytes 1572872 | tf_op jit(solution)/shard_map/ppermute | solution.py:201
  105.0 18.3 %collective-permute-start.2 = (bf16[2,1024,128]{2,1,0:T(8,128)(2,1)S(1)}, bf16[2,1024,128]{2,1,0:T(8,128)(2,1)S(1)}, u32[]{:S(2)}, u32[]{:S(2)}) collective-permute-start(bf16[2,1024,128]{2,1,0:T(8,128)(2,1)S(1)} %pad_maximum_fusion.2), channel_id=1, source_target_pairs={{0,4},{2,6},{4,0},{6,2},{1,5},{3,7},{5,1},{7,3},{8,12},{10,14},{12... | collective-permute-start | bytes 1572872 | tf_op jit(solution)/shard_map/ppermute | solution.py:201
  107.5 26.2 %collective-permute-start.1 = (bf16[2,1024,128]{2,1,0:T(8,128)(2,1)S(1)}, bf16[2,1024,128]{2,1,0:T(8,128)(2,1)S(1)}, u32[]{:S(2)}, u32[]{:S(2)}) collective-permute-start(bf16[2,1024,128]{2,1,0:T(8,128)(2,1)S(1)} %pad_maximum_fusion.1), channel_id=1, source_target_pairs={{0,2},{2,4},{4,6},{6,0},{1,3},{3,5},{5,7},{7,1},{8,10},{10,12},{12... | collective-permute-start | bytes 1572872 | tf_op jit(solution)/shard_map/ppermute | solution.py:201
  118.5 15.1 %copy-start.1 = (bf16[2,1024,128]{2,1,0:T(8,128)(2,1)}, bf16[2,1024,128]{2,1,0:T(8,128)(2,1)S(1)}, u32[]{:S(2)}) copy-start(bf16[2,1024,128]{2,1,0:T(8,128)(2,1)S(1)} %collective-permute-done.3.refs_3_) | copy-start | bytes 1572868
  123.2 10.5 %copy-start.2 = (bf16[2,1024,128]{2,1,0:T(8,128)(2,1)}, bf16[2,1024,128]{2,1,0:T(8,128)(2,1)S(1)}, u32[]{:S(2)}) copy-start(bf16[2,1024,128]{2,1,0:T(8,128)(2,1)S(1)} %collective-permute-done.2.refs_2_) | copy-start | bytes 1572868
  133.7 0.8 copy-start.3
  140.6 3.8 %copy-start = (bf16[1024,512]{1,0:T(8,128)(2,1)S(1)}, bf16[1024,512]{1,0:T(8,128)(2,1)}, u32[]{:S(2)}) copy-start(bf16[1024,512]{1,0:T(8,128)(2,1)} %own.1) | copy-start | bytes 3145732
  140.6 24.9 %all-to-all-start.1 = ((bf16[4,2,768,128]{3,2,1,0:T(8,128)(2,1)}), bf16[4,2,768,128]{3,2,1,0:T(8,128)(2,1)S(1)}, u32[]{:S(2)}, u32[]{:S(2)}) async-start(bf16[4,2,768,128]{3,2,1,0:T(8,128)(2,1)} %shard_map.65), calls=%async_computation.1 | async-start | bytes 3145728 | tf_op jit(solution)/shard_map/all_to_all | solution.py:208
  144.4 26.0 %collective-permute-start.4 = (bf16[1024,512]{1,0:T(8,128)(2,1)S(1)}, bf16[1024,512]{1,0:T(8,128)(2,1)}, u32[]{:S(2)}, u32[]{:S(2)}) collective-permute-start(bf16[1024,512]{1,0:T(8,128)(2,1)S(1)} %copy-done), channel_id=1, source_target_pairs={{0,1},{1,0},{2,3},{3,2},{4,5},{5,4},{6,7},{7,6},{8,9},{9,8},{10,11... | collective-permute-start | bytes 3145736 | tf_op jit(solution)/shard_map/ppermute | solution.py:202
  166.6 16.7 %all-to-all-start.2 = ((bf16[8,384,128]{2,1,0:T(8,128)(2,1)}), bf16[8,384,128]{2,1,0:T(8,128)(2,1)S(1)}, u32[]{:S(2)}, u32[]{:S(2)}) async-start(bf16[8,384,128]{2,1,0:T(8,128)(2,1)} %shard_map.66), calls=%async_computation.2 | async-start | bytes 1572864 | tf_op jit(solution)/shard_map/all_to_all | solution.py:209

commit v7 on v4

--- a/solution.py
+++ b/solution.py
@@ -11,7 +11,6 @@
 NEAR = 4
 CORES = 2
 PART = CAP // CORES
-SLOTS = EXPERTS * PART
 
 EPSILON = 1e-05
 
@@ -27,7 +26,17 @@
     return [pltpu.with_memory_space_constraint(array, pltpu.VMEM) for array in arrays]
 
 
-def pack_kernel(tokens, ids, gates, packed, combine, residual):
+def pack_kernel(*refs):
+    sources, (packed, combine, residual), held, sems = refs[:3], refs[3:6], refs[6:9], refs[9]
+    moves = [
+        pltpu.make_async_copy(source, place, sems.at[number])
+        for number, (source, place) in enumerate(zip(sources, held))
+    ]
+    for move in moves:
+        move.start()
+    for move in moves:
+        move.wait()
+    tokens, ids, gates = held
     f32, bf16 = jnp.float32, jnp.bfloat16
     half = packed.shape[2]
     rows = tokens.shape[0]
@@ -35,33 +44,26 @@
     out_width = residual.shape[1]
     floats = tokens[...].astype(f32)
     scale = lax.rsqrt(jnp.mean(floats * floats, axis=1, keepdims=True) + EPSILON)
-    slot = lax.broadcasted_iota(jnp.int32, (SLOTS, rows), 0)
-    expert = sum((slot >= PART * e).astype(jnp.int32) for e in range(1, EXPERTS))
-    wanted = (slot - expert * PART + core * PART).astype(f32)
-    first = ids[0:1, :] == expert
-    second = ids[1:2, :] == expert
     before = jnp.where(
         lax.broadcasted_iota(jnp.int32, (rows, rows), 0)
         < lax.broadcasted_iota(jnp.int32, (rows, rows), 1),
         1.0,
         0.0,
     ).astype(bf16)
-
-    def picked(named, wanted):
-        position = jnp.dot(named.astype(bf16), before, preferred_element_type=f32)
-        return jnp.where(position == wanted, named, 0.0)
-
+    lines = EXPERTS * CAP
+    line = lax.broadcasted_iota(jnp.int32, (lines, rows), 0)
+    expert = sum((line >= CAP * e).astype(jnp.int32) for e in range(1, EXPERTS))
+    at = line - expert * CAP
+    first = ids[0:1, :] == expert
+    second = ids[1:2, :] == expert
+    named = jnp.where(jnp.logical_or(first, second), 1.0, 0.0)
+    position = jnp.dot(named.astype(bf16), before, preferred_element_type=f32)
     gate = jnp.where(first, gates[0:1, :], jnp.where(second, gates[1:2, :], 0.0))
-    named = jnp.where(jnp.logical_or(first, second), 1.0, 0.0)
-    combine[...] = picked(named, wanted) * gate
-    line = lax.broadcasted_iota(jnp.int32, (2 * SLOTS, rows), 0)
-    expert = sum((line >= 2 * PART * e).astype(jnp.int32) for e in range(1, EXPERTS))
-    at = line - expert * (2 * PART)
+    combine[...] = jnp.where(position == at.astype(f32), gate, 0.0)
     upper = (at >= PART).astype(jnp.int32)
     wanted = (at - upper * PART + core * PART).astype(f32)
-    named = jnp.where(jnp.logical_or(ids[0:1, :] == expert, ids[1:2, :] == expert), 1.0, 0.0)
-    picker = picked(named, wanted)
-    total = jnp.zeros((2 * SLOTS, half), f32)
+    picker = jnp.where(position == wanted, named, 0.0)
+    total = jnp.zeros((lines, half), f32)
     for part in range(2):
         start = pl.multiple_of((x * 2 + part) * half, half)
         normed = (tokens[:, pl.ds(start, half)].astype(f32) * scale).astype(bf16)
@@ -71,33 +73,40 @@
     copies = packed.shape[0] // EXPERTS
     for e in range(EXPERTS):
         for copy in range(copies):
-            packed[e * copies + copy] = total[e * 2 * PART : (e + 1) * 2 * PART]
+            packed[e * copies + copy] = total[e * CAP : (e + 1) * CAP]
     start = pl.multiple_of((x * CORES + core) * out_width, out_width)
     residual[...] = tokens[:, pl.ds(start, out_width)]
 
 
 def pack(tokens, ids, gates, far, chip_width, out_width):
     rows = tokens.shape[0]
+    arrays = (tokens, ids.T, gates.T)
     return pl.pallas_call(
         pack_kernel,
         compiler_params=PARAMS,
-        in_specs=[whole()] * 3,
+        in_specs=[whole(pltpu.HBM)] * 3,
         out_specs=[whole()] * 3,
         out_shape=[
-            pltpu.VMEM((far, 2 * PART, chip_width // 2), jnp.bfloat16),
-            pltpu.VMEM((SLOTS, rows), jnp.float32),
+            pltpu.VMEM((far, CAP, chip_width // 2), jnp.bfloat16),
+            pltpu.VMEM((EXPERTS * CAP, rows), jnp.float32),
             pltpu.VMEM((rows, out_width), jnp.bfloat16),
         ],
-    )(tokens, ids.T, gates.T)
-
-
-def product_kernel(rows, own, other, out):
+        scratch_shapes=[pltpu.VMEM(array.shape, array.dtype) for array in arrays]
+        + [pltpu.SemaphoreType.DMA((3,))],
+    )(*[pltpu.with_memory_space_constraint(array, pltpu.HBM) for array in arrays])
+
+
+def product_kernel(rows, own, other, out, held, sem):
     xs, kinds, _, width = own.shape
+    move = pltpu.make_async_copy(other, held, sem)
+    move.start()
     x = lax.axis_index("x")
     left = rows[...]
-    for shift in range(xs):
-        to = lax.rem(x + (xs - shift), xs)
-        for core, weights in enumerate((own, other)):
+    for core, weights in enumerate((own, held)):
+        if core:
+            move.wait()
+        for shift in range(xs):
+            to = lax.rem(x + (xs - shift), xs)
             both = jnp.concatenate([weights[shift, kind] for kind in range(kinds)], axis=1)
             product = jnp.dot(left, both, preferred_element_type=jnp.float32).astype(out.dtype)
             for kind in range(kinds):
@@ -110,10 +119,11 @@
     return pl.pallas_call(
         product_kernel,
         compiler_params=PARAMS,
-        in_specs=[whole()] * 3,
+        in_specs=[whole(), whole(), whole(pltpu.HBM)],
         out_specs=whole(),
         out_shape=pltpu.VMEM((xs, CORES, kinds, n_rows, width), jnp.bfloat16),
-    )(*near_memory(rows, own, other))
+        scratch_shapes=[pltpu.VMEM(other.shape, other.dtype), pltpu.SemaphoreType.DMA],
+    )(*near_memory(rows, own), pltpu.with_memory_space_constraint(other, pltpu.HBM))
 
 
 def hidden_kernel(sums, out):
@@ -146,16 +156,13 @@
 
 
 def down_kernel(units, own, other, out):
-    xs, _, _ = units.shape
-    near, block, _ = out.shape
-    width = own.shape[1]
-    left = jnp.concatenate([units[source] for source in range(xs)], axis=1)
-    for core, weight in enumerate((own, other)):
+    near, _, block, _ = out.shape
+    core = lax.axis_index("core")
+    left = jnp.concatenate([units[source] for source in range(units.shape[0])], axis=1)
+    for side, weight in ((core, own), (1 - core, other)):
         product = jnp.dot(left, weight[...], preferred_element_type=jnp.float32).astype(out.dtype)
         for line in range(near):
-            out[line, :, core * width : (core + 1) * width] = product[
-                line * block : (line + 1) * block
-            ]
+            out[line, side] = product[line * block : (line + 1) * block]
 
 
 def down(units, own, other, near):
@@ -165,7 +172,7 @@
         compiler_params=PARAMS,
         in_specs=[whole()] * 3,
         out_specs=whole(),
-        out_shape=pltpu.VMEM((near, n_rows // near, CORES * own.shape[1]), jnp.bfloat16),
+        out_shape=pltpu.VMEM((near, CORES, n_rows // near, own.shape[1]), jnp.bfloat16),
     )(*near_memory(units, own, other))
 
 
@@ -207,15 +214,17 @@
     sums = lax.all_to_all(partial, "x", 0, 0, tiled=True)
     units = lax.all_to_all(hidden_units(sums), "x", 0, 0, tiled=True)
     produced = down(units, down_weight, down_other, near)
-    parts = lax.all_to_all(produced, "near", 0, 0, tiled=True)
-    summed = jnp.sum(parts.astype(f32), axis=0).astype(bf16)
-    out_lanes = 2 * out_width // 128
-    returned = lax.all_to_all(
-        summed.reshape(far, PART, out_lanes, 128), "far", 0, 0, tiled=True
-    )
+    parts = lax.all_to_all(
+        produced.reshape(near * CORES, far * PART, out_width), ("near", "core"), 0, 0, tiled=True
+    )
+    summed = jnp.sum(
+        parts.reshape(near, CORES, far, PART, out_width).astype(f32), axis=0
+    ).astype(bf16)
+    summed = jnp.swapaxes(summed, 0, 1).reshape(far, CAP, out_width)
+    returned = lax.all_to_all(summed, "far", 0, 0, tiled=True)
     returned = jnp.sum(
-        returned.reshape(EXPERTS, copies, PART, out_lanes, 128).astype(f32), axis=1
-    ).reshape(SLOTS, 2 * out_width)
+        returned.reshape(EXPERTS, copies, CAP, out_width).astype(f32), axis=1
+    ).reshape(EXPERTS * CAP, out_width)
     mixture = jnp.einsum(
         "st,sd->td",
         combine,
@@ -223,7 +232,6 @@
         precision=lax.Precision.HIGHEST,
         preferred_element_type=f32,
     )
-    mixture = mixture[:, :out_width] + lax.ppermute(mixture[:, out_width:], "core", swap)
     return (residual.astype(f32) + mixture).astype(bf16)
 
 

time: 241 us -> 236 us (0.979)
  the two profiles are of different devices: /device:TPU:33 before, /device:TPU:40 now
where the time goes in v7:
time: 236 us
  blocking collectives  140 us (59%)
  waiting for transfers between devices  53.4 us (23%)
  starting transfers between devices  29.7 us (13%)
  Pallas kernels  7.98 us (3%)
  local copies, waits for them, and re-layouts  2.92 us (1%)
    all_to_all x1, blocking collectives, layer(): arrived = lax.all_to_all(sent, 'far', 0, 0, tiled=True)  75.5 us
    all_to_all x1, blocking collectives, layer(): returned = lax.all_to_all(summed, 'far', 0, 0, tiled=True)  38.9 us
    all_to_all x1, blocking collectives, layer(): lax.all_to_all(produced.reshape(near * CORES, far * PART, out_width), ('n...  25.6 us
    all_to_all x1, waiting for transfers between devices, layer(): sums = lax.all_to_all(partial, 'x', 0, 0, tiled=True)  19.1 us
    ppermute x3, waiting for transfers between devices, layer(): lax.ppermute(chunk(shift), 'x', [(i, (i + shift) % xs) for i in range(xs)])  18.5 us
    ppermute x3, starting transfers between devices, layer(): lax.ppermute(chunk(shift), 'x', [(i, (i + shift) % xs) for i in range(xs)])  11.7 us
    all_to_all x1, waiting for transfers between devices, layer(): units = lax.all_to_all(hidden_units(sums), 'x', 0, 0, tiled=True)  11.6 us
    all_to_all x1, starting transfers between devices, layer(): lax.all_to_all(jnp.broadcast_to(arrived, (near, far * PART, chip_width)),...  5.99 us
  transfers between devices with their start and end apart: 8, of which 6 were waited for; matrix products, arithmetic and copies ran while one was open for 0% of the time, Pallas kernels for 1%

profile of v7, /device:TPU:40, one launch (start us, length us, event | category | flops | bytes accessed | tf_op | source)
XLA Modules:
  0.0 235.7 jit_solution(12450523437777821289)
XLA Ops:
  0.0 1.3 shard_map.64
  1.3 0.0 copy-start.2
  1.3 0.0 copy-start.3
  1.3 75.5 %all_to_all.30 = bf16[8,24,512]{2,1,0:T(8,128)(2,1)S(1)} all-to-all(bf16[8,24,512]{2,1,0:T(8,128)(2,1)S(1)} %get-tuple-element.10), channel_id=1, replica_groups=mesh['groups'=2,'far'=8,'near'=4,'x'=4,'core'=2] {'far'}, dimensions={0} | all-to-all | bytes 393216 | tf_op jit(solution)/shard_map/all_to_all | solution.py:189
  76.8 0.1 copy.16
  76.9 0.2 copy.17
  77.1 1.0 broadcast_in_dim.8
  78.1 6.0 %all-to-all-start.1 = ((bf16[4,96,1024]{2,1,0:T(8,128)(2,1)}), bf16[4,96,1024]{2,1,0:T(8,128)(2,1)S(1)}, u32[]{:S(2)}, u32[]{:S(2)}) async-start(bf16[4,96,1024]{2,1,0:T(8,128)(2,1)} %broadcast_in_dim.8), calls=%async_computation.1 | async-start | bytes 1572864 | tf_op jit(solution)/shard_map/all_to_all | solution.py:209
  84.1 0.0 copy-done.2
  84.1 0.0 copy-done.3
  84.1 0.2 dynamic-slice_bitcast_fusion.6
  84.3 0.1 pad_maximum_fusion.1
  84.3 3.6 %collective-permute-start = (bf16[2,1024,128]{2,1,0:T(8,128)(2,1)S(1)}, bf16[2,1024,128]{2,1,0:T(8,128)(2,1)S(1)}, u32[]{:S(2)}, u32[]{:S(2)}) collective-permute-start(bf16[2,1024,128]{2,1,0:T(8,128)(2,1)S(1)} %pad_maximum_fusion.1), channel_id=1, source_target_pairs={{0,2},{2,4},{4,6},{6,0},{1,3},{3,5},{5,7},{7,1},{8,10},{10,12},{12... | collective-permute-start | bytes 1572872 | tf_op jit(solution)/shard_map/ppermute | solution.py:202
  87.9 0.1 pad_maximum_fusion.2
  88.0 4.9 %collective-permute-start.1 = (bf16[2,1024,128]{2,1,0:T(8,128)(2,1)S(1)}, bf16[2,1024,128]{2,1,0:T(8,128)(2,1)S(1)}, u32[]{:S(2)}, u32[]{:S(2)}) collective-permute-start(bf16[2,1024,128]{2,1,0:T(8,128)(2,1)S(1)} %pad_maximum_fusion.2), channel_id=1, source_target_pairs={{0,4},{2,6},{4,0},{6,2},{1,5},{3,7},{5,1},{7,3},{8,12},{10,14},{12... | collective-permute-start | bytes 1572872 | tf_op jit(solution)/shard_map/ppermute | solution.py:202
  92.9 0.1 pad_maximum_fusion.3
  93.0 3.2 %collective-permute-start.2 = (bf16[2,1024,128]{2,1,0:T(8,128)(2,1)S(1)}, bf16[2,1024,128]{2,1,0:T(8,128)(2,1)S(1)}, u32[]{:S(2)}, u32[]{:S(2)}) collective-permute-start(bf16[2,1024,128]{2,1,0:T(8,128)(2,1)S(1)} %pad_maximum_fusion.3), channel_id=1, source_target_pairs={{0,6},{2,0},{4,2},{6,4},{1,7},{3,1},{5,3},{7,5},{8,14},{10,8},{12,... | collective-permute-start | bytes 1572872 | tf_op jit(solution)/shard_map/ppermute | solution.py:202
  96.2 0.1 maximum_bitcast_fusion
  96.2 5.1 %collective-permute-done = bf16[2,1024,128]{2,1,0:T(8,128)(2,1)S(1)} collective-permute-done((bf16[2,1024,128]{2,1,0:T(8,128)(2,1)S(1)}, bf16[2,1024,128]{2,1,0:T(8,128)(2,1)S(1)}, u32[]{:S(2)}, u32[]{:S(2)}) %collective-permute-start) | collective-permute-done | bytes 524320 | tf_op jit(solution)/shard_map/ppermute | solution.py:202
  101.3 11.9 %collective-permute-done.1 = bf16[2,1024,128]{2,1,0:T(8,128)(2,1)S(1)} collective-permute-done((bf16[2,1024,128]{2,1,0:T(8,128)(2,1)S(1)}, bf16[2,1024,128]{2,1,0:T(8,128)(2,1)S(1)}, u32[]{:S(2)}, u32[]{:S(2)}) %collective-permute-start.1) | collective-permute-done | bytes 524320 | tf_op jit(solution)/shard_map/ppermute | solution.py:202
  113.2 1.5 collective-permute-done.2
  114.7 0.3 pad_maximum_fusion.own
  115.0 2.0 collective-permute-start.3
  116.9 4.3 %collective-permute-done.3.other = bf16[4,2,1024,128]{3,2,1,0:T(8,128)(2,1)} collective-permute-done((bf16[4,2,1024,128]{3,2,1,0:T(8,128)(2,1)S(1)}, bf16[4,2,1024,128]{3,2,1,0:T(8,128)(2,1)}, u32[]{:S(2)}, u32[]{:S(2)}) %collective-permute-start.3) | collective-permute-done | bytes 2097184 | tf_op jit(solution)/shard_map/ppermute | solution.py:204
  121.2 0.0 all-to-all-done.1
  121.2 3.3 %shard_map.65 = bf16[4,2,2,384,128]{4,3,2,1,0:T(8,128)(2,1)S(1)} custom-call(bf16[384,1024]{1,0:T(8,128)(2,1)S(1)} %bitcast.42, bf16[4,2,1024,128]{3,2,1,0:T(8,128)(2,1)S(1)} %pad_maximum_fusion.own, bf16[4,2,1024,128]{3,2,1,0:T(8,128)(2,1)} %collective-permute-done.3.other), custom_call_target="tpu_custom_call" | custom-call | tf_op jit(solution)/shard_map/pallas_call | solution.py:119
  124.5 0.0 copy-start
  124.5 1.1 copy-done
  125.6 0.0 copy-start.1
  125.6 4.5 %all-to-all-start.2 = ((bf16[4,2,2,384,128]{4,3,2,1,0:T(8,128)(2,1)}), bf16[4,2,2,384,128]{4,3,2,1,0:T(8,128)(2,1)S(1)}, u32[]{:S(2)}, u32[]{:S(2)}) async-start(bf16[4,2,2,384,128]{4,3,2,1,0:T(8,128)(2,1)} %copy-done), calls=%async_computation.2 | async-start | bytes 3145728 | tf_op jit(solution)/shard_map/all_to_all | solution.py:214
  130.1 0.0 copy-done.1
  130.1 1.9 collective-permute-start.4
  132.1 19.1 %all-to-all-done.2.sums = bf16[4,2,2,384,128]{4,3,2,1,0:T(8,128)(2,1)S(1)} async-done(((bf16[4,2,2,384,128]{4,3,2,1,0:T(8,128)(2,1)}), bf16[4,2,2,384,128]{4,3,2,1,0:T(8,128)(2,1)S(1)}, u32[]{:S(2)}, u32[]{:S(2)}) %all-to-all-start.2) | async-done | bytes 1572896 | tf_op jit(solution)/shard_map/all_to_all | solution.py:214
  151.1 1.2 shard_map.66
  152.3 3.6 %all-to-all-start.3 = ((bf16[4,384,256]{2,1,0:T(8,128)(2,1)}), bf16[4,384,256]{2,1,0:T(8,128)(2,1)S(1)}, u32[]{:S(2)}, u32[]{:S(2)}) async-start(bf16[4,384,256]{2,1,0:T(8,128)(2,1)} %shard_map.66), calls=%async_computation.3 | async-start | bytes 1572864 | tf_op jit(solution)/shard_map/all_to_all | solution.py:215
  155.9 0.0 collective-permute-done.4.other
  155.9 11.6 %all-to-all-done.3.units = bf16[4,384,256]{2,1,0:T(8,128)(2,1)S(1)} async-done(((bf16[4,384,256]{2,1,0:T(8,128)(2,1)}), bf16[4,384,256]{2,1,0:T(8,128)(2,1)S(1)}, u32[]{:S(2)}, u32[]{:S(2)}) %all-to-all-start.3) | async-done | bytes 786464 | tf_op jit(solution)/shard_map/all_to_all | solution.py:215
  167.6 2.2 shard_map.67
  169.8 25.6 %all_to_all.31 = bf16[8,96,512]{2,1,0:T(8,128)(2,1)S(1)} all-to-all(bf16[8,96,512]{2,1,0:T(8,128)(2,1)S(1)} %bitcast.43), channel_id=1, replica_groups=mesh['groups'=2,'far'=8,'near'=4,'x'=4,'core'=2] {'near','core'}, dimensions={0} | all-to-all | bytes 1572864 | tf_op jit(solution)/shard_map/all_to_all | solution.py:217
  195.3 0.2 reduce.1
  195.5 0.2 copy.23
  195.7 0.1 copy.19
  195.8 0.1 copy.20
  195.8 38.9 %all_to_all.32 = bf16[8,24,512]{2,1,0:T(8,128)(2,1)S(1)} all-to-all(bf16[8,24,512]{2,1,0:T(8,128)(2,1)S(1)} %copy.20), channel_id=1, replica_groups=mesh['groups'=2,'far'=8,'near'=4,'x'=4,'core'=2] {'far'}, dimensions={0} | all-to-all | bytes 393216 | tf_op jit(solution)/shard_map/all_to_all | solution.py:224
  234.8 0.9 fusion
  (2 shorter events, 0.0 us)
Async XLA Ops:
  1.3 82.8 %copy-start.2 = (bf16[4096,128]{1,0:T(8,128)(2,1)S(1)}, bf16[4096,128]{1,0:T(8,128)(2,1)}, u32[]{:S(2)}) copy-start(bf16[4096,128]{1,0:T(8,128)(2,1)} %param.10) | copy-start | bytes 3145732
  1.3 82.8 %copy-start.3 = (bf16[4096,128]{1,0:T(8,128)(2,1)S(1)}, bf16[4096,128]{1,0:T(8,128)(2,1)}, u32[]{:S(2)}) copy-start(bf16[4096,128]{1,0:T(8,128)(2,1)} %param.9) | copy-start | bytes 3145732
  78.1 43.1 %all-to-all-start.1 = ((bf16[4,96,1024]{2,1,0:T(8,128)(2,1)}), bf16[4,96,1024]{2,1,0:T(8,128)(2,1)S(1)}, u32[]{:S(2)}, u32[]{:S(2)}) async-start(bf16[4,96,1024]{2,1,0:T(8,128)(2,1)} %broadcast_in_dim.8), calls=%async_computation.1 | async-start | bytes 1572864 | tf_op jit(solution)/shard_map/all_to_all | solution.py:209
  84.3 17.0 %collective-permute-start = (bf16[2,1024,128]{2,1,0:T(8,128)(2,1)S(1)}, bf16[2,1024,128]{2,1,0:T(8,128)(2,1)S(1)}, u32[]{:S(2)}, u32[]{:S(2)}) collective-permute-start(bf16[2,1024,128]{2,1,0:T(8,128)(2,1)S(1)} %pad_maximum_fusion.1), channel_id=1, source_target_pairs={{0,2},{2,4},{4,6},{6,0},{1,3},{3,5},{5,7},{7,1},{8,10},{10,12},{12... | collective-permute-start | bytes 1572872 | tf_op jit(solution)/shard_map/ppermute | solution.py:202
  88.0 25.3 %collective-permute-start.1 = (bf16[2,1024,128]{2,1,0:T(8,128)(2,1)S(1)}, bf16[2,1024,128]{2,1,0:T(8,128)(2,1)S(1)}, u32[]{:S(2)}, u32[]{:S(2)}) collective-permute-start(bf16[2,1024,128]{2,1,0:T(8,128)(2,1)S(1)} %pad_maximum_fusion.2), channel_id=1, source_target_pairs={{0,4},{2,6},{4,0},{6,2},{1,5},{3,7},{5,1},{7,3},{8,12},{10,14},{12... | collective-permute-start | bytes 1572872 | tf_op jit(solution)/shard_map/ppermute | solution.py:202
  93.0 21.7 %collective-permute-start.2 = (bf16[2,1024,128]{2,1,0:T(8,128)(2,1)S(1)}, bf16[2,1024,128]{2,1,0:T(8,128)(2,1)S(1)}, u32[]{:S(2)}, u32[]{:S(2)}) collective-permute-start(bf16[2,1024,128]{2,1,0:T(8,128)(2,1)S(1)} %pad_maximum_fusion.3), channel_id=1, source_target_pairs={{0,6},{2,0},{4,2},{6,4},{1,7},{3,1},{5,3},{7,5},{8,14},{10,8},{12,... | collective-permute-start | bytes 1572872 | tf_op jit(solution)/shard_map/ppermute | solution.py:202
  115.0 6.2 %collective-permute-start.3 = (bf16[4,2,1024,128]{3,2,1,0:T(8,128)(2,1)S(1)}, bf16[4,2,1024,128]{3,2,1,0:T(8,128)(2,1)}, u32[]{:S(2)}, u32[]{:S(2)}) collective-permute-start(bf16[4,2,1024,128]{3,2,1,0:T(8,128)(2,1)S(1)} %pad_maximum_fusion.own), channel_id=1, source_target_pairs={{0,1},{1,0},{2,3},{3,2},{4,5},{5,4},{6,7},{7,6},{8,9},{9,8},{10,11... | collective-permute-start | bytes 6291464 | tf_op jit(solution)/shard_map/ppermute | solution.py:204
  124.5 1.2 copy-start
  125.6 4.5 %copy-start.1 = (bf16[1024,512]{1,0:T(8,128)(2,1)S(1)}, bf16[1024,512]{1,0:T(8,128)(2,1)}, u32[]{:S(2)}) copy-start(bf16[1024,512]{1,0:T(8,128)(2,1)} %own.1) | copy-start | bytes 3145732
  125.6 25.5 %all-to-all-start.2 = ((bf16[4,2,2,384,128]{4,3,2,1,0:T(8,128)(2,1)}), bf16[4,2,2,384,128]{4,3,2,1,0:T(8,128)(2,1)S(1)}, u32[]{:S(2)}, u32[]{:S(2)}) async-start(bf16[4,2,2,384,128]{4,3,2,1,0:T(8,128)(2,1)} %copy-done), calls=%async_computation.2 | async-start | bytes 3145728 | tf_op jit(solution)/shard_map/all_to_all | solution.py:214
  130.1 25.8 %collective-permute-start.4 = (bf16[1024,512]{1,0:T(8,128)(2,1)S(1)}, bf16[1024,512]{1,0:T(8,128)(2,1)}, u32[]{:S(2)}, u32[]{:S(2)}) collective-permute-start(bf16[1024,512]{1,0:T(8,128)(2,1)S(1)} %copy-done.1), channel_id=1, source_target_pairs={{0,1},{1,0},{2,3},{3,2},{4,5},{5,4},{6,7},{7,6},{8,9},{9,8},{10,11... | collective-permute-start | bytes 3145736 | tf_op jit(solution)/shard_map/ppermute | solution.py:205
  152.3 15.2 %all-to-all-start.3 = ((bf16[4,384,256]{2,1,0:T(8,128)(2,1)}), bf16[4,384,256]{2,1,0:T(8,128)(2,1)S(1)}, u32[]{:S(2)}, u32[]{:S(2)}) async-start(bf16[4,384,256]{2,1,0:T(8,128)(2,1)} %shard_map.66), calls=%async_computation.3 | async-start | bytes 1572864 | tf_op jit(solution)/shard_map/all_to_all | solution.py:215

commit v8 on v7

--- a/solution.py
+++ b/solution.py
@@ -8,7 +8,7 @@
 
 EXPERTS = 4
 CAP = 24
-NEAR = 4
+NEAR = 8
 CORES = 2
 PART = CAP // CORES
 
@@ -98,14 +98,18 @@
 
 def product_kernel(rows, own, other, out, held, sem):
     xs, kinds, _, width = own.shape
-    move = pltpu.make_async_copy(other, held, sem)
-    move.start()
+    moves = [
+        pltpu.make_async_copy(other.at[shift], held.at[shift], sem.at[shift])
+        for shift in range(xs)
+    ]
+    for move in moves:
+        move.start()
     x = lax.axis_index("x")
     left = rows[...]
     for core, weights in enumerate((own, held)):
-        if core:
-            move.wait()
         for shift in range(xs):
+            if core:
+                moves[shift].wait()
             to = lax.rem(x + (xs - shift), xs)
             both = jnp.concatenate([weights[shift, kind] for kind in range(kinds)], axis=1)
             product = jnp.dot(left, both, preferred_element_type=jnp.float32).astype(out.dtype)
@@ -122,11 +126,18 @@
         in_specs=[whole(), whole(), whole(pltpu.HBM)],
         out_specs=whole(),
         out_shape=pltpu.VMEM((xs, CORES, kinds, n_rows, width), jnp.bfloat16),
-        scratch_shapes=[pltpu.VMEM(other.shape, other.dtype), pltpu.SemaphoreType.DMA],
+        scratch_shapes=[pltpu.VMEM(other.shape, other.dtype), pltpu.SemaphoreType.DMA((xs,))],
     )(*near_memory(rows, own), pltpu.with_memory_space_constraint(other, pltpu.HBM))
 
 
-def hidden_kernel(sums, out):
+def hidden_kernel(sums, *refs):
+    sources, out, places, sems = refs[:CORES], refs[CORES], refs[CORES + 1 : -1], refs[-1]
+    moves = [
+        pltpu.make_async_copy(source, place, sems.at[number])
+        for number, (source, place) in enumerate(zip(sources, places))
+    ]
+    for move in moves:
+        move.start()
     f32 = jnp.float32
     xs, _, _, n_rows, width = sums.shape
     straight = lax.axis_index("core") == 0
@@ -142,17 +153,22 @@
         for copy in range(out.shape[0]):
             out[copy, at : at + block, 0:width] = low
             out[copy, at : at + block, width : 2 * width] = high
-
-
-def hidden_units(sums):
+    for move in moves:
+        move.wait()
+
+
+def hidden_units(sums, *weights):
     xs, cores, _, n_rows, width = sums.shape
+    far_weights = [pltpu.with_memory_space_constraint(weight, pltpu.HBM) for weight in weights]
     return pl.pallas_call(
         hidden_kernel,
         compiler_params=PARAMS,
-        in_specs=[whole()],
-        out_specs=whole(),
-        out_shape=pltpu.VMEM((xs, n_rows, cores * width), jnp.bfloat16),
-    )(*near_memory(sums))
+        in_specs=[whole()] + [whole(pltpu.HBM)] * CORES,
+        out_specs=[whole()] * (1 + CORES),
+        out_shape=[pltpu.VMEM((xs, n_rows, cores * width), jnp.bfloat16)]
+        + [pltpu.VMEM(weight.shape, weight.dtype) for weight in weights],
+        scratch_shapes=[pltpu.SemaphoreType.DMA((CORES,))],
+    )(*near_memory(sums), *far_weights)
 
 
 def down_kernel(units, own, other, out):
@@ -210,9 +226,11 @@
         jnp.broadcast_to(arrived, (near, far * PART, chip_width)), "near", 0, 0, tiled=True
     )
     n_rows = near * far * PART
+    rows, down_other = lax.optimization_barrier((rows, down_other))
     partial = products(rows.reshape(n_rows, chip_width), own, other)
     sums = lax.all_to_all(partial, "x", 0, 0, tiled=True)
-    units = lax.all_to_all(hidden_units(sums), "x", 0, 0, tiled=True)
+    hidden, down_weight, down_other = hidden_units(sums, down_weight, down_other)
+    units = lax.all_to_all(hidden, "x", 0, 0, tiled=True)
     produced = down(units, down_weight, down_other, near)
     parts = lax.all_to_all(
         produced.reshape(near * CORES, far * PART, out_width), ("near", "core"), 0, 0, tiled=True

time: 236 us -> 245 us (1.038)
  the two profiles are of different devices: /device:TPU:40 before, /device:TPU:33 now
where the time goes in v8:
time: 245 us; the launch traced here: 243 us
  blocking collectives  182 us (74%)
  starting transfers between devices  28.2 us (12%)
  waiting for transfers between devices  21.3 us (9%)
  Pallas kernels  7.99 us (3%)
    all_to_all x1, blocking collectives, layer(): arrived = lax.all_to_all(sent, 'far', 0, 0, tiled=True)  65.7 us
    all_to_all x1, blocking collectives, layer(): lax.all_to_all(produced.reshape(near * CORES, far * PART, out_width), ('n...  57.5 us
    all_to_all x1, blocking collectives, layer(): returned = lax.all_to_all(summed, 'far', 0, 0, tiled=True)  28.6 us
    all_to_all x1, blocking collectives, layer(): sums = lax.all_to_all(partial, 'x', 0, 0, tiled=True)  19.9 us
    ppermute x3, waiting for transfers between devices, layer(): lax.ppermute(chunk(shift), 'x', [(i, (i + shift) % xs) for i in range(xs)])  17.9 us
    all_to_all x1, starting transfers between devices, layer(): lax.all_to_all(jnp.broadcast_to(arrived, (near, far * PART, chip_width)),...  12.7 us
    all_to_all x1, blocking collectives, layer(): units = lax.all_to_all(hidden, 'x', 0, 0, tiled=True)  10.8 us
    ppermute x3, starting transfers between devices, layer(): lax.ppermute(chunk(shift), 'x', [(i, (i + shift) % xs) for i in range(xs)])  10.3 us
  transfers between devices with their start and end apart: 6, of which 4 were waited for; matrix products, arithmetic and copies ran while one was open for 0% of the time, Pallas kernels for 0%

profile of v8, /device:TPU:33, one launch (start us, length us, event | category | flops | bytes accessed | tf_op | source)
XLA Modules:
  0.0 243.1 jit_solution(8226537984017489100)
XLA Ops:
  0.0 0.0 copy-start.1
  0.0 0.0 copy-start.2
  0.0 1.5 shard_map.64
  1.5 65.7 %all_to_all.30 = bf16[4,24,512]{2,1,0:T(8,128)(2,1)S(1)} all-to-all(bf16[4,24,512]{2,1,0:T(8,128)(2,1)S(1)} %get-tuple-element.15), channel_id=1, replica_groups=mesh['groups'=2,'far'=4,'near'=8,'x'=4,'core'=2] {'far'}, dimensions={0} | all-to-all | bytes 196608 | tf_op jit(solution)/shard_map/all_to_all | solution.py:205
  67.1 0.1 copy.14
  67.2 0.1 copy.15
  67.3 1.0 broadcast_in_dim.8
  68.3 12.7 %all-to-all-start.1 = ((bf16[8,48,1024]{2,1,0:T(8,128)(2,1)}), bf16[8,48,1024]{2,1,0:T(8,128)(2,1)S(1)}, u32[]{:S(2)}, u32[]{:S(2)}) async-start(bf16[8,48,1024]{2,1,0:T(8,128)(2,1)} %broadcast_in_dim.8), calls=%async_computation.1 | async-start | bytes 1572864 | tf_op jit(solution)/shard_map/all_to_all | solution.py:225
  81.0 0.0 copy-done.1
  81.0 0.0 copy-done.2
  81.0 0.2 dynamic-slice_bitcast_fusion.6
  81.2 0.1 pad_maximum_fusion.2
  81.3 5.0 %collective-permute-start.2 = (bf16[2,1024,128]{2,1,0:T(8,128)(2,1)S(1)}, bf16[2,1024,128]{2,1,0:T(8,128)(2,1)S(1)}, u32[]{:S(2)}, u32[]{:S(2)}) collective-permute-start(bf16[2,1024,128]{2,1,0:T(8,128)(2,1)S(1)} %pad_maximum_fusion.2), channel_id=1, source_target_pairs={{0,4},{2,6},{4,0},{6,2},{1,5},{3,7},{5,1},{7,3},{8,12},{10,14},{12... | collective-permute-start | bytes 1572872 | tf_op jit(solution)/shard_map/ppermute | solution.py:218
  86.2 0.1 pad_maximum_fusion.3
  86.3 2.6 %collective-permute-start.3 = (bf16[2,1024,128]{2,1,0:T(8,128)(2,1)S(1)}, bf16[2,1024,128]{2,1,0:T(8,128)(2,1)S(1)}, u32[]{:S(2)}, u32[]{:S(2)}) collective-permute-start(bf16[2,1024,128]{2,1,0:T(8,128)(2,1)S(1)} %pad_maximum_fusion.3), channel_id=1, source_target_pairs={{0,6},{2,0},{4,2},{6,4},{1,7},{3,1},{5,3},{7,5},{8,14},{10,8},{12,... | collective-permute-start | bytes 1572872 | tf_op jit(solution)/shard_map/ppermute | solution.py:218
  88.9 0.1 pad_maximum_fusion.1
  89.0 2.7 %collective-permute-start.1 = (bf16[2,1024,128]{2,1,0:T(8,128)(2,1)S(1)}, bf16[2,1024,128]{2,1,0:T(8,128)(2,1)S(1)}, u32[]{:S(2)}, u32[]{:S(2)}) collective-permute-start(bf16[2,1024,128]{2,1,0:T(8,128)(2,1)S(1)} %pad_maximum_fusion.1), channel_id=1, source_target_pairs={{0,2},{2,4},{4,6},{6,0},{1,3},{3,5},{5,7},{7,1},{8,10},{10,12},{12... | collective-permute-start | bytes 1572872 | tf_op jit(solution)/shard_map/ppermute | solution.py:218
  91.7 0.1 maximum_bitcast_fusion
  91.8 5.0 %collective-permute-done.2 = bf16[2,1024,128]{2,1,0:T(8,128)(2,1)S(1)} collective-permute-done((bf16[2,1024,128]{2,1,0:T(8,128)(2,1)S(1)}, bf16[2,1024,128]{2,1,0:T(8,128)(2,1)S(1)}, u32[]{:S(2)}, u32[]{:S(2)}) %collective-permute-start.2) | collective-permute-done | bytes 524320 | tf_op jit(solution)/shard_map/ppermute | solution.py:218
  96.8 12.5 %collective-permute-done.3 = bf16[2,1024,128]{2,1,0:T(8,128)(2,1)S(1)} collective-permute-done((bf16[2,1024,128]{2,1,0:T(8,128)(2,1)S(1)}, bf16[2,1024,128]{2,1,0:T(8,128)(2,1)S(1)}, u32[]{:S(2)}, u32[]{:S(2)}) %collective-permute-start.3) | collective-permute-done | bytes 524320 | tf_op jit(solution)/shard_map/ppermute | solution.py:218
  109.2 0.4 collective-permute-done.1
  109.7 0.0 copy-start
  109.7 0.3 pad_maximum_fusion.own
  109.9 3.2 %collective-permute-start.4 = (bf16[4,2,1024,128]{3,2,1,0:T(8,128)(2,1)S(1)}, bf16[4,2,1024,128]{3,2,1,0:T(8,128)(2,1)}, u32[]{:S(2)}, u32[]{:S(2)}) collective-permute-start(bf16[4,2,1024,128]{3,2,1,0:T(8,128)(2,1)S(1)} %pad_maximum_fusion.own), channel_id=1, source_target_pairs={{0,1},{1,0},{2,3},{3,2},{4,5},{5,4},{6,7},{7,6},{8,9},{9,8},{10,11... | collective-permute-start | bytes 6291464 | tf_op jit(solution)/shard_map/ppermute | solution.py:220
  113.1 0.0 copy-done
  113.1 2.0 collective-permute-start
  115.1 3.4 %collective-permute-done.refs_1_ = bf16[1024,512]{1,0:T(8,128)(2,1)} collective-permute-done((bf16[1024,512]{1,0:T(8,128)(2,1)S(1)}, bf16[1024,512]{1,0:T(8,128)(2,1)}, u32[]{:S(2)}, u32[]{:S(2)}) %collective-permute-start) | collective-permute-done | bytes 1048608 | tf_op jit(solution)/shard_map/ppermute | solution.py:221
  118.5 0.0 all-to-all-done.1
  118.5 0.0 collective-permute-done.4.other
  118.5 4.0 %shard_map.65 = bf16[4,2,2,384,128]{4,3,2,1,0:T(8,128)(2,1)S(1)} custom-call(bf16[384,1024]{1,0:T(8,128)(2,1)S(1)} %bitcast.39, bf16[4,2,1024,128]{3,2,1,0:T(8,128)(2,1)S(1)} %pad_maximum_fusion.own, bf16[4,2,1024,128]{3,2,1,0:T(8,128)(2,1)} %collective-permute-done.4.other), custom_call_target="tpu_custom_call" | custom-call | tf_op jit(solution)/shard_map/pallas_call | solution.py:123
  122.5 19.9 %all_to_all.31.sums = bf16[4,2,2,384,128]{4,3,2,1,0:T(8,128)(2,1)S(1)} all-to-all(bf16[4,2,2,384,128]{4,3,2,1,0:T(8,128)(2,1)S(1)} %shard_map.65), channel_id=1, replica_groups=mesh['groups'=2,'far'=4,'near'=8,'x'=4,'core'=2] {'x'}, dimensions={0} | all-to-all | bytes 3145728 | tf_op jit(solution)/shard_map/all_to_all | solution.py:231
  142.5 1.6 shard_map.66
  144.0 10.8 %all_to_all.32.units = bf16[4,384,256]{2,1,0:T(8,128)(2,1)S(1)} all-to-all(bf16[4,384,256]{2,1,0:T(8,128)(2,1)S(1)} %get-tuple-element.18), channel_id=1, replica_groups=mesh['groups'=2,'far'=4,'near'=8,'x'=4,'core'=2] {'x'}, dimensions={0} | all-to-all | bytes 1572864 | tf_op jit(solution)/shard_map/all_to_all | solution.py:233
  154.8 1.0 shard_map.67
  155.8 57.5 %all_to_all.33 = bf16[16,48,512]{2,1,0:T(8,128)(2,1)S(1)} all-to-all(bf16[16,48,512]{2,1,0:T(8,128)(2,1)S(1)} %bitcast.40), channel_id=1, replica_groups=mesh['groups'=2,'far'=4,'near'=8,'x'=4,'core'=2] {'near','core'}, dimensions={0} | all-to-all | bytes 1572864 | tf_op jit(solution)/shard_map/all_to_all | solution.py:235
  213.3 0.1 reduce.1
  213.4 0.1 copy.19
  213.5 0.1 copy.17
  213.6 28.6 %all_to_all.34 = bf16[4,24,512]{2,1,0:T(8,128)(2,1)S(1)} all-to-all(bf16[4,24,512]{2,1,0:T(8,128)(2,1)S(1)} %copy.18), channel_id=1, replica_groups=mesh['groups'=2,'far'=4,'near'=8,'x'=4,'core'=2] {'far'}, dimensions={0} | all-to-all | bytes 196608 | tf_op jit(solution)/shard_map/all_to_all | solution.py:242
  242.2 0.8 fusion
  (2 shorter events, 0.0 us)
Async XLA Ops:
  0.0 81.0 %copy-start.1 = (bf16[4096,128]{1,0:T(8,128)(2,1)S(1)}, bf16[4096,128]{1,0:T(8,128)(2,1)}, u32[]{:S(2)}) copy-start(bf16[4096,128]{1,0:T(8,128)(2,1)} %param.10) | copy-start | bytes 3145732
  0.0 81.0 %copy-start.2 = (bf16[4096,128]{1,0:T(8,128)(2,1)S(1)}, bf16[4096,128]{1,0:T(8,128)(2,1)}, u32[]{:S(2)}) copy-start(bf16[4096,128]{1,0:T(8,128)(2,1)} %param.9) | copy-start | bytes 3145732
  68.3 50.2 %all-to-all-start.1 = ((bf16[8,48,1024]{2,1,0:T(8,128)(2,1)}), bf16[8,48,1024]{2,1,0:T(8,128)(2,1)S(1)}, u32[]{:S(2)}, u32[]{:S(2)}) async-start(bf16[8,48,1024]{2,1,0:T(8,128)(2,1)} %broadcast_in_dim.8), calls=%async_computation.1 | async-start | bytes 1572864 | tf_op jit(solution)/shard_map/all_to_all | solution.py:225
  81.3 15.5 %collective-permute-start.2 = (bf16[2,1024,128]{2,1,0:T(8,128)(2,1)S(1)}, bf16[2,1024,128]{2,1,0:T(8,128)(2,1)S(1)}, u32[]{:S(2)}, u32[]{:S(2)}) collective-permute-start(bf16[2,1024,128]{2,1,0:T(8,128)(2,1)S(1)} %pad_maximum_fusion.2), channel_id=1, source_target_pairs={{0,4},{2,6},{4,0},{6,2},{1,5},{3,7},{5,1},{7,3},{8,12},{10,14},{12... | collective-permute-start | bytes 1572872 | tf_op jit(solution)/shard_map/ppermute | solution.py:218
  86.3 22.9 %collective-permute-start.3 = (bf16[2,1024,128]{2,1,0:T(8,128)(2,1)S(1)}, bf16[2,1024,128]{2,1,0:T(8,128)(2,1)S(1)}, u32[]{:S(2)}, u32[]{:S(2)}) collective-permute-start(bf16[2,1024,128]{2,1,0:T(8,128)(2,1)S(1)} %pad_maximum_fusion.3), channel_id=1, source_target_pairs={{0,6},{2,0},{4,2},{6,4},{1,7},{3,1},{5,3},{7,5},{8,14},{10,8},{12,... | collective-permute-start | bytes 1572872 | tf_op jit(solution)/shard_map/ppermute | solution.py:218
  89.0 20.7 %collective-permute-start.1 = (bf16[2,1024,128]{2,1,0:T(8,128)(2,1)S(1)}, bf16[2,1024,128]{2,1,0:T(8,128)(2,1)S(1)}, u32[]{:S(2)}, u32[]{:S(2)}) collective-permute-start(bf16[2,1024,128]{2,1,0:T(8,128)(2,1)S(1)} %pad_maximum_fusion.1), channel_id=1, source_target_pairs={{0,2},{2,4},{4,6},{6,0},{1,3},{3,5},{5,7},{7,1},{8,10},{10,12},{12... | collective-permute-start | bytes 1572872 | tf_op jit(solution)/shard_map/ppermute | solution.py:218
  109.7 3.5 %copy-start = (bf16[1024,512]{1,0:T(8,128)(2,1)S(1)}, bf16[1024,512]{1,0:T(8,128)(2,1)}, u32[]{:S(2)}) copy-start(bf16[1024,512]{1,0:T(8,128)(2,1)} %refs_0_.3) | copy-start | bytes 3145732
  109.9 8.6 %collective-permute-start.4 = (bf16[4,2,1024,128]{3,2,1,0:T(8,128)(2,1)S(1)}, bf16[4,2,1024,128]{3,2,1,0:T(8,128)(2,1)}, u32[]{:S(2)}, u32[]{:S(2)}) collective-permute-start(bf16[4,2,1024,128]{3,2,1,0:T(8,128)(2,1)S(1)} %pad_maximum_fusion.own), channel_id=1, source_target_pairs={{0,1},{1,0},{2,3},{3,2},{4,5},{5,4},{6,7},{7,6},{8,9},{9,8},{10,11... | collective-permute-start | bytes 6291464 | tf_op jit(solution)/shard_map/ppermute | solution.py:220
  113.1 5.4 %collective-permute-start = (bf16[1024,512]{1,0:T(8,128)(2,1)S(1)}, bf16[1024,512]{1,0:T(8,128)(2,1)}, u32[]{:S(2)}, u32[]{:S(2)}) collective-permute-start(bf16[1024,512]{1,0:T(8,128)(2,1)S(1)} %copy-done), channel_id=1, source_target_pairs={{0,1},{1,0},{2,3},{3,2},{4,5},{5,4},{6,7},{7,6},{8,9},{9,8},{10,11... | collective-permute-start | bytes 3145736 | tf_op jit(solution)/shard_map/ppermute | solution.py:221

commit v9 on v5

--- a/solution.py
+++ b/solution.py
@@ -11,7 +11,6 @@
 NEAR = 4
 CORES = 2
 PART = CAP // CORES
-SLOTS = EXPERTS * PART
 
 EPSILON = 1e-05
 
@@ -45,33 +44,26 @@
     out_width = residual.shape[1]
     floats = tokens[...].astype(f32)
     scale = lax.rsqrt(jnp.mean(floats * floats, axis=1, keepdims=True) + EPSILON)
-    slot = lax.broadcasted_iota(jnp.int32, (SLOTS, rows), 0)
-    expert = sum((slot >= PART * e).astype(jnp.int32) for e in range(1, EXPERTS))
-    wanted = (slot - expert * PART + core * PART).astype(f32)
-    first = ids[0:1, :] == expert
-    second = ids[1:2, :] == expert
     before = jnp.where(
         lax.broadcasted_iota(jnp.int32, (rows, rows), 0)
         < lax.broadcasted_iota(jnp.int32, (rows, rows), 1),
         1.0,
         0.0,
     ).astype(bf16)
-
-    def picked(named, wanted):
-        position = jnp.dot(named.astype(bf16), before, preferred_element_type=f32)
-        return jnp.where(position == wanted, named, 0.0)
-
+    lines = EXPERTS * CAP
+    line = lax.broadcasted_iota(jnp.int32, (lines, rows), 0)
+    expert = sum((line >= CAP * e).astype(jnp.int32) for e in range(1, EXPERTS))
+    at = line - expert * CAP
+    first = ids[0:1, :] == expert
+    second = ids[1:2, :] == expert
+    named = jnp.where(jnp.logical_or(first, second), 1.0, 0.0)
+    position = jnp.dot(named.astype(bf16), before, preferred_element_type=f32)
     gate = jnp.where(first, gates[0:1, :], jnp.where(second, gates[1:2, :], 0.0))
-    named = jnp.where(jnp.logical_or(first, second), 1.0, 0.0)
-    combine[...] = picked(named, wanted) * gate
-    line = lax.broadcasted_iota(jnp.int32, (2 * SLOTS, rows), 0)
-    expert = sum((line >= 2 * PART * e).astype(jnp.int32) for e in range(1, EXPERTS))
-    at = line - expert * (2 * PART)
+    combine[...] = jnp.where(position == at.astype(f32), gate, 0.0)
     upper = (at >= PART).astype(jnp.int32)
     wanted = (at - upper * PART + core * PART).astype(f32)
-    named = jnp.where(jnp.logical_or(ids[0:1, :] == expert, ids[1:2, :] == expert), 1.0, 0.0)
-    picker = picked(named, wanted)
-    total = jnp.zeros((2 * SLOTS, half), f32)
+    picker = jnp.where(position == wanted, named, 0.0)
+    total = jnp.zeros((lines, half), f32)
     for part in range(2):
         start = pl.multiple_of((x * 2 + part) * half, half)
         normed = (tokens[:, pl.ds(start, half)].astype(f32) * scale).astype(bf16)
@@ -81,7 +73,7 @@
     copies = packed.shape[0] // EXPERTS
     for e in range(EXPERTS):
         for copy in range(copies):
-            packed[e * copies + copy] = total[e * 2 * PART : (e + 1) * 2 * PART]
+            packed[e * copies + copy] = total[e * CAP : (e + 1) * CAP]
     start = pl.multiple_of((x * CORES + core) * out_width, out_width)
     residual[...] = tokens[:, pl.ds(start, out_width)]
 
@@ -95,8 +87,8 @@
         in_specs=[whole(pltpu.HBM)] * 3,
         out_specs=[whole()] * 3,
         out_shape=[
-            pltpu.VMEM((far, 2 * PART, chip_width // 2), jnp.bfloat16),
-            pltpu.VMEM((SLOTS, rows), jnp.float32),
+            pltpu.VMEM((far, CAP, chip_width // 2), jnp.bfloat16),
+            pltpu.VMEM((EXPERTS * CAP, rows), jnp.float32),
             pltpu.VMEM((rows, out_width), jnp.bfloat16),
         ],
         scratch_shapes=[pltpu.VMEM(array.shape, array.dtype) for array in arrays]
@@ -190,52 +182,62 @@
     )(*near_memory(sums))
 
 
-def hidden_kernel(ready, sums, out):
-    straight = lax.axis_index("core") == 0
-    block, width = 64, ready.shape[1]
-    for at in range(0, ready.shape[0], block):
-        mine = ready[at : at + block, :]
-        theirs = hidden_of(sums, at, block, out.dtype)
-        low = jnp.where(straight, mine, theirs)
-        high = jnp.where(straight, theirs, mine)
+def hidden_kernel(sums, *refs):
+    sources, out, places, sems = refs[:CORES], refs[CORES], refs[CORES + 1 : -1], refs[-1]
+    moves = [
+        pltpu.make_async_copy(source, place, sems.at[number])
+        for number, (source, place) in enumerate(zip(sources, places))
+    ]
+    for move in moves:
+        move.start()
+    block = 64
+    for at in range(0, out.shape[1], block):
+        hidden = hidden_of(sums, at, block, out.dtype)
         for copy in range(out.shape[0]):
-            out[copy, at : at + block, 0:width] = low
-            out[copy, at : at + block, width : 2 * width] = high
-
-
-def hidden_units(ready, sums):
+            out[copy, at : at + block, :] = hidden
+    for move in moves:
+        move.wait()
+
+
+def hidden_units(sums, *weights):
     xs, _, n_rows, width = sums.shape
+    far_weights = [pltpu.with_memory_space_constraint(weight, pltpu.HBM) for weight in weights]
     return pl.pallas_call(
         hidden_kernel,
         compiler_params=PARAMS,
-        in_specs=[whole()] * 2,
+        in_specs=[whole()] + [whole(pltpu.HBM)] * CORES,
+        out_specs=[whole()] * (1 + CORES),
+        out_shape=[pltpu.VMEM((xs, n_rows, width), jnp.bfloat16)]
+        + [pltpu.VMEM(weight.shape, weight.dtype) for weight in weights],
+        scratch_shapes=[pltpu.SemaphoreType.DMA((CORES,))],
+    )(*near_memory(sums), *far_weights)
+
+
+def down_kernel(*refs):
+    passed, units, own, other, out = refs[:-4], *refs[-4:]
+    near, _, block, _ = out.shape
+    xs, _, width = units.shape
+    x, core = lax.axis_index("x"), lax.axis_index("core")
+    left = jnp.concatenate([ref[...] for ref in passed] + [units[n] for n in range(xs)], axis=1)
+    starts = [lax.rem(x + (xs - shift), xs) * CORES + core for shift in range(xs)]
+    starts += [number * CORES + (1 - core) for number in range(xs)]
+    starts = [pl.multiple_of(start * width, width) for start in starts]
+    for side, weight in ((core, own), (1 - core, other)):
+        right = jnp.concatenate([weight[pl.ds(start, width), :] for start in starts], axis=0)
+        product = jnp.dot(left, right, preferred_element_type=jnp.float32).astype(out.dtype)
+        for line in range(near):
+            out[line, side] = product[line * block : (line + 1) * block]
+
+
+def down(passed, units, own, other, near):
+    n_rows = units.shape[1]
+    return pl.pallas_call(
+        down_kernel,
+        compiler_params=PARAMS,
+        in_specs=[whole()] * (len(passed) + 3),
         out_specs=whole(),
-        out_shape=pltpu.VMEM((xs, n_rows, CORES * width), jnp.bfloat16),
-    )(*near_memory(ready, sums))
-
-
-def down_kernel(units, own, other, out):
-    xs, _, _ = units.shape
-    near, block, _ = out.shape
-    width = own.shape[1]
-    left = jnp.concatenate([units[source] for source in range(xs)], axis=1)
-    for core, weight in enumerate((own, other)):
-        product = jnp.dot(left, weight[...], preferred_element_type=jnp.float32).astype(out.dtype)
-        for line in range(near):
-            out[line, :, core * width : (core + 1) * width] = product[
-                line * block : (line + 1) * block
-            ]
-
-
-def down(units, own, other, near):
-    n_rows = units.shape[1]
-    return pl.pallas_call(
-        down_kernel,
-        compiler_params=PARAMS,
-        in_specs=[whole()] * 3,
-        out_specs=whole(),
-        out_shape=pltpu.VMEM((near, n_rows // near, CORES * own.shape[1]), jnp.bfloat16),
-    )(*near_memory(units, own, other))
+        out_shape=pltpu.VMEM((near, CORES, n_rows // near, own.shape[1]), jnp.bfloat16),
+    )(*near_memory(*passed, units, own, other))
 
 
 def layer(tokens, route_ids, route_gates, gate_weight, up_weight, down_weight):
@@ -267,23 +269,31 @@
     arrived = arrived.reshape(far, 2, PART, chip_width // 2)
     arrived = jnp.swapaxes(arrived, 1, 2).reshape(far * PART, chip_width)
     rows = lax.all_gather(arrived, "near", axis=0, tiled=True)
+    rows, down_other = lax.optimization_barrier((rows, down_other))
     mine, stacked = own_products(rows, chunks)
     mine = lax.all_to_all(mine, "x", 0, 0, tiled=True)
     stacked = lax.ppermute(stacked, "core", swap)
     theirs = other_products(rows, stacked)
     theirs = lax.all_to_all(theirs, "x", 0, 0, tiled=True)
     ready = first_units(mine)
-    units = lax.all_to_all(hidden_units(ready, theirs), "x", 0, 0, tiled=True)
-    produced = down(units, down_weight, down_other, near)
-    parts = lax.all_to_all(produced, "near", 0, 0, tiled=True)
-    summed = jnp.sum(parts.astype(f32), axis=0).astype(bf16)
-    out_lanes = 2 * out_width // 128
-    returned = lax.all_to_all(
-        summed.reshape(far, PART, out_lanes, 128), "far", 0, 0, tiled=True
+    passed = [ready]
+    for shift in range(1, xs):
+        passed.append(lax.ppermute(ready, "x", [(i, (i + shift) % xs) for i in range(xs)]))
+    theirs, *passed = lax.optimization_barrier((theirs, *passed))
+    hidden, down_weight, down_other = hidden_units(theirs, down_weight, down_other)
+    units = lax.all_to_all(hidden, "x", 0, 0, tiled=True)
+    produced = down(passed, units, down_weight, down_other, near)
+    parts = lax.all_to_all(
+        produced.reshape(near * CORES, far * PART, out_width), ("near", "core"), 0, 0, tiled=True
     )
+    summed = jnp.sum(
+        parts.reshape(near, CORES, far, PART, out_width).astype(f32), axis=0
+    ).astype(bf16)
+    summed = jnp.swapaxes(summed, 0, 1).reshape(far, CAP, out_width)
+    returned = lax.all_to_all(summed, "far", 0, 0, tiled=True)
     returned = jnp.sum(
-        returned.reshape(EXPERTS, copies, PART, out_lanes, 128).astype(f32), axis=1
-    ).reshape(SLOTS, 2 * out_width)
+        returned.reshape(EXPERTS, copies, CAP, out_width).astype(f32), axis=1
+    ).reshape(EXPERTS * CAP, out_width)
     mixture = jnp.einsum(
         "st,sd->td",
         combine,
@@ -291,7 +301,6 @@
         precision=lax.Precision.HIGHEST,
         preferred_element_type=f32,
     )
-    mixture = mixture[:, :out_width] + lax.ppermute(mixture[:, out_width:], "core", swap)
     return (residual.astype(f32) + mixture).astype(bf16)
 
 

time: 220 us -> 220 us (level)
  the two profiles are of different devices: /device:TPU:33 before, /device:TPU:40 now
where the time goes in v9:
time: 220 us; the launch traced here: 219 us
  blocking collectives  93.2 us (42%)
  starting transfers between devices  80.5 us (37%)
  waiting for transfers between devices  29.1 us (13%)
  Pallas kernels  10.7 us (5%)
  local copies, waits for them, and re-layouts  2.28 us (1%)
    all_to_all x1, starting transfers between devices, layer(): arrived = lax.all_to_all(sent, 'far', 0, 0, tiled=True)  43.5 us
    all_to_all x1, blocking collectives, layer(): returned = lax.all_to_all(summed, 'far', 0, 0, tiled=True)  39.2 us
    all_to_all x1, blocking collectives, layer(): lax.all_to_all(produced.reshape(near * CORES, far * PART, out_width), ('n...  24.1 us
    all_gather x1, blocking collectives, layer(): rows = lax.all_gather(arrived, 'near', axis=0, tiled=True)  20.1 us
    all_to_all x1, waiting for transfers between devices, layer(): arrived = lax.all_to_all(sent, 'far', 0, 0, tiled=True)  14.2 us
    ppermute x3, starting transfers between devices, layer(): lax.ppermute(chunk(shift), 'x', [(i, (i + shift) % xs) for i in range(xs)])  12.3 us
    ppermute x3, starting transfers between devices, layer(): lax.ppermute(ready, 'x', [(i, (i + shift) % xs) for i in range(xs)])  10.7 us
    all_to_all x1, blocking collectives, layer(): units = lax.all_to_all(hidden, 'x', 0, 0, tiled=True)  9.81 us
  transfers between devices with their start and end apart: 11, of which 5 were waited for; matrix products, arithmetic and copies ran while one was open for 2% of the time, Pallas kernels for 2%

profile of v9, /device:TPU:40, one launch (start us, length us, event | category | flops | bytes accessed | tf_op | source)
XLA Modules:
  0.0 218.9 jit_solution(17532751868190170101)
XLA Ops:
  0.0 2.0 shard_map.64
  2.0 43.5 %all-to-all-start = ((bf16[8,24,512]{2,1,0:T(8,128)(2,1)}), bf16[8,24,512]{2,1,0:T(8,128)(2,1)S(1)}, u32[]{:S(2)}, u32[]{:S(2)}) async-start(bf16[8,24,512]{2,1,0:T(8,128)(2,1)} %get-tuple-element.22), calls=%async_computation | async-start | bytes 393216 | tf_op jit(solution)/shard_map/all_to_all | solution.py:253
  45.5 1.9 collective-permute-start
  47.5 1.7 dynamic-slice_bitcast_fusion
  49.1 0.1 pad_maximum_fusion.2
  49.2 5.2 %collective-permute-start.2 = (bf16[2,1024,128]{2,1,0:T(8,128)(2,1)S(1)}, bf16[2,1024,128]{2,1,0:T(8,128)(2,1)S(1)}, u32[]{:S(2)}, u32[]{:S(2)}) collective-permute-start(bf16[2,1024,128]{2,1,0:T(8,128)(2,1)S(1)} %pad_maximum_fusion.2), channel_id=1, source_target_pairs={{0,4},{2,6},{4,0},{6,2},{1,5},{3,7},{5,1},{7,3},{8,12},{10,14},{12... | collective-permute-start | bytes 1572872 | tf_op jit(solution)/shard_map/ppermute | solution.py:266
  54.4 0.9 pad_maximum_fusion.1
  55.3 2.7 %collective-permute-start.1 = (bf16[2,1024,128]{2,1,0:T(8,128)(2,1)}, bf16[2,1024,128]{2,1,0:T(8,128)(2,1)S(1)}, u32[]{:S(2)}, u32[]{:S(2)}) collective-permute-start(bf16[2,1024,128]{2,1,0:T(8,128)(2,1)} %pad_maximum_fusion.1), channel_id=1, source_target_pairs={{0,2},{2,4},{4,6},{6,0},{1,3},{3,5},{5,7},{7,1},{8,10},{10,12},{12... | collective-permute-start | bytes 1572872 | tf_op jit(solution)/shard_map/ppermute | solution.py:266
  58.0 0.8 pad_maximum_fusion.3
  58.8 4.4 %collective-permute-start.3 = (bf16[2,1024,128]{2,1,0:T(8,128)(2,1)}, bf16[2,1024,128]{2,1,0:T(8,128)(2,1)S(1)}, u32[]{:S(2)}, u32[]{:S(2)}) collective-permute-start(bf16[2,1024,128]{2,1,0:T(8,128)(2,1)} %pad_maximum_fusion.3), channel_id=1, source_target_pairs={{0,6},{2,0},{4,2},{6,4},{1,7},{3,1},{5,3},{7,5},{8,14},{10,8},{12,... | collective-permute-start | bytes 1572872 | tf_op jit(solution)/shard_map/ppermute | solution.py:266
  63.2 0.1 pad_maximum_fusion.refs_0_
  63.3 14.2 %all-to-all-done = bf16[8,24,512]{2,1,0:T(8,128)(2,1)S(1)} async-done(((bf16[8,24,512]{2,1,0:T(8,128)(2,1)}), bf16[8,24,512]{2,1,0:T(8,128)(2,1)S(1)}, u32[]{:S(2)}, u32[]{:S(2)}) %all-to-all-start) | async-done | bytes 196640 | tf_op jit(solution)/shard_map/all_to_all | solution.py:253
  77.5 0.1 copy.17
  77.6 0.2 copy.18
  77.8 20.1 %all_gather.3.rows = bf16[384,1024]{1,0:T(8,128)(2,1)S(1)} all-gather(bf16[96,1024]{1,0:T(8,128)(2,1)S(1)} %bitcast.43), channel_id=1, replica_groups=mesh['groups'=2,'far'=8,'near'=4,'x'=4,'core'=2] {'near'}, dimensions={0}, use_global_device_ids=true | all-gather | bytes 983040 | tf_op jit(solution)/shard_map/all_gather | solution.py:271
  97.9 0.0 collective-permute-done.refs_1_
  97.9 0.0 collective-permute-done.2.refs_2_
  97.9 0.0 collective-permute-done.1.refs_1_
  98.0 0.0 collective-permute-done.3.refs_3_
  98.0 2.6 %shard_map.65 = (bf16[4,2,384,128]{3,2,1,0:T(8,128)(2,1)}, bf16[4,2,1024,128]{3,2,1,0:T(8,128)(2,1)}) custom-call(bf16[384,1024]{1,0:T(8,128)(2,1)S(1)} %all_gather.3.rows, bf16[2,1024,128]{2,1,0:T(8,128)(2,1)S(1)} %pad_maximum_fusion.refs_0_, bf16[2,1024,128]{2,1,0:T(8,128)(2,1)S(1)} %collective-permute-done.1.refs_1_, ...), custom_call_target="tpu_custom_call" | custom-call | tf_op jit(solution)/shard_map/pallas_call | solution.py:124
  100.6 2.0 collective-permute-start.4
  102.5 6.6 %all-to-all-start.2 = ((bf16[4,2,384,128]{3,2,1,0:T(8,128)(2,1)}), bf16[4,2,384,128]{3,2,1,0:T(8,128)(2,1)S(1)}, u32[]{:S(2)}, u32[]{:S(2)}) async-start(bf16[4,2,384,128]{3,2,1,0:T(8,128)(2,1)} %get-tuple-element.25), calls=%async_computation.2 | async-start | bytes 1572864 | tf_op jit(solution)/shard_map/all_to_all | solution.py:274
  109.1 0.0 collective-permute-done.4.stacked
  109.2 3.5 %shard_map.66 = bf16[4,2,384,128]{3,2,1,0:T(8,128)(2,1)} custom-call(bf16[384,1024]{1,0:T(8,128)(2,1)S(1)} %all_gather.3.rows, bf16[4,2,1024,128]{3,2,1,0:T(8,128)(2,1)} %collective-permute-done.4.stacked), custom_call_target="tpu_custom_call" | custom-call | tf_op jit(solution)/shard_map/pallas_call | solution.py:151
  112.6 9.5 %all-to-all-done.2.sums = bf16[4,2,384,128]{3,2,1,0:T(8,128)(2,1)S(1)} async-done(((bf16[4,2,384,128]{3,2,1,0:T(8,128)(2,1)}), bf16[4,2,384,128]{3,2,1,0:T(8,128)(2,1)S(1)}, u32[]{:S(2)}, u32[]{:S(2)}) %all-to-all-start.2) | async-done | bytes 786464 | tf_op jit(solution)/shard_map/all_to_all | solution.py:274
  122.1 3.6 %all-to-all-start.1 = ((bf16[4,2,384,128]{3,2,1,0:T(8,128)(2,1)}), bf16[4,2,384,128]{3,2,1,0:T(8,128)(2,1)S(1)}, u32[]{:S(2)}, u32[]{:S(2)}) async-start(bf16[4,2,384,128]{3,2,1,0:T(8,128)(2,1)} %shard_map.66), calls=%async_computation.1 | async-start | bytes 1572864 | tf_op jit(solution)/shard_map/all_to_all | solution.py:277
  125.7 0.1 shard_map.67.refs_0_
  125.8 5.1 %collective-permute-start.7 = (bf16[384,128]{1,0:T(8,128)(2,1)S(1)}, bf16[384,128]{1,0:T(8,128)(2,1)S(1)}, u32[]{:S(2)}, u32[]{:S(2)}) collective-permute-start(bf16[384,128]{1,0:T(8,128)(2,1)S(1)} %shard_map.67.refs_0_), channel_id=1, source_target_pairs={{0,6},{2,0},{4,2},{6,4},{1,7},{3,1},{5,3},{7,5},{8,14},{10,8},{12,... | collective-permute-start | bytes 294920 | tf_op jit(solution)/shard_map/ppermute | solution.py:281
  130.9 2.8 %collective-permute-start.6 = (bf16[384,128]{1,0:T(8,128)(2,1)S(1)}, bf16[384,128]{1,0:T(8,128)(2,1)S(1)}, u32[]{:S(2)}, u32[]{:S(2)}) collective-permute-start(bf16[384,128]{1,0:T(8,128)(2,1)S(1)} %shard_map.67.refs_0_), channel_id=1, source_target_pairs={{0,4},{2,6},{4,0},{6,2},{1,5},{3,7},{5,1},{7,3},{8,12},{10,14},{12... | collective-permute-start | bytes 294920 | tf_op jit(solution)/shard_map/ppermute | solution.py:281
  133.7 2.8 %collective-permute-start.5 = (bf16[384,128]{1,0:T(8,128)(2,1)S(1)}, bf16[384,128]{1,0:T(8,128)(2,1)S(1)}, u32[]{:S(2)}, u32[]{:S(2)}) collective-permute-start(bf16[384,128]{1,0:T(8,128)(2,1)S(1)} %shard_map.67.refs_0_), channel_id=1, source_target_pairs={{0,2},{2,4},{4,6},{6,0},{1,3},{3,5},{5,7},{7,1},{8,10},{10,12},{12... | collective-permute-start | bytes 294920 | tf_op jit(solution)/shard_map/ppermute | solution.py:281
  136.5 2.8 %collective-permute-done.7.refs_3_ = bf16[384,128]{1,0:T(8,128)(2,1)S(1)} collective-permute-done((bf16[384,128]{1,0:T(8,128)(2,1)S(1)}, bf16[384,128]{1,0:T(8,128)(2,1)S(1)}, u32[]{:S(2)}, u32[]{:S(2)}) %collective-permute-start.7) | collective-permute-done | bytes 98336 | tf_op jit(solution)/shard_map/ppermute | solution.py:281
  139.4 1.5 collective-permute-done.6.refs_2_
  140.8 1.1 collective-permute-done.5.refs_1_
  141.9 0.0 all-to-all-done.1.sums
  141.9 1.6 shard_map.68
  143.5 9.8 %all_to_all.30.refs_4_ = bf16[4,384,128]{2,1,0:T(8,128)(2,1)S(1)} all-to-all(bf16[4,384,128]{2,1,0:T(8,128)(2,1)S(1)} %get-tuple-element.32), channel_id=1, replica_groups=mesh['groups'=2,'far'=8,'near'=4,'x'=4,'core'=2] {'x'}, dimensions={0} | all-to-all | bytes 786432 | tf_op jit(solution)/shard_map/all_to_all | solution.py:284
  153.3 1.0 shard_map.69
  154.3 24.1 %all_to_all.31 = bf16[8,96,512]{2,1,0:T(8,128)(2,1)S(1)} all-to-all(bf16[8,96,512]{2,1,0:T(8,128)(2,1)S(1)} %bitcast.36), channel_id=1, replica_groups=mesh['groups'=2,'far'=8,'near'=4,'x'=4,'core'=2] {'near','core'}, dimensions={0} | all-to-all | bytes 1572864 | tf_op jit(solution)/shard_map/all_to_all | solution.py:286
  178.3 0.2 reduce.1
  178.5 0.2 copy.24
  178.7 0.1 copy.20
  178.8 0.1 copy.21
  178.8 39.2 %all_to_all.32 = bf16[8,24,512]{2,1,0:T(8,128)(2,1)S(1)} all-to-all(bf16[8,24,512]{2,1,0:T(8,128)(2,1)S(1)} %copy.21), channel_id=1, replica_groups=mesh['groups'=2,'far'=8,'near'=4,'x'=4,'core'=2] {'far'}, dimensions={0} | all-to-all | bytes 393216 | tf_op jit(solution)/shard_map/all_to_all | solution.py:293
  218.1 0.9 fusion
  (2 shorter events, 0.0 us)
Async XLA Ops:
  2.0 75.5 %all-to-all-start = ((bf16[8,24,512]{2,1,0:T(8,128)(2,1)}), bf16[8,24,512]{2,1,0:T(8,128)(2,1)S(1)}, u32[]{:S(2)}, u32[]{:S(2)}) async-start(bf16[8,24,512]{2,1,0:T(8,128)(2,1)} %get-tuple-element.22), calls=%async_computation | async-start | bytes 393216 | tf_op jit(solution)/shard_map/all_to_all | solution.py:253
  45.5 52.5 %collective-permute-start = (bf16[1024,512]{1,0:T(8,128)(2,1)}, bf16[1024,512]{1,0:T(8,128)(2,1)}, u32[]{:S(2)}, u32[]{:S(2)}) collective-permute-start(bf16[1024,512]{1,0:T(8,128)(2,1)} %refs_0_.3), channel_id=1, source_target_pairs={{0,1},{1,0},{2,3},{3,2},{4,5},{5,4},{6,7},{7,6},{8,9},{9,8},{10,11... | collective-permute-start | bytes 3145736 | tf_op jit(solution)/shard_map/ppermute | solution.py:267
  49.2 48.7 %collective-permute-start.2 = (bf16[2,1024,128]{2,1,0:T(8,128)(2,1)S(1)}, bf16[2,1024,128]{2,1,0:T(8,128)(2,1)S(1)}, u32[]{:S(2)}, u32[]{:S(2)}) collective-permute-start(bf16[2,1024,128]{2,1,0:T(8,128)(2,1)S(1)} %pad_maximum_fusion.2), channel_id=1, source_target_pairs={{0,4},{2,6},{4,0},{6,2},{1,5},{3,7},{5,1},{7,3},{8,12},{10,14},{12... | collective-permute-start | bytes 1572872 | tf_op jit(solution)/shard_map/ppermute | solution.py:266
  55.3 42.7 %collective-permute-start.1 = (bf16[2,1024,128]{2,1,0:T(8,128)(2,1)}, bf16[2,1024,128]{2,1,0:T(8,128)(2,1)S(1)}, u32[]{:S(2)}, u32[]{:S(2)}) collective-permute-start(bf16[2,1024,128]{2,1,0:T(8,128)(2,1)} %pad_maximum_fusion.1), channel_id=1, source_target_pairs={{0,2},{2,4},{4,6},{6,0},{1,3},{3,5},{5,7},{7,1},{8,10},{10,12},{12... | collective-permute-start | bytes 1572872 | tf_op jit(solution)/shard_map/ppermute | solution.py:266
  58.8 39.2 %collective-permute-start.3 = (bf16[2,1024,128]{2,1,0:T(8,128)(2,1)}, bf16[2,1024,128]{2,1,0:T(8,128)(2,1)S(1)}, u32[]{:S(2)}, u32[]{:S(2)}) collective-permute-start(bf16[2,1024,128]{2,1,0:T(8,128)(2,1)} %pad_maximum_fusion.3), channel_id=1, source_target_pairs={{0,6},{2,0},{4,2},{6,4},{1,7},{3,1},{5,3},{7,5},{8,14},{10,8},{12,... | collective-permute-start | bytes 1572872 | tf_op jit(solution)/shard_map/ppermute | solution.py:266
  100.6 8.6 %collective-permute-start.4 = (bf16[4,2,1024,128]{3,2,1,0:T(8,128)(2,1)}, bf16[4,2,1024,128]{3,2,1,0:T(8,128)(2,1)}, u32[]{:S(2)}, u32[]{:S(2)}) collective-permute-start(bf16[4,2,1024,128]{3,2,1,0:T(8,128)(2,1)} %get-tuple-element.24), channel_id=1, source_target_pairs={{0,1},{1,0},{2,3},{3,2},{4,5},{5,4},{6,7},{7,6},{8,9},{9,8},{10,11... | collective-permute-start | bytes 6291464 | tf_op jit(solution)/shard_map/ppermute | solution.py:275
  102.5 19.6 %all-to-all-start.2 = ((bf16[4,2,384,128]{3,2,1,0:T(8,128)(2,1)}), bf16[4,2,384,128]{3,2,1,0:T(8,128)(2,1)S(1)}, u32[]{:S(2)}, u32[]{:S(2)}) async-start(bf16[4,2,384,128]{3,2,1,0:T(8,128)(2,1)} %get-tuple-element.25), calls=%async_computation.2 | async-start | bytes 1572864 | tf_op jit(solution)/shard_map/all_to_all | solution.py:274
  122.1 19.8 %all-to-all-start.1 = ((bf16[4,2,384,128]{3,2,1,0:T(8,128)(2,1)}), bf16[4,2,384,128]{3,2,1,0:T(8,128)(2,1)S(1)}, u32[]{:S(2)}, u32[]{:S(2)}) async-start(bf16[4,2,384,128]{3,2,1,0:T(8,128)(2,1)} %shard_map.66), calls=%async_computation.1 | async-start | bytes 1572864 | tf_op jit(solution)/shard_map/all_to_all | solution.py:277
  125.8 13.5 %collective-permute-start.7 = (bf16[384,128]{1,0:T(8,128)(2,1)S(1)}, bf16[384,128]{1,0:T(8,128)(2,1)S(1)}, u32[]{:S(2)}, u32[]{:S(2)}) collective-permute-start(bf16[384,128]{1,0:T(8,128)(2,1)S(1)} %shard_map.67.refs_0_), channel_id=1, source_target_pairs={{0,6},{2,0},{4,2},{6,4},{1,7},{3,1},{5,3},{7,5},{8,14},{10,8},{12,... | collective-permute-start | bytes 294920 | tf_op jit(solution)/shard_map/ppermute | solution.py:281
  130.9 9.9 %collective-permute-start.6 = (bf16[384,128]{1,0:T(8,128)(2,1)S(1)}, bf16[384,128]{1,0:T(8,128)(2,1)S(1)}, u32[]{:S(2)}, u32[]{:S(2)}) collective-permute-start(bf16[384,128]{1,0:T(8,128)(2,1)S(1)} %shard_map.67.refs_0_), channel_id=1, source_target_pairs={{0,4},{2,6},{4,0},{6,2},{1,5},{3,7},{5,1},{7,3},{8,12},{10,14},{12... | collective-permute-start | bytes 294920 | tf_op jit(solution)/shard_map/ppermute | solution.py:281
  133.7 8.2 %collective-permute-start.5 = (bf16[384,128]{1,0:T(8,128)(2,1)S(1)}, bf16[384,128]{1,0:T(8,128)(2,1)S(1)}, u32[]{:S(2)}, u32[]{:S(2)}) collective-permute-start(bf16[384,128]{1,0:T(8,128)(2,1)S(1)} %shard_map.67.refs_0_), channel_id=1, source_target_pairs={{0,2},{2,4},{4,6},{6,0},{1,3},{3,5},{5,7},{7,1},{8,10},{10,12},{12... | collective-permute-start | bytes 294920 | tf_op jit(solution)/shard_map/ppermute | solution.py:281

commit v10 on v8

--- a/solution.py
+++ b/solution.py
@@ -8,7 +8,7 @@
 
 EXPERTS = 4
 CAP = 24
-NEAR = 8
+NEAR = 4
 CORES = 2
 PART = CAP // CORES
 
@@ -96,38 +96,50 @@
     )(*[pltpu.with_memory_space_constraint(array, pltpu.HBM) for array in arrays])
 
 
-def product_kernel(rows, own, other, out, held, sem):
-    xs, kinds, _, width = own.shape
+def product_kernel(rows, *refs):
+    xs = refs[-1].shape[0] + 1
+    own, late, other, out = refs[:xs], refs[xs], refs[xs + 1 : 2 * xs], refs[2 * xs]
+    held, sems = list(refs[2 * xs + 1 : -1]), refs[-1]
     moves = [
-        pltpu.make_async_copy(other.at[shift], held.at[shift], sem.at[shift])
-        for shift in range(xs)
+        pltpu.make_async_copy(source, place, sems.at[number])
+        for number, (source, place) in enumerate(zip(other, held))
     ]
     for move in moves:
         move.start()
+    held.insert(xs // 2, late)
     x = lax.axis_index("x")
     left = rows[...]
-    for core, weights in enumerate((own, held)):
+    width = out.shape[-1]
+    for core, chunks in enumerate((own, held)):
+        if core:
+            for move in moves:
+                move.wait()
         for shift in range(xs):
-            if core:
-                moves[shift].wait()
             to = lax.rem(x + (xs - shift), xs)
-            both = jnp.concatenate([weights[shift, kind] for kind in range(kinds)], axis=1)
+            both = jnp.concatenate([chunks[shift][kind] for kind in range(2)], axis=1)
             product = jnp.dot(left, both, preferred_element_type=jnp.float32).astype(out.dtype)
-            for kind in range(kinds):
+            for kind in range(2):
                 out[to, core, kind] = product[:, kind * width : (kind + 1) * width]
 
 
 def products(rows, own, other):
-    n_rows = rows.shape[0]
-    xs, kinds, _, width = own.shape
+    n_rows, xs = rows.shape[0], len(own)
+    width = own[0].shape[2]
+    late = other[xs // 2]
+    other = [
+        pltpu.with_memory_space_constraint(chunk, pltpu.HBM)
+        for shift, chunk in enumerate(other)
+        if shift != xs // 2
+    ]
     return pl.pallas_call(
         product_kernel,
         compiler_params=PARAMS,
-        in_specs=[whole(), whole(), whole(pltpu.HBM)],
+        in_specs=[whole()] * (2 + xs) + [whole(pltpu.HBM)] * len(other),
         out_specs=whole(),
-        out_shape=pltpu.VMEM((xs, CORES, kinds, n_rows, width), jnp.bfloat16),
-        scratch_shapes=[pltpu.VMEM(other.shape, other.dtype), pltpu.SemaphoreType.DMA((xs,))],
-    )(*near_memory(rows, own), pltpu.with_memory_space_constraint(other, pltpu.HBM))
+        out_shape=pltpu.VMEM((xs, CORES, 2, n_rows, width), jnp.bfloat16),
+        scratch_shapes=[pltpu.VMEM(chunk.shape, chunk.dtype) for chunk in other]
+        + [pltpu.SemaphoreType.DMA((len(other),))],
+    )(*near_memory(rows, *own, late), *other)
 
 
 def hidden_kernel(sums, *refs):
@@ -216,18 +228,16 @@
     chunks = [chunk(0)]
     for shift in range(1, xs):
         chunks.append(lax.ppermute(chunk(shift), "x", [(i, (i + shift) % xs) for i in range(xs)]))
-    own = jnp.stack(chunks)
-    other = lax.ppermute(own, "core", swap)
+    swapped = []
+    for shift in range(xs):
+        swapped.append(lax.ppermute(chunks[shift], "core", swap))
     down_other = lax.ppermute(down_weight, "core", swap)
 
     arrived = arrived.reshape(far, 2, PART, chip_width // 2)
-    arrived = jnp.swapaxes(arrived, 1, 2).reshape(1, far * PART, chip_width)
-    rows = lax.all_to_all(
-        jnp.broadcast_to(arrived, (near, far * PART, chip_width)), "near", 0, 0, tiled=True
-    )
-    n_rows = near * far * PART
+    arrived = jnp.swapaxes(arrived, 1, 2).reshape(far * PART, chip_width)
+    rows = lax.all_gather(arrived, "near", axis=0, tiled=True)
     rows, down_other = lax.optimization_barrier((rows, down_other))
-    partial = products(rows.reshape(n_rows, chip_width), own, other)
+    partial = products(rows, chunks, swapped)
     sums = lax.all_to_all(partial, "x", 0, 0, tiled=True)
     hidden, down_weight, down_other = hidden_units(sums, down_weight, down_other)
     units = lax.all_to_all(hidden, "x", 0, 0, tiled=True)

time: 245 us -> 227 us (0.927)
  the two profiles are of different devices: /device:TPU:33 before, /device:TPU:40 now
where the time goes in v10:
time: 227 us
  blocking collectives  136 us (60%)
  starting transfers between devices  66 us (29%)
  waiting for transfers between devices  12.6 us (6%)
  Pallas kernels  7.57 us (3%)
  local copies, waits for them, and re-layouts  3.06 us (1%)
    all_to_all x1, blocking collectives, layer(): returned = lax.all_to_all(summed, 'far', 0, 0, tiled=True)  55 us
    all_to_all x1, starting transfers between devices, layer(): arrived = lax.all_to_all(sent, 'far', 0, 0, tiled=True)  43.5 us
    all_to_all x1, blocking collectives, layer(): lax.all_to_all(produced.reshape(near * CORES, far * PART, out_width), ('n...  25.8 us
    all_to_all x1, blocking collectives, layer(): sums = lax.all_to_all(partial, 'x', 0, 0, tiled=True)  22.4 us
    all_gather x1, blocking collectives, layer(): rows = lax.all_gather(arrived, 'near', axis=0, tiled=True)  20.8 us
    ppermute x3, waiting for transfers between devices, layer(): lax.ppermute(chunk(shift), 'x', [(i, (i + shift) % xs) for i in range(xs)])  12.6 us
    ppermute x3, starting transfers between devices, layer(): lax.ppermute(chunk(shift), 'x', [(i, (i + shift) % xs) for i in range(xs)])  12.3 us
    all_to_all x1, blocking collectives, layer(): units = lax.all_to_all(hidden, 'x', 0, 0, tiled=True)  11.9 us
  transfers between devices with their start and end apart: 9, of which 2 were waited for; matrix products, arithmetic and copies ran while one was open for 1% of the time, Pallas kernels for 0%

profile of v10, /device:TPU:40, one launch (start us, length us, event | category | flops | bytes accessed | tf_op | source)
XLA Modules:
  0.0 226.8 jit_solution(16655660393330140223)
XLA Ops:
  0.0 2.0 shard_map.64
  2.0 43.5 %all-to-all-start = ((bf16[8,24,512]{2,1,0:T(8,128)(2,1)}), bf16[8,24,512]{2,1,0:T(8,128)(2,1)S(1)}, u32[]{:S(2)}, u32[]{:S(2)}) async-start(bf16[8,24,512]{2,1,0:T(8,128)(2,1)} %get-tuple-element.15), calls=%async_computation | async-start | bytes 393216 | tf_op jit(solution)/shard_map/all_to_all | solution.py:217
  45.5 1.9 collective-permute-start
  47.5 1.7 dynamic-slice_bitcast_fusion
  49.1 0.1 pad_maximum_fusion.2
  49.2 5.2 %collective-permute-start.2 = (bf16[2,1024,128]{2,1,0:T(8,128)(2,1)S(1)}, bf16[2,1024,128]{2,1,0:T(8,128)(2,1)S(1)}, u32[]{:S(2)}, u32[]{:S(2)}) collective-permute-start(bf16[2,1024,128]{2,1,0:T(8,128)(2,1)S(1)} %pad_maximum_fusion.2), channel_id=1, source_target_pairs={{0,4},{2,6},{4,0},{6,2},{1,5},{3,7},{5,1},{7,3},{8,12},{10,14},{12... | collective-permute-start | bytes 1572872 | tf_op jit(solution)/shard_map/ppermute | solution.py:230
  54.4 0.1 pad_maximum_fusion.1
  54.5 2.7 %collective-permute-start.1 = (bf16[2,1024,128]{2,1,0:T(8,128)(2,1)S(1)}, bf16[2,1024,128]{2,1,0:T(8,128)(2,1)S(1)}, u32[]{:S(2)}, u32[]{:S(2)}) collective-permute-start(bf16[2,1024,128]{2,1,0:T(8,128)(2,1)S(1)} %pad_maximum_fusion.1), channel_id=1, source_target_pairs={{0,2},{2,4},{4,6},{6,0},{1,3},{3,5},{5,7},{7,1},{8,10},{10,12},{12... | collective-permute-start | bytes 1572872 | tf_op jit(solution)/shard_map/ppermute | solution.py:230
  57.2 0.1 pad_maximum_fusion.3
  57.2 4.4 %collective-permute-start.3 = (bf16[2,1024,128]{2,1,0:T(8,128)(2,1)S(1)}, bf16[2,1024,128]{2,1,0:T(8,128)(2,1)S(1)}, u32[]{:S(2)}, u32[]{:S(2)}) collective-permute-start(bf16[2,1024,128]{2,1,0:T(8,128)(2,1)S(1)} %pad_maximum_fusion.3), channel_id=1, source_target_pairs={{0,6},{2,0},{4,2},{6,4},{1,7},{3,1},{5,3},{7,5},{8,14},{10,8},{12,... | collective-permute-start | bytes 1572872 | tf_op jit(solution)/shard_map/ppermute | solution.py:230
  61.7 0.1 pad_maximum_fusion.refs_0_
  61.7 2.0 collective-permute-start.5
  63.7 3.8 %collective-permute-done.2.refs_2_ = bf16[2,1024,128]{2,1,0:T(8,128)(2,1)S(1)} collective-permute-done((bf16[2,1024,128]{2,1,0:T(8,128)(2,1)S(1)}, bf16[2,1024,128]{2,1,0:T(8,128)(2,1)S(1)}, u32[]{:S(2)}, u32[]{:S(2)}) %collective-permute-start.2) | collective-permute-done | bytes 524320 | tf_op jit(solution)/shard_map/ppermute | solution.py:230
  67.5 1.9 collective-permute-start.4
  69.4 8.8 %collective-permute-done.1.refs_1_ = bf16[2,1024,128]{2,1,0:T(8,128)(2,1)S(1)} collective-permute-done((bf16[2,1024,128]{2,1,0:T(8,128)(2,1)S(1)}, bf16[2,1024,128]{2,1,0:T(8,128)(2,1)S(1)}, u32[]{:S(2)}, u32[]{:S(2)}) %collective-permute-start.1) | collective-permute-done | bytes 524320 | tf_op jit(solution)/shard_map/ppermute | solution.py:230
  78.2 2.0 collective-permute-start.6
  80.2 0.0 collective-permute-done.3.refs_3_
  80.2 2.4 %collective-permute-start.7 = (bf16[2,1024,128]{2,1,0:T(8,128)(2,1)S(1)}, bf16[2,1024,128]{2,1,0:T(8,128)(2,1)}, u32[]{:S(2)}, u32[]{:S(2)}) collective-permute-start(bf16[2,1024,128]{2,1,0:T(8,128)(2,1)S(1)} %collective-permute-done.3.refs_3_), channel_id=1, source_target_pairs={{0,1},{1,0},{2,3},{3,2},{4,5},{5,4},{6,7},{7,6},{8,9},{9,8},{10,11... | collective-permute-start | bytes 1572872 | tf_op jit(solution)/shard_map/ppermute | solution.py:233
  82.6 0.0 all-to-all-done
  82.6 0.1 copy.17
  82.7 0.2 copy.18
  83.0 20.8 %all_gather.3.rows = bf16[384,1024]{1,0:T(8,128)(2,1)S(1)} all-gather(bf16[96,1024]{1,0:T(8,128)(2,1)S(1)} %bitcast.43), channel_id=1, replica_groups=mesh['groups'=2,'far'=8,'near'=4,'x'=4,'core'=2] {'near'}, dimensions={0}, use_global_device_ids=true | all-gather | bytes 983040 | tf_op jit(solution)/shard_map/all_gather | solution.py:238
  103.7 0.0 collective-permute-done.refs_1_
  103.7 0.0 collective-permute-done.5.refs_5_
  103.7 0.0 copy-start
  103.7 0.0 collective-permute-done.4.refs_4_
  103.8 0.0 collective-permute-done.6.refs_6_
  103.8 0.0 collective-permute-done.7.refs_7_
  103.8 0.8 copy-done
  104.5 3.1 %shard_map.65 = bf16[4,2,2,384,128]{4,3,2,1,0:T(8,128)(2,1)S(1)} custom-call(bf16[384,1024]{1,0:T(8,128)(2,1)S(1)} %all_gather.3.rows, bf16[2,1024,128]{2,1,0:T(8,128)(2,1)S(1)} %pad_maximum_fusion.refs_0_, bf16[2,1024,128]{2,1,0:T(8,128)(2,1)S(1)} %collective-permute-done.1.refs_1_, bf16[2,1024,128]{2,1,0:T(8,128)(2,1)S(1)} %collective-permute-done.2.refs_2_, ...), custom_call_target="tpu_custom_call" | custom-call | tf_op jit(solution)/shard_map/pallas_call | solution.py:134
  107.6 22.4 %all_to_all.25.sums = bf16[4,2,2,384,128]{4,3,2,1,0:T(8,128)(2,1)S(1)} all-to-all(bf16[4,2,2,384,128]{4,3,2,1,0:T(8,128)(2,1)S(1)} %shard_map.65), channel_id=1, replica_groups=mesh['groups'=2,'far'=8,'near'=4,'x'=4,'core'=2] {'x'}, dimensions={0} | all-to-all | bytes 3145728 | tf_op jit(solution)/shard_map/all_to_all | solution.py:241
  130.0 1.6 shard_map.66
  131.6 11.9 %all_to_all.26.units = bf16[4,384,256]{2,1,0:T(8,128)(2,1)S(1)} all-to-all(bf16[4,384,256]{2,1,0:T(8,128)(2,1)S(1)} %get-tuple-element.18), channel_id=1, replica_groups=mesh['groups'=2,'far'=8,'near'=4,'x'=4,'core'=2] {'x'}, dimensions={0} | all-to-all | bytes 1572864 | tf_op jit(solution)/shard_map/all_to_all | solution.py:243
  143.5 1.0 shard_map.67
  144.5 25.8 %all_to_all.27 = bf16[8,96,512]{2,1,0:T(8,128)(2,1)S(1)} all-to-all(bf16[8,96,512]{2,1,0:T(8,128)(2,1)S(1)} %bitcast.36), channel_id=1, replica_groups=mesh['groups'=2,'far'=8,'near'=4,'x'=4,'core'=2] {'near','core'}, dimensions={0} | all-to-all | bytes 1572864 | tf_op jit(solution)/shard_map/all_to_all | solution.py:245
  170.3 0.2 reduce.1
  170.5 0.2 copy.24
  170.7 0.1 copy.20
  170.8 0.1 copy.21
  170.8 55.0 %all_to_all.28 = bf16[8,24,512]{2,1,0:T(8,128)(2,1)S(1)} all-to-all(bf16[8,24,512]{2,1,0:T(8,128)(2,1)S(1)} %copy.21), channel_id=1, replica_groups=mesh['groups'=2,'far'=8,'near'=4,'x'=4,'core'=2] {'far'}, dimensions={0} | all-to-all | bytes 393216 | tf_op jit(solution)/shard_map/all_to_all | solution.py:252
  225.9 0.9 fusion
  (2 shorter events, 0.0 us)
Async XLA Ops:
  2.0 80.7 %all-to-all-start = ((bf16[8,24,512]{2,1,0:T(8,128)(2,1)}), bf16[8,24,512]{2,1,0:T(8,128)(2,1)S(1)}, u32[]{:S(2)}, u32[]{:S(2)}) async-start(bf16[8,24,512]{2,1,0:T(8,128)(2,1)} %get-tuple-element.15), calls=%async_computation | async-start | bytes 393216 | tf_op jit(solution)/shard_map/all_to_all | solution.py:217
  45.5 58.3 %collective-permute-start = (bf16[1024,512]{1,0:T(8,128)(2,1)}, bf16[1024,512]{1,0:T(8,128)(2,1)}, u32[]{:S(2)}, u32[]{:S(2)}) collective-permute-start(bf16[1024,512]{1,0:T(8,128)(2,1)} %refs_0_.3), channel_id=1, source_target_pairs={{0,1},{1,0},{2,3},{3,2},{4,5},{5,4},{6,7},{7,6},{8,9},{9,8},{10,11... | collective-permute-start | bytes 3145736 | tf_op jit(solution)/shard_map/ppermute | solution.py:234
  49.2 18.3 %collective-permute-start.2 = (bf16[2,1024,128]{2,1,0:T(8,128)(2,1)S(1)}, bf16[2,1024,128]{2,1,0:T(8,128)(2,1)S(1)}, u32[]{:S(2)}, u32[]{:S(2)}) collective-permute-start(bf16[2,1024,128]{2,1,0:T(8,128)(2,1)S(1)} %pad_maximum_fusion.2), channel_id=1, source_target_pairs={{0,4},{2,6},{4,0},{6,2},{1,5},{3,7},{5,1},{7,3},{8,12},{10,14},{12... | collective-permute-start | bytes 1572872 | tf_op jit(solution)/shard_map/ppermute | solution.py:230
  54.5 23.7 %collective-permute-start.1 = (bf16[2,1024,128]{2,1,0:T(8,128)(2,1)S(1)}, bf16[2,1024,128]{2,1,0:T(8,128)(2,1)S(1)}, u32[]{:S(2)}, u32[]{:S(2)}) collective-permute-start(bf16[2,1024,128]{2,1,0:T(8,128)(2,1)S(1)} %pad_maximum_fusion.1), channel_id=1, source_target_pairs={{0,2},{2,4},{4,6},{6,0},{1,3},{3,5},{5,7},{7,1},{8,10},{10,12},{12... | collective-permute-start | bytes 1572872 | tf_op jit(solution)/shard_map/ppermute | solution.py:230
  57.2 23.0 %collective-permute-start.3 = (bf16[2,1024,128]{2,1,0:T(8,128)(2,1)S(1)}, bf16[2,1024,128]{2,1,0:T(8,128)(2,1)S(1)}, u32[]{:S(2)}, u32[]{:S(2)}) collective-permute-start(bf16[2,1024,128]{2,1,0:T(8,128)(2,1)S(1)} %pad_maximum_fusion.3), channel_id=1, source_target_pairs={{0,6},{2,0},{4,2},{6,4},{1,7},{3,1},{5,3},{7,5},{8,14},{10,8},{12,... | collective-permute-start | bytes 1572872 | tf_op jit(solution)/shard_map/ppermute | solution.py:230
  61.7 42.0 %collective-permute-start.5 = (bf16[2,1024,128]{2,1,0:T(8,128)(2,1)S(1)}, bf16[2,1024,128]{2,1,0:T(8,128)(2,1)S(1)}, u32[]{:S(2)}, u32[]{:S(2)}) collective-permute-start(bf16[2,1024,128]{2,1,0:T(8,128)(2,1)S(1)} %pad_maximum_fusion.refs_0_), channel_id=1, source_target_pairs={{0,1},{1,0},{2,3},{3,2},{4,5},{5,4},{6,7},{7,6},{8,9},{9,8},{10,11... | collective-permute-start | bytes 1572872 | tf_op jit(solution)/shard_map/ppermute | solution.py:233
  67.5 36.3 %collective-permute-start.4 = (bf16[2,1024,128]{2,1,0:T(8,128)(2,1)S(1)}, bf16[2,1024,128]{2,1,0:T(8,128)(2,1)S(1)}, u32[]{:S(2)}, u32[]{:S(2)}) collective-permute-start(bf16[2,1024,128]{2,1,0:T(8,128)(2,1)S(1)} %collective-permute-done.2.refs_2_), channel_id=1, source_target_pairs={{0,1},{1,0},{2,3},{3,2},{4,5},{5,4},{6,7},{7,6},{8,9},{9,8},{10,11... | collective-permute-start | bytes 1572872 | tf_op jit(solution)/shard_map/ppermute | solution.py:233
  78.2 25.5 %collective-permute-start.6 = (bf16[2,1024,128]{2,1,0:T(8,128)(2,1)S(1)}, bf16[2,1024,128]{2,1,0:T(8,128)(2,1)}, u32[]{:S(2)}, u32[]{:S(2)}) collective-permute-start(bf16[2,1024,128]{2,1,0:T(8,128)(2,1)S(1)} %collective-permute-done.1.refs_1_), channel_id=1, source_target_pairs={{0,1},{1,0},{2,3},{3,2},{4,5},{5,4},{6,7},{7,6},{8,9},{9,8},{10,11... | collective-permute-start | bytes 1572872 | tf_op jit(solution)/shard_map/ppermute | solution.py:233
  80.2 23.5 %collective-permute-start.7 = (bf16[2,1024,128]{2,1,0:T(8,128)(2,1)S(1)}, bf16[2,1024,128]{2,1,0:T(8,128)(2,1)}, u32[]{:S(2)}, u32[]{:S(2)}) collective-permute-start(bf16[2,1024,128]{2,1,0:T(8,128)(2,1)S(1)} %collective-permute-done.3.refs_3_), channel_id=1, source_target_pairs={{0,1},{1,0},{2,3},{3,2},{4,5},{5,4},{6,7},{7,6},{8,9},{9,8},{10,11... | collective-permute-start | bytes 1572872 | tf_op jit(solution)/shard_map/ppermute | solution.py:233
  103.7 0.8 copy-start

commit v11 on v8

--- a/solution.py
+++ b/solution.py
@@ -8,7 +8,7 @@
 
 EXPERTS = 4
 CAP = 24
-NEAR = 8
+NEAR = 4
 CORES = 2
 PART = CAP // CORES
 
@@ -34,8 +34,7 @@
     ]
     for move in moves:
         move.start()
-    for move in moves:
-        move.wait()
+    moves[0].wait()
     tokens, ids, gates = held
     f32, bf16 = jnp.float32, jnp.bfloat16
     half = packed.shape[2]
@@ -44,6 +43,8 @@
     out_width = residual.shape[1]
     floats = tokens[...].astype(f32)
     scale = lax.rsqrt(jnp.mean(floats * floats, axis=1, keepdims=True) + EPSILON)
+    for move in moves[1:]:
+        move.wait()
     before = jnp.where(
         lax.broadcasted_iota(jnp.int32, (rows, rows), 0)
         < lax.broadcasted_iota(jnp.int32, (rows, rows), 1),
@@ -98,9 +99,12 @@
 
 def product_kernel(rows, own, other, out, held, sem):
     xs, kinds, _, width = own.shape
+    half = xs // 2
     moves = [
-        pltpu.make_async_copy(other.at[shift], held.at[shift], sem.at[shift])
-        for shift in range(xs)
+        pltpu.make_async_copy(
+            other.at[pl.ds(part * half, half)], held.at[pl.ds(part * half, half)], sem.at[part]
+        )
+        for part in range(2)
     ]
     for move in moves:
         move.start()
@@ -108,8 +112,8 @@
     left = rows[...]
     for core, weights in enumerate((own, held)):
         for shift in range(xs):
-            if core:
-                moves[shift].wait()
+            if core and shift % half == 0:
+                moves[shift // half].wait()
             to = lax.rem(x + (xs - shift), xs)
             both = jnp.concatenate([weights[shift, kind] for kind in range(kinds)], axis=1)
             product = jnp.dot(left, both, preferred_element_type=jnp.float32).astype(out.dtype)
@@ -126,7 +130,7 @@
         in_specs=[whole(), whole(), whole(pltpu.HBM)],
         out_specs=whole(),
         out_shape=pltpu.VMEM((xs, CORES, kinds, n_rows, width), jnp.bfloat16),
-        scratch_shapes=[pltpu.VMEM(other.shape, other.dtype), pltpu.SemaphoreType.DMA((xs,))],
+        scratch_shapes=[pltpu.VMEM(other.shape, other.dtype), pltpu.SemaphoreType.DMA((2,))],
     )(*near_memory(rows, own), pltpu.with_memory_space_constraint(other, pltpu.HBM))
 
 

time: 245 us -> 232 us (0.947)
  the two profiles are of different devices: /device:TPU:33 before, /device:TPU:40 now
where the time goes in v11:
time: 232 us; the launch traced here: 231 us
  blocking collectives  179 us (77%)
  starting transfers between devices  23.1 us (10%)
  waiting for transfers between devices  18.8 us (8%)
  Pallas kernels  7.05 us (3%)
    all_to_all x1, blocking collectives, layer(): arrived = lax.all_to_all(sent, 'far', 0, 0, tiled=True)  75.5 us
    all_to_all x1, blocking collectives, layer(): returned = lax.all_to_all(summed, 'far', 0, 0, tiled=True)  38.9 us
    all_to_all x1, blocking collectives, layer(): lax.all_to_all(produced.reshape(near * CORES, far * PART, out_width), ('n...  25.6 us
    all_to_all x1, blocking collectives, layer(): sums = lax.all_to_all(partial, 'x', 0, 0, tiled=True)  24.9 us
    ppermute x3, waiting for transfers between devices, layer(): lax.ppermute(chunk(shift), 'x', [(i, (i + shift) % xs) for i in range(xs)])  15.5 us
    all_to_all x1, blocking collectives, layer(): units = lax.all_to_all(hidden, 'x', 0, 0, tiled=True)  13.9 us
    ppermute x3, starting transfers between devices, layer(): lax.ppermute(chunk(shift), 'x', [(i, (i + shift) % xs) for i in range(xs)])  12.6 us
    all_to_all x1, starting transfers between devices, layer(): lax.all_to_all(jnp.broadcast_to(arrived, (near, far * PART, chip_width)),...  6 us
  transfers between devices with their start and end apart: 6, of which 3 were waited for; matrix products, arithmetic and copies ran while one was open for 0% of the time, Pallas kernels for 0%

profile of v11, /device:TPU:40, one launch (start us, length us, event | category | flops | bytes accessed | tf_op | source)
XLA Modules:
  0.0 231.2 jit_solution(1130389605091000834)
XLA Ops:
  0.0 1.4 shard_map.64
  1.4 0.0 copy-start.1
  1.4 0.0 copy-start.2
  1.5 75.5 %all_to_all.30 = bf16[8,24,512]{2,1,0:T(8,128)(2,1)S(1)} all-to-all(bf16[8,24,512]{2,1,0:T(8,128)(2,1)S(1)} %get-tuple-element.15), channel_id=1, replica_groups=mesh['groups'=2,'far'=8,'near'=4,'x'=4,'core'=2] {'far'}, dimensions={0} | all-to-all | bytes 393216 | tf_op jit(solution)/shard_map/all_to_all | solution.py:209
  76.9 0.1 copy.16
  77.0 0.2 copy.17
  77.2 1.0 broadcast_in_dim.8
  78.2 6.0 %all-to-all-start.1 = ((bf16[4,96,1024]{2,1,0:T(8,128)(2,1)}), bf16[4,96,1024]{2,1,0:T(8,128)(2,1)S(1)}, u32[]{:S(2)}, u32[]{:S(2)}) async-start(bf16[4,96,1024]{2,1,0:T(8,128)(2,1)} %broadcast_in_dim.8), calls=%async_computation.1 | async-start | bytes 1572864 | tf_op jit(solution)/shard_map/all_to_all | solution.py:229
  84.2 0.0 copy-done.1
  84.2 0.0 copy-done.2
  84.2 0.2 dynamic-slice_bitcast_fusion.6
  84.4 0.1 pad_maximum_fusion.2
  84.4 6.7 %collective-permute-start.2 = (bf16[2,1024,128]{2,1,0:T(8,128)(2,1)S(1)}, bf16[2,1024,128]{2,1,0:T(8,128)(2,1)S(1)}, u32[]{:S(2)}, u32[]{:S(2)}) collective-permute-start(bf16[2,1024,128]{2,1,0:T(8,128)(2,1)S(1)} %pad_maximum_fusion.2), channel_id=1, source_target_pairs={{0,4},{2,6},{4,0},{6,2},{1,5},{3,7},{5,1},{7,3},{8,12},{10,14},{12... | collective-permute-start | bytes 1572872 | tf_op jit(solution)/shard_map/ppermute | solution.py:222
  91.2 0.1 pad_maximum_fusion.3
  91.2 2.0 collective-permute-start.3
  93.2 0.1 pad_maximum_fusion.1
  93.2 4.0 %collective-permute-start.1 = (bf16[2,1024,128]{2,1,0:T(8,128)(2,1)S(1)}, bf16[2,1024,128]{2,1,0:T(8,128)(2,1)S(1)}, u32[]{:S(2)}, u32[]{:S(2)}) collective-permute-start(bf16[2,1024,128]{2,1,0:T(8,128)(2,1)S(1)} %pad_maximum_fusion.1), channel_id=1, source_target_pairs={{0,2},{2,4},{4,6},{6,0},{1,3},{3,5},{5,7},{7,1},{8,10},{10,12},{12... | collective-permute-start | bytes 1572872 | tf_op jit(solution)/shard_map/ppermute | solution.py:222
  97.2 0.1 maximum_bitcast_fusion
  97.3 6.7 %collective-permute-done.2 = bf16[2,1024,128]{2,1,0:T(8,128)(2,1)S(1)} collective-permute-done((bf16[2,1024,128]{2,1,0:T(8,128)(2,1)S(1)}, bf16[2,1024,128]{2,1,0:T(8,128)(2,1)S(1)}, u32[]{:S(2)}, u32[]{:S(2)}) %collective-permute-start.2) | collective-permute-done | bytes 524320 | tf_op jit(solution)/shard_map/ppermute | solution.py:222
  103.9 8.9 %collective-permute-done.3 = bf16[2,1024,128]{2,1,0:T(8,128)(2,1)S(1)} collective-permute-done((bf16[2,1024,128]{2,1,0:T(8,128)(2,1)S(1)}, bf16[2,1024,128]{2,1,0:T(8,128)(2,1)S(1)}, u32[]{:S(2)}, u32[]{:S(2)}) %collective-permute-start.3) | collective-permute-done | bytes 524320 | tf_op jit(solution)/shard_map/ppermute | solution.py:222
  112.8 0.0 collective-permute-done.1
  112.8 0.0 copy-start
  112.8 0.3 pad_maximum_fusion.own
  113.1 2.1 collective-permute-start.4
  115.2 0.0 copy-done
  115.2 2.4 %collective-permute-start = (bf16[1024,512]{1,0:T(8,128)(2,1)S(1)}, bf16[1024,512]{1,0:T(8,128)(2,1)}, u32[]{:S(2)}, u32[]{:S(2)}) collective-permute-start(bf16[1024,512]{1,0:T(8,128)(2,1)S(1)} %copy-done), channel_id=1, source_target_pairs={{0,1},{1,0},{2,3},{3,2},{4,5},{5,4},{6,7},{7,6},{8,9},{9,8},{10,11... | collective-permute-start | bytes 3145736 | tf_op jit(solution)/shard_map/ppermute | solution.py:225
  117.6 3.3 %collective-permute-done.refs_1_ = bf16[1024,512]{1,0:T(8,128)(2,1)} collective-permute-done((bf16[1024,512]{1,0:T(8,128)(2,1)S(1)}, bf16[1024,512]{1,0:T(8,128)(2,1)}, u32[]{:S(2)}, u32[]{:S(2)}) %collective-permute-start) | collective-permute-done | bytes 1048608 | tf_op jit(solution)/shard_map/ppermute | solution.py:225
  120.9 0.0 all-to-all-done.1
  120.9 0.0 collective-permute-done.4.other
  120.9 3.1 %shard_map.65 = bf16[4,2,2,384,128]{4,3,2,1,0:T(8,128)(2,1)S(1)} custom-call(bf16[384,1024]{1,0:T(8,128)(2,1)S(1)} %bitcast.42, bf16[4,2,1024,128]{3,2,1,0:T(8,128)(2,1)S(1)} %pad_maximum_fusion.own, bf16[4,2,1024,128]{3,2,1,0:T(8,128)(2,1)} %collective-permute-done.4.other), custom_call_target="tpu_custom_call" | custom-call | tf_op jit(solution)/shard_map/pallas_call | solution.py:127
  124.0 24.9 %all_to_all.31.sums = bf16[4,2,2,384,128]{4,3,2,1,0:T(8,128)(2,1)S(1)} all-to-all(bf16[4,2,2,384,128]{4,3,2,1,0:T(8,128)(2,1)S(1)} %shard_map.65), channel_id=1, replica_groups=mesh['groups'=2,'far'=8,'near'=4,'x'=4,'core'=2] {'x'}, dimensions={0} | all-to-all | bytes 3145728 | tf_op jit(solution)/shard_map/all_to_all | solution.py:235
  148.9 1.6 shard_map.66
  150.4 13.9 %all_to_all.32.units = bf16[4,384,256]{2,1,0:T(8,128)(2,1)S(1)} all-to-all(bf16[4,384,256]{2,1,0:T(8,128)(2,1)S(1)} %get-tuple-element.18), channel_id=1, replica_groups=mesh['groups'=2,'far'=8,'near'=4,'x'=4,'core'=2] {'x'}, dimensions={0} | all-to-all | bytes 1572864 | tf_op jit(solution)/shard_map/all_to_all | solution.py:237
  164.3 1.0 shard_map.67
  165.3 25.6 %all_to_all.33 = bf16[8,96,512]{2,1,0:T(8,128)(2,1)S(1)} all-to-all(bf16[8,96,512]{2,1,0:T(8,128)(2,1)S(1)} %bitcast.43), channel_id=1, replica_groups=mesh['groups'=2,'far'=8,'near'=4,'x'=4,'core'=2] {'near','core'}, dimensions={0} | all-to-all | bytes 1572864 | tf_op jit(solution)/shard_map/all_to_all | solution.py:239
  190.9 0.2 reduce.1
  191.0 0.2 copy.23
  191.2 0.1 copy.19
  191.3 0.1 copy.20
  191.4 38.9 %all_to_all.34 = bf16[8,24,512]{2,1,0:T(8,128)(2,1)S(1)} all-to-all(bf16[8,24,512]{2,1,0:T(8,128)(2,1)S(1)} %copy.20), channel_id=1, replica_groups=mesh['groups'=2,'far'=8,'near'=4,'x'=4,'core'=2] {'far'}, dimensions={0} | all-to-all | bytes 393216 | tf_op jit(solution)/shard_map/all_to_all | solution.py:246
  230.3 0.9 fusion
  (2 shorter events, 0.0 us)
Async XLA Ops:
  1.4 82.8 %copy-start.1 = (bf16[4096,128]{1,0:T(8,128)(2,1)S(1)}, bf16[4096,128]{1,0:T(8,128)(2,1)}, u32[]{:S(2)}) copy-start(bf16[4096,128]{1,0:T(8,128)(2,1)} %param.10) | copy-start | bytes 3145732
  1.4 82.7 %copy-start.2 = (bf16[4096,128]{1,0:T(8,128)(2,1)S(1)}, bf16[4096,128]{1,0:T(8,128)(2,1)}, u32[]{:S(2)}) copy-start(bf16[4096,128]{1,0:T(8,128)(2,1)} %param.9) | copy-start | bytes 3145732
  78.2 42.7 %all-to-all-start.1 = ((bf16[4,96,1024]{2,1,0:T(8,128)(2,1)}), bf16[4,96,1024]{2,1,0:T(8,128)(2,1)S(1)}, u32[]{:S(2)}, u32[]{:S(2)}) async-start(bf16[4,96,1024]{2,1,0:T(8,128)(2,1)} %broadcast_in_dim.8), calls=%async_computation.1 | async-start | bytes 1572864 | tf_op jit(solution)/shard_map/all_to_all | solution.py:229
  84.4 19.5 %collective-permute-start.2 = (bf16[2,1024,128]{2,1,0:T(8,128)(2,1)S(1)}, bf16[2,1024,128]{2,1,0:T(8,128)(2,1)S(1)}, u32[]{:S(2)}, u32[]{:S(2)}) collective-permute-start(bf16[2,1024,128]{2,1,0:T(8,128)(2,1)S(1)} %pad_maximum_fusion.2), channel_id=1, source_target_pairs={{0,4},{2,6},{4,0},{6,2},{1,5},{3,7},{5,1},{7,3},{8,12},{10,14},{12... | collective-permute-start | bytes 1572872 | tf_op jit(solution)/shard_map/ppermute | solution.py:222
  91.2 21.6 %collective-permute-start.3 = (bf16[2,1024,128]{2,1,0:T(8,128)(2,1)S(1)}, bf16[2,1024,128]{2,1,0:T(8,128)(2,1)S(1)}, u32[]{:S(2)}, u32[]{:S(2)}) collective-permute-start(bf16[2,1024,128]{2,1,0:T(8,128)(2,1)S(1)} %pad_maximum_fusion.3), channel_id=1, source_target_pairs={{0,6},{2,0},{4,2},{6,4},{1,7},{3,1},{5,3},{7,5},{8,14},{10,8},{12,... | collective-permute-start | bytes 1572872 | tf_op jit(solution)/shard_map/ppermute | solution.py:222
  93.2 19.6 %collective-permute-start.1 = (bf16[2,1024,128]{2,1,0:T(8,128)(2,1)S(1)}, bf16[2,1024,128]{2,1,0:T(8,128)(2,1)S(1)}, u32[]{:S(2)}, u32[]{:S(2)}) collective-permute-start(bf16[2,1024,128]{2,1,0:T(8,128)(2,1)S(1)} %pad_maximum_fusion.1), channel_id=1, source_target_pairs={{0,2},{2,4},{4,6},{6,0},{1,3},{3,5},{5,7},{7,1},{8,10},{10,12},{12... | collective-permute-start | bytes 1572872 | tf_op jit(solution)/shard_map/ppermute | solution.py:222
  112.8 2.4 %copy-start = (bf16[1024,512]{1,0:T(8,128)(2,1)S(1)}, bf16[1024,512]{1,0:T(8,128)(2,1)}, u32[]{:S(2)}) copy-start(bf16[1024,512]{1,0:T(8,128)(2,1)} %refs_0_.3) | copy-start | bytes 3145732
  113.1 7.9 %collective-permute-start.4 = (bf16[4,2,1024,128]{3,2,1,0:T(8,128)(2,1)S(1)}, bf16[4,2,1024,128]{3,2,1,0:T(8,128)(2,1)}, u32[]{:S(2)}, u32[]{:S(2)}) collective-permute-start(bf16[4,2,1024,128]{3,2,1,0:T(8,128)(2,1)S(1)} %pad_maximum_fusion.own), channel_id=1, source_target_pairs={{0,1},{1,0},{2,3},{3,2},{4,5},{5,4},{6,7},{7,6},{8,9},{9,8},{10,11... | collective-permute-start | bytes 6291464 | tf_op jit(solution)/shard_map/ppermute | solution.py:224
  115.2 5.7 %collective-permute-start = (bf16[1024,512]{1,0:T(8,128)(2,1)S(1)}, bf16[1024,512]{1,0:T(8,128)(2,1)}, u32[]{:S(2)}, u32[]{:S(2)}) collective-permute-start(bf16[1024,512]{1,0:T(8,128)(2,1)S(1)} %copy-done), channel_id=1, source_target_pairs={{0,1},{1,0},{2,3},{3,2},{4,5},{5,4},{6,7},{7,6},{8,9},{9,8},{10,11... | collective-permute-start | bytes 3145736 | tf_op jit(solution)/shard_map/ppermute | solution.py:225

commit v12 on v8

--- a/solution.py
+++ b/solution.py
@@ -8,7 +8,7 @@
 
 EXPERTS = 4
 CAP = 24
-NEAR = 8
+NEAR = 2
 CORES = 2
 PART = CAP // CORES
 
@@ -98,18 +98,14 @@
 
 def product_kernel(rows, own, other, out, held, sem):
     xs, kinds, _, width = own.shape
-    moves = [
-        pltpu.make_async_copy(other.at[shift], held.at[shift], sem.at[shift])
-        for shift in range(xs)
-    ]
-    for move in moves:
-        move.start()
+    move = pltpu.make_async_copy(other, held, sem)
+    move.start()
     x = lax.axis_index("x")
     left = rows[...]
     for core, weights in enumerate((own, held)):
+        if core:
+            move.wait()
         for shift in range(xs):
-            if core:
-                moves[shift].wait()
             to = lax.rem(x + (xs - shift), xs)
             both = jnp.concatenate([weights[shift, kind] for kind in range(kinds)], axis=1)
             product = jnp.dot(left, both, preferred_element_type=jnp.float32).astype(out.dtype)
@@ -126,7 +122,7 @@
         in_specs=[whole(), whole(), whole(pltpu.HBM)],
         out_specs=whole(),
         out_shape=pltpu.VMEM((xs, CORES, kinds, n_rows, width), jnp.bfloat16),
-        scratch_shapes=[pltpu.VMEM(other.shape, other.dtype), pltpu.SemaphoreType.DMA((xs,))],
+        scratch_shapes=[pltpu.VMEM(other.shape, other.dtype), pltpu.SemaphoreType.DMA],
     )(*near_memory(rows, own), pltpu.with_memory_space_constraint(other, pltpu.HBM))
 
 

time: 245 us -> 252 us (1.029)
  the two profiles are of different devices: /device:TPU:33 before, /device:TPU:168 now
where the time goes in v12:
time: 252 us; the launch traced here: 251 us
  blocking collectives  113 us (45%)
  starting transfers between devices  73.2 us (29%)
  waiting for transfers between devices  49.9 us (20%)
  Pallas kernels  7.87 us (3%)
  local copies, waits for them, and re-layouts  4.78 us (2%)
    all_to_all x1, blocking collectives, layer(): returned = lax.all_to_all(summed, 'far', 0, 0, tiled=True)  59.4 us
    all_to_all x1, starting transfers between devices, layer(): arrived = lax.all_to_all(sent, 'far', 0, 0, tiled=True)  42.2 us
    all_to_all x1, waiting for transfers between devices, layer(): arrived = lax.all_to_all(sent, 'far', 0, 0, tiled=True)  33.4 us
    all_to_all x1, blocking collectives, layer(): sums = lax.all_to_all(partial, 'x', 0, 0, tiled=True)  24.8 us
    all_to_all x1, starting transfers between devices, layer(): lax.all_to_all(jnp.broadcast_to(arrived, (near, far * PART, chip_width)),...  15.3 us
    all_to_all x1, blocking collectives, layer(): lax.all_to_all(produced.reshape(near * CORES, far * PART, out_width), ('n...  15.3 us
    all_to_all x1, blocking collectives, layer(): units = lax.all_to_all(hidden, 'x', 0, 0, tiled=True)  13.9 us
    ppermute x3, waiting for transfers between devices, layer(): lax.ppermute(chunk(shift), 'x', [(i, (i + shift) % xs) for i in range(xs)])  13.2 us
  transfers between devices with their start and end apart: 7, of which 5 were waited for; matrix products, arithmetic and copies ran while one was open for 1% of the time, Pallas kernels for 0%

profile of v12, /device:TPU:168, one launch (start us, length us, event | category | flops | bytes accessed | tf_op | source)
XLA Modules:
  0.0 250.9 jit_solution(5638780998092462391)
XLA Ops:
  0.0 2.1 shard_map.64
  2.1 42.2 %all-to-all-start = ((bf16[16,24,512]{2,1,0:T(8,128)(2,1)}), bf16[16,24,512]{2,1,0:T(8,128)(2,1)S(1)}, u32[]{:S(2)}, u32[]{:S(2)}) async-start(bf16[16,24,512]{2,1,0:T(8,128)(2,1)} %get-tuple-element.15), calls=%async_computation | async-start | bytes 786432 | tf_op jit(solution)/shard_map/all_to_all | solution.py:201
  44.3 2.5 dynamic-slice_bitcast_fusion.6
  46.8 33.4 %all-to-all-done = bf16[16,24,512]{2,1,0:T(8,128)(2,1)S(1)} async-done(((bf16[16,24,512]{2,1,0:T(8,128)(2,1)}), bf16[16,24,512]{2,1,0:T(8,128)(2,1)S(1)}, u32[]{:S(2)}, u32[]{:S(2)}) %all-to-all-start) | async-done | bytes 393248 | tf_op jit(solution)/shard_map/all_to_all | solution.py:201
  80.1 0.1 copy.16
  80.3 0.4 copy.17
  80.7 0.0 copy-start.3
  80.7 0.0 copy-start.1
  80.7 0.0 copy-start.2
  80.7 1.0 broadcast_in_dim.8
  81.7 15.3 %all-to-all-start.1 = ((bf16[2,192,1024]{2,1,0:T(8,128)(2,1)}), bf16[2,192,1024]{2,1,0:T(8,128)(2,1)S(1)}, u32[]{:S(2)}, u32[]{:S(2)}) async-start(bf16[2,192,1024]{2,1,0:T(8,128)(2,1)} %broadcast_in_dim.8), calls=%async_computation.1 | async-start | bytes 1572864 | tf_op jit(solution)/shard_map/all_to_all | solution.py:221
  97.1 0.0 copy-done.3
  97.1 0.1 pad_maximum_fusion.2
  97.1 5.2 %collective-permute-start.2 = (bf16[2,1024,128]{2,1,0:T(8,128)(2,1)S(1)}, bf16[2,1024,128]{2,1,0:T(8,128)(2,1)S(1)}, u32[]{:S(2)}, u32[]{:S(2)}) collective-permute-start(bf16[2,1024,128]{2,1,0:T(8,128)(2,1)S(1)} %pad_maximum_fusion.2), channel_id=1, source_target_pairs={{0,4},{2,6},{4,0},{6,2},{1,5},{3,7},{5,1},{7,3},{8,12},{10,14},{12... | collective-permute-start | bytes 1572872 | tf_op jit(solution)/shard_map/ppermute | solution.py:214
  102.4 0.0 copy-done.1
  102.4 0.0 copy-done.2
  102.4 0.1 pad_maximum_fusion.3
  102.5 3.0 %collective-permute-start.3 = (bf16[2,1024,128]{2,1,0:T(8,128)(2,1)S(1)}, bf16[2,1024,128]{2,1,0:T(8,128)(2,1)S(1)}, u32[]{:S(2)}, u32[]{:S(2)}) collective-permute-start(bf16[2,1024,128]{2,1,0:T(8,128)(2,1)S(1)} %pad_maximum_fusion.3), channel_id=1, source_target_pairs={{0,6},{2,0},{4,2},{6,4},{1,7},{3,1},{5,3},{7,5},{8,14},{10,8},{12,... | collective-permute-start | bytes 1572872 | tf_op jit(solution)/shard_map/ppermute | solution.py:214
  105.5 0.1 pad_maximum_fusion.1
  105.5 2.9 %collective-permute-start.1 = (bf16[2,1024,128]{2,1,0:T(8,128)(2,1)S(1)}, bf16[2,1024,128]{2,1,0:T(8,128)(2,1)S(1)}, u32[]{:S(2)}, u32[]{:S(2)}) collective-permute-start(bf16[2,1024,128]{2,1,0:T(8,128)(2,1)S(1)} %pad_maximum_fusion.1), channel_id=1, source_target_pairs={{0,2},{2,4},{4,6},{6,0},{1,3},{3,5},{5,7},{7,1},{8,10},{10,12},{12... | collective-permute-start | bytes 1572872 | tf_op jit(solution)/shard_map/ppermute | solution.py:214
  108.4 0.1 maximum_bitcast_fusion
  108.5 6.5 %collective-permute-done.2 = bf16[2,1024,128]{2,1,0:T(8,128)(2,1)S(1)} collective-permute-done((bf16[2,1024,128]{2,1,0:T(8,128)(2,1)S(1)}, bf16[2,1024,128]{2,1,0:T(8,128)(2,1)S(1)}, u32[]{:S(2)}, u32[]{:S(2)}) %collective-permute-start.2) | collective-permute-done | bytes 524320 | tf_op jit(solution)/shard_map/ppermute | solution.py:214
  114.9 6.6 %collective-permute-done.3 = bf16[2,1024,128]{2,1,0:T(8,128)(2,1)S(1)} collective-permute-done((bf16[2,1024,128]{2,1,0:T(8,128)(2,1)S(1)}, bf16[2,1024,128]{2,1,0:T(8,128)(2,1)S(1)}, u32[]{:S(2)}, u32[]{:S(2)}) %collective-permute-start.3) | collective-permute-done | bytes 524320 | tf_op jit(solution)/shard_map/ppermute | solution.py:214
  121.6 0.2 collective-permute-done.1
  121.7 0.0 copy-start
  121.7 0.3 pad_maximum_fusion.own
  122.0 2.1 collective-permute-start.4
  124.1 0.0 copy-done
  124.1 2.4 collective-permute-start
  126.6 3.3 %collective-permute-done.refs_1_ = bf16[1024,512]{1,0:T(8,128)(2,1)} collective-permute-done((bf16[1024,512]{1,0:T(8,128)(2,1)S(1)}, bf16[1024,512]{1,0:T(8,128)(2,1)}, u32[]{:S(2)}, u32[]{:S(2)}) %collective-permute-start) | collective-permute-done | bytes 1048608 | tf_op jit(solution)/shard_map/ppermute | solution.py:217
  129.9 0.0 all-to-all-done.1
  129.9 0.0 collective-permute-done.4.other
  129.9 3.3 %shard_map.65 = bf16[4,2,2,384,128]{4,3,2,1,0:T(8,128)(2,1)S(1)} custom-call(bf16[384,1024]{1,0:T(8,128)(2,1)S(1)} %bitcast.42, bf16[4,2,1024,128]{3,2,1,0:T(8,128)(2,1)S(1)} %pad_maximum_fusion.own, bf16[4,2,1024,128]{3,2,1,0:T(8,128)(2,1)} %collective-permute-done.4.other), custom_call_target="tpu_custom_call" | custom-call | tf_op jit(solution)/shard_map/pallas_call | solution.py:119
  133.2 24.8 %all_to_all.30.sums = bf16[4,2,2,384,128]{4,3,2,1,0:T(8,128)(2,1)S(1)} all-to-all(bf16[4,2,2,384,128]{4,3,2,1,0:T(8,128)(2,1)S(1)} %shard_map.65), channel_id=1, replica_groups=mesh['groups'=2,'far'=16,'near'=2,'x'=4,'core'=2] {'x'}, dimensions={0} | all-to-all | bytes 3145728 | tf_op jit(solution)/shard_map/all_to_all | solution.py:227
  157.9 1.6 shard_map.66
  159.5 13.9 %all_to_all.31.units = bf16[4,384,256]{2,1,0:T(8,128)(2,1)S(1)} all-to-all(bf16[4,384,256]{2,1,0:T(8,128)(2,1)S(1)} %get-tuple-element.18), channel_id=1, replica_groups=mesh['groups'=2,'far'=16,'near'=2,'x'=4,'core'=2] {'x'}, dimensions={0} | all-to-all | bytes 1572864 | tf_op jit(solution)/shard_map/all_to_all | solution.py:229
  173.4 1.0 shard_map.67
  174.3 15.3 %all_to_all.32 = bf16[4,192,512]{2,1,0:T(8,128)(2,1)S(1)} all-to-all(bf16[4,192,512]{2,1,0:T(8,128)(2,1)S(1)} %bitcast.43), channel_id=1, replica_groups=mesh['groups'=2,'far'=16,'near'=2,'x'=4,'core'=2] {'near','core'}, dimensions={0} | all-to-all | bytes 1572864 | tf_op jit(solution)/shard_map/all_to_all | solution.py:231
  189.6 0.2 reduce.1
  189.8 0.4 copy.23
  190.2 0.1 copy.19
  190.3 0.2 copy.20
  190.6 59.4 %all_to_all.33 = bf16[16,24,512]{2,1,0:T(8,128)(2,1)S(1)} all-to-all(bf16[16,24,512]{2,1,0:T(8,128)(2,1)S(1)} %copy.20), channel_id=1, replica_groups=mesh['groups'=2,'far'=16,'near'=2,'x'=4,'core'=2] {'far'}, dimensions={0} | all-to-all | bytes 786432 | tf_op jit(solution)/shard_map/all_to_all | solution.py:238
  250.0 0.1 convert_reduce_fusion
  250.0 0.9 fusion
  (1 shorter events, 0.0 us)
Async XLA Ops:
  2.1 78.1 %all-to-all-start = ((bf16[16,24,512]{2,1,0:T(8,128)(2,1)}), bf16[16,24,512]{2,1,0:T(8,128)(2,1)S(1)}, u32[]{:S(2)}, u32[]{:S(2)}) async-start(bf16[16,24,512]{2,1,0:T(8,128)(2,1)} %get-tuple-element.15), calls=%async_computation | async-start | bytes 786432 | tf_op jit(solution)/shard_map/all_to_all | solution.py:201
  80.7 16.4 %copy-start.3 = (bf16[1,1024,128]{2,1,0:T(8,128)(2,1)S(1)}, bf16[1,1024,128]{2,1,0:T(8,128)(2,1)}, u32[]{:S(2)}) copy-start(bf16[1,1024,128]{2,1,0:T(8,128)(2,1)} %get-tuple-element.28) | copy-start | bytes 786436
  80.7 21.6 %copy-start.1 = (bf16[1,1024,128]{2,1,0:T(8,128)(2,1)S(1)}, bf16[1,1024,128]{2,1,0:T(8,128)(2,1)}, u32[]{:S(2)}) copy-start(bf16[1,1024,128]{2,1,0:T(8,128)(2,1)} %get-tuple-element.27) | copy-start | bytes 786436
  80.7 21.6 %copy-start.2 = (bf16[1,1024,128]{2,1,0:T(8,128)(2,1)S(1)}, bf16[1,1024,128]{2,1,0:T(8,128)(2,1)}, u32[]{:S(2)}) copy-start(bf16[1,1024,128]{2,1,0:T(8,128)(2,1)} %get-tuple-element.30) | copy-start | bytes 786436
  81.7 48.1 %all-to-all-start.1 = ((bf16[2,192,1024]{2,1,0:T(8,128)(2,1)}), bf16[2,192,1024]{2,1,0:T(8,128)(2,1)S(1)}, u32[]{:S(2)}, u32[]{:S(2)}) async-start(bf16[2,192,1024]{2,1,0:T(8,128)(2,1)} %broadcast_in_dim.8), calls=%async_computation.1 | async-start | bytes 1572864 | tf_op jit(solution)/shard_map/all_to_all | solution.py:221
  97.1 17.8 %collective-permute-start.2 = (bf16[2,1024,128]{2,1,0:T(8,128)(2,1)S(1)}, bf16[2,1024,128]{2,1,0:T(8,128)(2,1)S(1)}, u32[]{:S(2)}, u32[]{:S(2)}) collective-permute-start(bf16[2,1024,128]{2,1,0:T(8,128)(2,1)S(1)} %pad_maximum_fusion.2), channel_id=1, source_target_pairs={{0,4},{2,6},{4,0},{6,2},{1,5},{3,7},{5,1},{7,3},{8,12},{10,14},{12... | collective-permute-start | bytes 1572872 | tf_op jit(solution)/shard_map/ppermute | solution.py:214
  102.5 19.1 %collective-permute-start.3 = (bf16[2,1024,128]{2,1,0:T(8,128)(2,1)S(1)}, bf16[2,1024,128]{2,1,0:T(8,128)(2,1)S(1)}, u32[]{:S(2)}, u32[]{:S(2)}) collective-permute-start(bf16[2,1024,128]{2,1,0:T(8,128)(2,1)S(1)} %pad_maximum_fusion.3), channel_id=1, source_target_pairs={{0,6},{2,0},{4,2},{6,4},{1,7},{3,1},{5,3},{7,5},{8,14},{10,8},{12,... | collective-permute-start | bytes 1572872 | tf_op jit(solution)/shard_map/ppermute | solution.py:214
  105.5 16.2 %collective-permute-start.1 = (bf16[2,1024,128]{2,1,0:T(8,128)(2,1)S(1)}, bf16[2,1024,128]{2,1,0:T(8,128)(2,1)S(1)}, u32[]{:S(2)}, u32[]{:S(2)}) collective-permute-start(bf16[2,1024,128]{2,1,0:T(8,128)(2,1)S(1)} %pad_maximum_fusion.1), channel_id=1, source_target_pairs={{0,2},{2,4},{4,6},{6,0},{1,3},{3,5},{5,7},{7,1},{8,10},{10,12},{12... | collective-permute-start | bytes 1572872 | tf_op jit(solution)/shard_map/ppermute | solution.py:214
  121.7 2.4 copy-start
  122.0 7.9 %collective-permute-start.4 = (bf16[4,2,1024,128]{3,2,1,0:T(8,128)(2,1)S(1)}, bf16[4,2,1024,128]{3,2,1,0:T(8,128)(2,1)}, u32[]{:S(2)}, u32[]{:S(2)}) collective-permute-start(bf16[4,2,1024,128]{3,2,1,0:T(8,128)(2,1)S(1)} %pad_maximum_fusion.own), channel_id=1, source_target_pairs={{0,1},{1,0},{2,3},{3,2},{4,5},{5,4},{6,7},{7,6},{8,9},{9,8},{10,11... | collective-permute-start | bytes 6291464 | tf_op jit(solution)/shard_map/ppermute | solution.py:216
  124.1 5.7 %collective-permute-start = (bf16[1024,512]{1,0:T(8,128)(2,1)S(1)}, bf16[1024,512]{1,0:T(8,128)(2,1)}, u32[]{:S(2)}, u32[]{:S(2)}) collective-permute-start(bf16[1024,512]{1,0:T(8,128)(2,1)S(1)} %copy-done), channel_id=1, source_target_pairs={{0,1},{1,0},{2,3},{3,2},{4,5},{5,4},{6,7},{7,6},{8,9},{9,8},{10,11... | collective-permute-start | bytes 3145736 | tf_op jit(solution)/shard_map/ppermute | solution.py:217
